TPU v7x, 16 devices: a 4x2x1 block of a 4x4x8 slice. The times are simulated.
16 devices in a mesh: dp: 2 (over y, z), tp: 8 (over x, core).
Axes of the slice: x: 4, y: 2, z: 1, core: 2. Of those that a mesh axis runs over, the one named last changes fastest.
The devices are a block of a 4x4x8 slice.
Arguments:
- x_in: bfloat16 [16, 512, 6144], P('dp', 'tp'), parts along dimension 0
- ln_gamma: float32 [6144], replicated
- ln_beta: float32 [6144], replicated
- w_q: bfloat16 [6144, 6144], P(None, 'tp')
- b_q: float32 [6144], P('tp')
- w_kv: bfloat16 [6144, 256], replicated
- b_kv: float32 [256], replicated
- w_o: bfloat16 [6144, 6144], P('tp')
- b_o: float32 [6144], replicated
- grad_y: bfloat16 [16, 512, 6144], P('dp', 'tp'), parts along dimension 0
Outputs:
- output 1: bfloat16 [16, 512, 6144], P('dp', 'tp'), parts along dimension 0
- output 2: bfloat16 [16, 512, 6144], P('dp', 'tp'), parts along dimension 0
- output 3: float32 [12288], P('dp'), parts along dimension 0
- output 4: float32 [12288], P('dp'), parts along dimension 0
- output 5: float32 [12288, 6144], P('dp', 'tp'), parts along dimension 0
- output 6: float32 [12288], P(('dp', 'tp')), parts along dimension 0
- output 7: float32 [12288, 256], P('dp'), parts along dimension 0
- output 8: float32 [512], P('dp'), parts along dimension 0
- output 9: float32 [12288, 6144], P(('dp', 'tp')), parts along dimension 0
- output 10: float32 [12288], P('dp'), parts along dimension 0
There are 2 independent parts. A program takes and returns all parts, laid end to end along the dimension named above; an argument that names none is the same for every part.
All inputs are finite; a program needn't handle non-finite values.
Results may differ from a plain program's by a relative error of at most 0.0160206.
Values are sent between devices in bfloat16 or wider.
A program may use at most 768 MiB of HBM per device.

v0:
```python
import jax
import jax.numpy as jnp
from jax import lax
from jax.sharding import PartitionSpec as P

LN_EPS = 1e-5


def norm_forward(x_loc, ln_gamma, ln_beta):
    x_wide = x_loc.astype(jnp.float32)
    centred = x_wide - jnp.mean(x_wide, axis=-1, keepdims=True)
    inv_std = lax.rsqrt(jnp.mean(centred * centred, axis=-1, keepdims=True) + LN_EPS)
    x_hat = centred * inv_std
    return x_hat, inv_std, (x_hat * ln_gamma + ln_beta).astype(jnp.bfloat16)


def norm_backward(grad_h, x_hat, inv_std, ln_gamma):
    grad_hat = grad_h * ln_gamma
    grad_in = inv_std * (grad_hat - jnp.mean(grad_hat, axis=-1, keepdims=True) - x_hat * jnp.mean(grad_hat * x_hat, axis=-1, keepdims=True))
    return grad_in, jnp.sum(grad_h * x_hat, axis=(0, 1)), jnp.sum(grad_h, axis=(0, 1))


def attn_forward(q_heads, key_rows, value_rows, causal):
    scores = jnp.einsum("bqhc,bkc->bhqk", q_heads, key_rows, preferred_element_type=jnp.float32) * q_heads.shape[-1] ** -0.5
    attn_prob = jax.nn.softmax(jnp.where(causal, scores, -1e30), axis=-1)
    prob_lo = attn_prob.astype(jnp.bfloat16)
    attended = jnp.einsum("bhqk,bkc->bqhc", prob_lo, value_rows, preferred_element_type=jnp.float32).astype(jnp.bfloat16)
    return attn_prob, prob_lo, attended


def attn_backward(grad_att, q_heads, key_rows, value_rows, attn_prob, prob_lo):
    grad_prob = jnp.einsum("bqhc,bkc->bhqk", grad_att, value_rows, preferred_element_type=jnp.float32).astype(jnp.bfloat16)
    row_dot = jnp.sum(attn_prob * grad_prob, axis=-1, keepdims=True)
    grad_score = (attn_prob * (grad_prob - row_dot) * q_heads.shape[-1] ** -0.5).astype(jnp.bfloat16)
    grad_q = jnp.einsum("bhqk,bkc->bqhc", grad_score, key_rows, preferred_element_type=jnp.float32).astype(jnp.bfloat16)
    grad_k = jnp.einsum("bhqk,bqhc->bkc", grad_score, q_heads, preferred_element_type=jnp.float32)
    grad_v = jnp.einsum("bhqk,bqhc->bkc", prob_lo, grad_att, preferred_element_type=jnp.float32)
    return grad_q, jnp.concatenate([grad_k, grad_v], axis=-1)


def solution(mesh):
    def device_block(x_loc, ln_gamma, ln_beta, w_q, b_q, w_kv, b_kv, w_o, b_o, dy_loc):
        head_dim = w_kv.shape[1] // 2
        local_heads = w_q.shape[1] // head_dim
        x_hat, inv_std, normed = norm_forward(x_loc, ln_gamma, ln_beta)
        normed_full = lax.all_gather(normed, "tp", axis=1, tiled=True)
        batch_size = normed_full.shape[0]
        seq_len = normed_full.shape[1]
        queries = (jnp.einsum("bsd,de->bse", normed_full, w_q, preferred_element_type=jnp.float32) + b_q).astype(jnp.bfloat16)
        q_heads = queries.reshape(batch_size, seq_len, local_heads, head_dim)
        key_val = (jnp.einsum("bsd,dc->bsc", normed_full, w_kv, preferred_element_type=jnp.float32) + b_kv).astype(jnp.bfloat16)
        key_rows = key_val[:, :, :head_dim]
        value_rows = key_val[:, :, head_dim:]
        positions = jnp.arange(seq_len)
        causal = positions[:, None] >= positions[None, :]
        attn_prob, prob_lo, attended = attn_forward(q_heads, key_rows, value_rows, causal)
        merged = attended.reshape(queries.shape)
        out_part = jnp.einsum("bse,ed->bsd", merged, w_o, preferred_element_type=jnp.float32).astype(jnp.bfloat16)
        out_loc = lax.psum_scatter(out_part, "tp", scatter_dimension=1, tiled=True)
        y_loc = (x_loc.astype(jnp.float32) + out_loc.astype(jnp.float32) + b_o).astype(jnp.bfloat16)

        grad_bo = lax.psum(jnp.sum(dy_loc, axis=(0, 1), dtype=jnp.float32), "tp")
        dy_full = lax.all_gather(dy_loc, "tp", axis=1, tiled=True)
        grad_wo = jnp.einsum("bse,bsd->ed", merged, dy_full, preferred_element_type=jnp.float32)
        grad_att = jnp.einsum("bsd,ed->bse", dy_full, w_o, preferred_element_type=jnp.float32).astype(jnp.bfloat16)
        grad_q, kv_wide = attn_backward(grad_att.reshape(q_heads.shape), q_heads, key_rows, value_rows, attn_prob, prob_lo)
        grad_q = grad_q.reshape(queries.shape)
        grad_kv = kv_wide.astype(jnp.bfloat16)
        grad_wq = jnp.einsum("bsd,bse->de", normed_full, grad_q, preferred_element_type=jnp.float32)
        grad_bq = jnp.sum(grad_q, axis=(0, 1), dtype=jnp.float32)
        grad_wkv, grad_bkv = lax.psum((jnp.einsum("bsd,bsc->dc", normed_full, grad_kv, preferred_element_type=jnp.float32), jnp.sum(grad_kv, axis=(0, 1), dtype=jnp.float32)), "tp")
        grad_h_part = (jnp.einsum("bse,de->bsd", grad_q, w_q, preferred_element_type=jnp.float32) + jnp.einsum("bsc,dc->bsd", grad_kv, w_kv, preferred_element_type=jnp.float32)).astype(jnp.bfloat16)
        grad_h = lax.psum_scatter(grad_h_part, "tp", scatter_dimension=1, tiled=True).astype(jnp.float32)
        grad_in, gamma_part, beta_part = norm_backward(grad_h, x_hat, inv_std, ln_gamma)
        grad_gamma, grad_beta = lax.psum((gamma_part, beta_part), "tp")
        grad_x = (dy_loc.astype(jnp.float32) + grad_in).astype(jnp.bfloat16)
        return (y_loc, grad_x, grad_gamma, grad_beta, grad_wq, grad_bq, grad_wkv, grad_bkv, grad_wo, grad_bo)

    return jax.shard_map(
        device_block,
        mesh=mesh,
        in_specs=(P("dp", "tp", None), P(None), P(None), P(None, "tp"), P("tp"), P(None, None), P(None), P("tp", None), P(None), P("dp", "tp", None)),
        out_specs=(P("dp", "tp", None), P("dp", "tp", None), P("dp"), P("dp"), P("dp", "tp"), P(("dp", "tp")), P("dp", None), P("dp"), P(("dp", "tp"), None), P("dp")),
        check_vma=False,
    )
```

profile of v0, /device:TPU:112, one launch (start us, length us, event | category | flops | bytes accessed | tf_op | source)
XLA Modules:
  0.0 1458.2 jit_solution(10506917916218907203)
XLA Ops:
  7.3 3.8 convert_reduce_fusion.1
  11.2 4.7 fusion.23
  16.5 6.3 fusion.20
  25.1 224.3 %all-gather.3.cloned.1.call-done = bf16[8,512,6144]{2,1,0:T(8,128)(2,1)} async-done(((bf16[8,64,6144]{2,1,0:T(8,128)(2,1)}), bf16[8,512,6144]{2,1,0:T(8,128)(2,1)}) %all-gather.3.cloned.1.call-update) | async-done | bytes 50331664 | tf_op jit(solution)/shard_map/all_gather | solution.py:46
  249.4 46.7 %add_convert_fusion.1 = bf16[8,512,768]{2,1,0:T(8,128)(2,1)} fusion(f32[768]{0:T(1024)S(1)} %copy-done.17, bf16[8,512,6144]{2,1,0:T(8,128)(2,1)} %all-gather.3.cloned.1.call-done, bf16[6144,768]{1,0:T(8,128)(2,1)} %param.13), kind=kOutput, calls=%fused_computation.50 | convolution fusion | flops 38660997120 | bytes 66063360 | tf_op jit(solution)/shard_map/bsd,de->bse/dot_general | solution.py:49
  296.2 8.6 copy.35
  304.8 169.6 %all-gather.5.cloned.1.call-done = bf16[8,512,6144]{2,1,0:T(8,128)(2,1)} async-done(((bf16[8,64,6144]{2,1,0:T(8,128)(2,1)}), bf16[8,512,6144]{2,1,0:T(8,128)(2,1)}) %all-gather.5.cloned.1.call-update) | async-done | bytes 50331664 | tf_op jit(solution)/shard_map/all_gather | solution.py:63
  474.3 47.1 %fusion.44 = bf16[8,512,768]{2,1,0:T(8,128)(2,1)} fusion(bf16[8,512,6144]{2,1,0:T(8,128)(2,1)} %all-gather.5.cloned.1.call-done, bf16[768,6144]{1,0:T(8,128)(2,1)} %param.17), kind=kOutput, calls=%fused_computation.64 | convolution fusion | flops 38657851392 | bytes 66060288 | tf_op jit(solution)/shard_map/bsd,ed->bse/dot_general | solution.py:65
  521.4 8.6 copy.40
  530.0 22.4 %add_convert_fusion.2 = bf16[8,512,256]{2,1,0:T(8,128)(2,1)} fusion(f32[256]{0:T(256)S(1)} %copy-done.18, bf16[8,512,6144]{2,1,0:T(8,128)(2,1)} %all-gather.3.cloned.1.call-done, bf16[6144,256]{1,0:T(8,128)(2,1)S(1)} %copy-done), kind=kOutput, calls=%fused_computation.62 | convolution fusion | flops 12886999040 | bytes 55575552 | tf_op jit(solution)/shard_map/bsd,dc->bsc/dot_general | solution.py:51
  552.5 14.0 convolution_convert_fusion.1
  566.5 26.5 %fusion.67 = (f32[8,6,512]{2,1,0:T(8,128)S(1)}, f32[8,6,512,512]{2,3,1,0:T(8,128)}) fusion(pred[512,512]{0,1:T(8,128)(4,1)S(1)} %copy-done.6, bf16[8,512,6,128]{1,3,2,0:T(8,128)(2,1)} %bitcast.134, bf16[8,512,256]{2,1,0:T(8,128)(2,1)} %add_convert_fusion.2), kind=kOutput, calls=%fused_computation.89 | convolution fusion | flops 3271557632 | bytes 58032128 | tf_op jit(solution)/shard_map/sub | solution.py:25
  593.0 50.5 %bitcast_convert_fusion.1 = bf16[8,512,128]{1,2,0:T(8,128)(2,1)} fusion(bf16[8,512,6,128]{1,3,2,0:T(8,128)(2,1)} %bitcast.135, bf16[8,512,512,6]{2,1,3,0:T(8,128)(2,1)} %convolution_convert_fusion.1, f32[8,6,512,512]{2,3,1,0:T(8,128)} %get-tuple-element.22, f32[8,6,512]{2,1,0:T(8,128)S(1)} %get-tuple-element.21), kind=kOutput, calls=%fused_computation.72 | convolution fusion | flops 3335021056 | bytes 82935808 | tf_op jit(solution)/shard_map/bhqk,bqhc->bkc/dot_general | solution.py:36
  643.5 51.3 %convert_reduce_fusion.3 = (f32[6,128]{1,0:T(8,128)}, bf16[8,128,6,512]{3,1,2,0:T(8,128)(2,1)}) fusion(bf16[8,512,512,6]{2,1,3,0:T(8,128)(2,1)} %convolution_convert_fusion.1, f32[8,6,512,512]{2,3,1,0:T(8,128)} %get-tuple-element.22, f32[8,6,512]{2,1,0:T(8,128)S(1)} %get-tuple-element.21, bf16[8,512,256]{2,1,0:T(8,128)(2,1)} %add_convert_fusion.2), kind=kOutput, calls=%fused_computation.45 | convolution fusion | flops 3343933184 | bytes 158600192 | tf_op jit(solution)/shard_map/bhqk,bkc->bqhc/dot_general | solution.py:35
  694.9 21.7 %bitcast_convert_fusion = bf16[8,512,128]{1,2,0:T(8,128)(2,1)} fusion(bf16[8,512,6,128]{1,3,2,0:T(8,128)(2,1)} %bitcast.133, f32[8,6,512,512]{2,3,1,0:T(8,128)} %get-tuple-element.22, f32[8,6,512]{2,1,0:T(8,128)S(1)} %get-tuple-element.21), kind=kOutput, calls=%fused_computation.71 | convolution fusion | flops 3246915584 | bytes 57769984 | tf_op jit(solution)/shard_map/bhqk,bqhc->bkc/dot_general | solution.py:37
  716.5 36.1 %fusion.50 = f32[8,512,6144]{2,1,0:T(8,128)} fusion(bf16[6144,256]{1,0:T(8,128)(2,1)S(1)} %copy-done, bf16[8,512,128]{1,2,0:T(8,128)(2,1)} %bitcast_convert_fusion, bf16[8,512,128]{1,2,0:T(8,128)(2,1)} %bitcast_convert_fusion.1), kind=kOutput, calls=%fused_computation.66 | convolution fusion | flops 12889096192 | bytes 105906176 | tf_op jit(solution)/shard_map/bsc,dc->bsd/dot_general | solution.py:72
  752.6 63.9 %add_convert_fusion = bf16[8,512,6144]{2,1,0:T(8,128)(2,1)} fusion(f32[8,512,6144]{2,1,0:T(8,128)} %fusion.50, bf16[8,512,768]{1,2,0:T(8,128)(2,1)} %bitcast.138, bf16[6144,768]{1,0:T(8,128)(2,1)} %param.13), kind=kOutput, calls=%fused_computation.2 | convolution fusion | flops 38705037312 | bytes 166723584 | tf_op jit(solution)/shard_map/bse,de->bsd/dot_general | solution.py:72
  816.6 1.5 copy-done.5
  818.1 20.0 %fusion.47 = bf16[8,128,6,512]{3,1,2,0:T(8,128)(2,1)} fusion(bf16[8,512,256]{2,1,0:T(8,128)(2,1)S(1)} %copy-done.5, f32[8,6,512,512]{2,3,1,0:T(8,128)} %get-tuple-element.22, f32[8,6,512]{2,1,0:T(8,128)S(1)} %get-tuple-element.21), kind=kOutput, calls=%fused_computation.65 | convolution fusion | flops 3249537024 | bytes 57802752 | tf_op jit(solution)/shard_map/bhqk,bkc->bqhc/dot_general | solution.py:27
  838.1 47.2 %convolution_convert_fusion = bf16[8,512,6144]{2,1,0:T(8,128)(2,1)} fusion(bf16[8,512,768]{1,2,0:T(8,128)(2,1)} %bitcast.136, bf16[768,6144]{1,0:T(8,128)(2,1)} %param.17), kind=kOutput, calls=%fused_computation.10 | convolution fusion | flops 38679871488 | bytes 66060288 | tf_op jit(solution)/shard_map/bse,ed->bsd/dot_general | solution.py:58
  887.8 23.0 %convolution_bitcast_fusion.2 = f32[6144,256]{1,0:T(8,128)} fusion(bf16[8,512,6144]{2,1,0:T(8,128)(2,1)} %all-gather.3.cloned.1.call-done, bf16[8,512,128]{1,2,0:T(8,128)(2,1)S(1)} %copy-done.4, bf16[8,512,128]{1,2,0:T(8,128)(2,1)S(1)} %copy-done.3), kind=kOutput, calls=%fused_computation.59 | convolution fusion | flops 12889096192 | bytes 58720256 | tf_op jit(solution)/shard_map/bsd,bsc->dc/dot_general | solution.py:71
  910.9 47.8 %convolution_bitcast_fusion = f32[6144,768]{1,0:T(8,128)} fusion(bf16[8,512,6144]{2,1,0:T(8,128)(2,1)} %all-gather.3.cloned.1.call-done, bf16[8,512,768]{1,2,0:T(8,128)(2,1)} %bitcast.139), kind=kOutput, calls=%fused_computation.51 | convolution fusion | flops 38654705664 | bytes 75497472 | tf_op jit(solution)/shard_map/bsd,bse->de/dot_general | solution.py:69
  958.7 103.1 %reduce-scatter.5.cloned.1.call-done = bf16[8,64,6144]{2,1,0:T(8,128)(2,1)} async-done(((bf16[8,512,6144]{2,1,0:T(8,128)(2,1)}), bf16[8,64,6144]{2,1,0:T(8,128)(2,1)}) %reduce-scatter.5.cloned.1.call-update) | async-done | bytes 6291472 | tf_op jit(solution)/shard_map/reduce_scatter | solution.py:73
  1061.8 9.2 fusion.28
  1071.0 238.0 %reduce-scatter.3.cloned.1.call-done = bf16[8,64,6144]{2,1,0:T(8,128)(2,1)} async-done(((bf16[8,512,6144]{2,1,0:T(8,128)(2,1)}), bf16[8,64,6144]{2,1,0:T(8,128)(2,1)}) %reduce-scatter.3.cloned.1.call-update) | async-done | bytes 6291472 | tf_op jit(solution)/shard_map/reduce_scatter | solution.py:59
  1309.0 16.4 %convert_reduce_fusion.2 = (f32[6144]{0:T(1024)}, bf16[8,64,6144]{2,1,0:T(8,128)(2,1)}, bf16[8,64,6144]{2,1,0:T(8,128)(2,1)}) fusion(bf16[8,64,6144]{2,1,0:T(8,128)(2,1)} %param.19, f32[8,64]{1,0:T(8,128)S(1)} %get-tuple-element.25, f32[8,64]{1,0:T(8,128)S(1)} %copy-done.10, bf16[8,64,6144]{2,1,0:T(8,128)(2,1)} %param.10, f32[8,64]{1,0:T(8,128)S(1)} %get-tuple-element.26, ...), kind=kLoop, calls=%fused_computation.28 | loop fusion | flops 53471232 | bytes 37830656 | tf_op jit(solution)/shard_map/reduce_sum | solution.py:62
  1325.5 47.2 %convolution_bitcast_fusion.1 = f32[768,6144]{1,0:T(8,128)} fusion(bf16[8,512,768]{1,2,0:T(8,128)(2,1)} %bitcast.137, bf16[8,512,6144]{2,1,0:T(8,128)(2,1)} %all-gather.5.cloned.1.call-done), kind=kOutput, calls=%fused_computation.52 | convolution fusion | flops 38654705664 | bytes 75497472 | tf_op jit(solution)/shard_map/bse,bsd->ed/dot_general | solution.py:64
  1372.7 14.3 all-reduce.4.cloned.1.call-done
  1387.0 54.3 %all-reduce.6.cloned.1.call-done = (f32[6144]{0:T(1024)}, f32[6144]{0:T(1024)}, f32[256]{0:T(256)}, f32[6144]{0:T(1024)}) async-done(((f32[6144]{0:T(1024)}, f32[6144]{0:T(1024)}, f32[256]{0:T(256)}, f32[6144]{0:T(1024)}), (f32[6144]{0:T(1024)}, f32[6144]{0:T(1024)}, f32[256]{0:T(256)}, f32[6144]{0:T(1024)})) %all-reduce.6.cloned.1.call-update) | async-done | bytes 74768 | tf_op jit(solution)/shard_map/psum | solution.py:75
  1441.3 1.4 copy.76
  1442.7 1.3 copy.77
  1444.0 5.9 copy.78
  (56 shorter events, 6.9 us)
Async XLA Ops:
  7.2 522.8 %copy-start = (bf16[6144,256]{1,0:T(8,128)(2,1)S(1)}, bf16[6144,256]{1,0:T(8,128)(2,1)}, u32[]{:S(2)}) copy-start(bf16[6144,256]{1,0:T(8,128)(2,1)} %param.15) | copy-start | bytes 9437188
  7.2 9.3 copy-start.7
  7.2 9.3 copy-start.15
  7.2 242.2 %all-gather.3.cloned.1.call-start = ((), (), s32[]{:S(2)}) async-start(), calls=%async_computation.2 | async-start | bytes 56623104 | tf_op jit(solution)/shard_map/all_gather | solution.py:46
  7.3 9.2 copy-start.2
  11.2 4.7 copy-start.9
  15.9 0.6 copy-start.11
  16.5 232.9 %copy-start.17 = (f32[768]{0:T(1024)S(1)}, f32[768]{0:T(1024)}, u32[]{:S(2)}) copy-start(f32[768]{0:T(1024)} %param.14) | copy-start | bytes 9220
  22.9 451.4 %all-gather.5.cloned.1.call-start = ((), (), s32[]{:S(2)}) async-start(), calls=%async_computation.4 | async-start | bytes 56623104 | tf_op jit(solution)/shard_map/all_gather | solution.py:63
  23.7 1038.1 %reduce-scatter.5.cloned.1.call-start = ((), (), s32[]{:S(2)}) async-start(), calls=%async_computation.5 | async-start | bytes 56623104 | tf_op jit(solution)/shard_map/reduce_scatter | solution.py:73
  521.4 8.6 copy-start.18
  552.5 14.0 copy-start.6
  816.5 1.6 copy-start.5
  816.5 492.5 %reduce-scatter.3.cloned.1.call-start = ((), (), s32[]{:S(2)}) async-start(), calls=%async_computation.3 | async-start | bytes 56623104 | tf_op jit(solution)/shard_map/reduce_scatter | solution.py:59
  885.3 1.2 copy-start.3
  885.3 1.5 copy-start.4
  885.4 501.6 %all-reduce.4.cloned.1.call-start = ((), (), s32[]{:S(2)}) async-start(), calls=%async_computation.6 | async-start | bytes 12582912 | tf_op jit(solution)/shard_map/psum | solution.py:71
  910.8 151.0 %copy-start.8 = (f32[6144]{0:T(1024)S(1)}, f32[6144]{0:T(1024)}, u32[]{:S(2)}) copy-start(f32[6144]{0:T(1024)} %param.11) | copy-start | bytes 73732
  910.8 150.9 %copy-start.10 = (f32[8,64]{1,0:T(8,128)S(1)}, f32[8,64]{1,0:T(8,128)}, u32[]{:S(2)}) copy-start(f32[8,64]{1,0:T(8,128)} %copy-done.9) | copy-start | bytes 6148
  910.9 150.9 %copy-start.12 = (f32[8,64]{1,0:T(8,128)S(1)}, f32[8,64]{1,0:T(8,128)}, u32[]{:S(2)}) copy-start(f32[8,64]{1,0:T(8,128)} %copy-done.11) | copy-start | bytes 6148
  910.9 530.4 %all-reduce.6.cloned.1.call-start = ((), (), s32[]{:S(2)}) async-start(), calls=%async_computation.7 | async-start | bytes 149504 | tf_op jit(solution)/shard_map/psum | solution.py:75
  958.7 350.3 %copy-start.13 = (f32[6144]{0:T(1024)S(1)}, f32[6144]{0:T(1024)}, u32[]{:S(2)}) copy-start(f32[6144]{0:T(1024)} %param.18) | copy-start | bytes 73732
  1325.5 125.6 %copy-start.1 = (bf16[6144,256]{1,0:T(8,128)(2,1)S(1)}, bf16[6144,256]{1,0:T(8,128)(2,1)}, u32[]{:S(2)}) copy-start(bf16[6144,256]{1,0:T(8,128)(2,1)} %param.15) | copy-start | bytes 9437188
  1441.3 8.6 copy-start.16
  1441.3 9.2 copy-start.14
Sparse Core Ops, SparseCore 0:
  23.0 226.3 all-gather.2
  251.0 223.2 all-gather.4
  816.7 245.0 reduce-scatter.4
  1064.0 244.9 reduce-scatter.2
  1311.3 75.6 all-reduce.3
  1390.6 50.6 all-reduce.5
where the time goes:
time: 1460 us
  waiting for transfers between devices  805 us (55%)
  matrix products  565 us (39%)
  other arithmetic  42.2 us (3%)
  local copies, waits for them, and re-layouts  30.6 us (2%)
    reduce_scatter x1, waiting for transfers between devices, device_block(): out_loc = lax.psum_scatter(out_part, 'tp', scatter_dimension=1, tiled=True)  238 us
    all_gather x1, waiting for transfers between devices, device_block(): normed_full = lax.all_gather(normed, 'tp', axis=1, tiled=True)  224 us
    all_gather x1, waiting for transfers between devices, device_block(): dy_full = lax.all_gather(dy_loc, 'tp', axis=1, tiled=True)  170 us
    reduce_scatter x1, waiting for transfers between devices, device_block(): lax.psum_scatter(grad_h_part, 'tp', scatter_dimension=1, tiled=True)  103 us
    dot_general x1, matrix products, device_block(): jnp.einsum('bse,de->bsd', grad_q, w_q, preferred_element_type=jnp.float32)  63.9 us
    psum x1, waiting for transfers between devices, device_block(): grad_gamma, grad_beta = lax.psum((gamma_part, beta_part), 'tp')  54.3 us
    dot_general x1, matrix products, attn_backward(): jnp.einsum('bhqk,bkc->bqhc', grad_score, key_rows, preferred_element_type...  51.3 us
    dot_general x1, matrix products, attn_backward(): jnp.einsum('bhqk,bqhc->bkc', grad_score, q_heads, preferred_element_type=...  50.5 us
  transfers between devices with their start and end apart: 6, of which 6 were waited for; matrix products, arithmetic and copies ran while one was open for 18% of the time, Pallas kernels for 0%

commit v1 on v0

--- a/solution.py
+++ b/solution.py
@@ -44,6 +44,9 @@
         local_heads = w_q.shape[1] // head_dim
         x_hat, inv_std, normed = norm_forward(x_loc, ln_gamma, ln_beta)
         normed_full = lax.all_gather(normed, "tp", axis=1, tiled=True)
+        dy_full = lax.all_gather(dy_loc, "tp", axis=1, tiled=True)
+        grad_bo_part = jnp.sum(dy_loc, axis=(0, 1), dtype=jnp.float32)
+
         batch_size = normed_full.shape[0]
         seq_len = normed_full.shape[1]
         queries = (jnp.einsum("bsd,de->bse", normed_full, w_q, preferred_element_type=jnp.float32) + b_q).astype(jnp.bfloat16)
@@ -56,23 +59,28 @@
         attn_prob, prob_lo, attended = attn_forward(q_heads, key_rows, value_rows, causal)
         merged = attended.reshape(queries.shape)
         out_part = jnp.einsum("bse,ed->bsd", merged, w_o, preferred_element_type=jnp.float32).astype(jnp.bfloat16)
+        out_part, dy_full = lax.optimization_barrier((out_part, dy_full))
         out_loc = lax.psum_scatter(out_part, "tp", scatter_dimension=1, tiled=True)
-        y_loc = (x_loc.astype(jnp.float32) + out_loc.astype(jnp.float32) + b_o).astype(jnp.bfloat16)
 
-        grad_bo = lax.psum(jnp.sum(dy_loc, axis=(0, 1), dtype=jnp.float32), "tp")
-        dy_full = lax.all_gather(dy_loc, "tp", axis=1, tiled=True)
-        grad_wo = jnp.einsum("bse,bsd->ed", merged, dy_full, preferred_element_type=jnp.float32)
         grad_att = jnp.einsum("bsd,ed->bse", dy_full, w_o, preferred_element_type=jnp.float32).astype(jnp.bfloat16)
         grad_q, kv_wide = attn_backward(grad_att.reshape(q_heads.shape), q_heads, key_rows, value_rows, attn_prob, prob_lo)
         grad_q = grad_q.reshape(queries.shape)
-        grad_kv = kv_wide.astype(jnp.bfloat16)
+        grad_kv = lax.psum(kv_wide.astype(jnp.bfloat16), "tp")
+        grad_h_part = jnp.einsum("bse,de->bsd", grad_q, w_q, preferred_element_type=jnp.float32).astype(jnp.bfloat16)
+        grad_h_part, grad_q, merged, out_loc = lax.optimization_barrier((grad_h_part, grad_q, merged, out_loc))
+        grad_h = lax.psum_scatter(grad_h_part, "tp", scatter_dimension=1, tiled=True).astype(jnp.float32)
+
+        y_loc = (x_loc.astype(jnp.float32) + out_loc.astype(jnp.float32) + b_o).astype(jnp.bfloat16)
+        grad_wo = jnp.einsum("bse,bsd->ed", merged, dy_full, preferred_element_type=jnp.float32)
         grad_wq = jnp.einsum("bsd,bse->de", normed_full, grad_q, preferred_element_type=jnp.float32)
         grad_bq = jnp.sum(grad_q, axis=(0, 1), dtype=jnp.float32)
-        grad_wkv, grad_bkv = lax.psum((jnp.einsum("bsd,bsc->dc", normed_full, grad_kv, preferred_element_type=jnp.float32), jnp.sum(grad_kv, axis=(0, 1), dtype=jnp.float32)), "tp")
-        grad_h_part = (jnp.einsum("bse,de->bsd", grad_q, w_q, preferred_element_type=jnp.float32) + jnp.einsum("bsc,dc->bsd", grad_kv, w_kv, preferred_element_type=jnp.float32)).astype(jnp.bfloat16)
-        grad_h = lax.psum_scatter(grad_h_part, "tp", scatter_dimension=1, tiled=True).astype(jnp.float32)
+        grad_wkv = jnp.einsum("bsd,bsc->dc", normed_full, grad_kv, preferred_element_type=jnp.float32)
+        grad_bkv = jnp.sum(grad_kv, axis=(0, 1), dtype=jnp.float32)
+        own_rows = x_loc.shape[1]
+        kv_loc = lax.dynamic_slice_in_dim(grad_kv, lax.axis_index("tp") * own_rows, own_rows, axis=1)
+        grad_h = grad_h + jnp.einsum("bsc,dc->bsd", kv_loc, w_kv, preferred_element_type=jnp.float32)
         grad_in, gamma_part, beta_part = norm_backward(grad_h, x_hat, inv_std, ln_gamma)
-        grad_gamma, grad_beta = lax.psum((gamma_part, beta_part), "tp")
+        grad_gamma, grad_beta, grad_bo = lax.psum((gamma_part, beta_part, grad_bo_part), "tp")
         grad_x = (dy_loc.astype(jnp.float32) + grad_in).astype(jnp.bfloat16)
         return (y_loc, grad_x, grad_gamma, grad_beta, grad_wq, grad_bq, grad_wkv, grad_bkv, grad_wo, grad_bo)
 

time: 1460 us -> 1130 us (0.77)
  waiting for transfers between devices: 805 us -> 515 us
  matrix products: 565 us -> 527 us
    reduce_scatter x1, waiting for transfers between devices: 238 us -> 3.65 us  [device_block(): out_loc = lax.psum_scatter(out_part, 'tp', scatter_dimension=1, tiled=True)]
    all_gather x1, waiting for transfers between devices: 170 us -> 53.2 us  [device_block(): dy_full = lax.all_gather(dy_loc, 'tp', axis=1, tiled=True)]
    psum x2, waiting for transfers between devices: 68.6 us -> 106 us  [the longest x1 59.9 us: device_block(): grad_kv = lax.psum(kv_wide.astype(jnp.bfloat16), 'tp')]
    reduce_scatter x1, waiting for transfers between devices: 103 us -> 126 us  [device_block(): lax.psum_scatter(grad_h_part, 'tp', scatter_dimension=1, tiled=True)]
    dot_general x1, matrix products: 36.1 us -> 13.9 us  [device_block(): jnp.einsum('bsc,dc->bsd', kv_loc, w_kv, preferred_element_type=jnp.float32)]
    dot_general x1, matrix products: 63.9 us -> 47.6 us  [device_block(): jnp.einsum('bse,de->bsd', grad_q, w_q, preferred_element_type=jnp.float32)]
  transfers between devices with their start and end apart: 6 -> 6, of which waited for: 6 -> 6; matrix products, arithmetic and copies ran while one was open for 18% -> 48% of each run, Pallas kernels for 0% -> 0%
where the time goes in v1:
time: 1130 us; the launch traced here: 1120 us
  matrix products  527 us (47%)
  waiting for transfers between devices  515 us (46%)
  other arithmetic  40.5 us (4%)
  local copies, waits for them, and re-layouts  22 us (2%)
  between operations  14.8 us (1%)
    all_gather x1, waiting for transfers between devices, device_block(): normed_full = lax.all_gather(normed, 'tp', axis=1, tiled=True)  225 us
    reduce_scatter x1, waiting for transfers between devices, device_block(): lax.psum_scatter(grad_h_part, 'tp', scatter_dimension=1, tiled=True)  126 us
    psum x1, waiting for transfers between devices, device_block(): grad_kv = lax.psum(kv_wide.astype(jnp.bfloat16), 'tp')  59.9 us
    all_gather x1, waiting for transfers between devices, device_block(): dy_full = lax.all_gather(dy_loc, 'tp', axis=1, tiled=True)  53.2 us
    dot_general x1, matrix products, attn_backward(): jnp.einsum('bhqk,bqhc->bkc', grad_score, q_heads, preferred_element_type=...  50.7 us
    dot_general x1, matrix products, attn_backward(): jnp.einsum('bhqk,bkc->bqhc', grad_score, key_rows, preferred_element_type...  50.6 us
    dot_general x1, matrix products, device_block(): jnp.einsum('bse,de->bsd', grad_q, w_q, preferred_element_type=jnp.float32)  47.6 us
    dot_general x1, matrix products, device_block(): jnp.einsum('bse,ed->bsd', merged, w_o, preferred_element_type=jnp.float32)  47.4 us
  transfers between devices with their start and end apart: 6, of which 6 were waited for; matrix products, arithmetic and copies ran while one was open for 48% of the time, Pallas kernels for 0%

profile of v1, /device:TPU:112, one launch (start us, length us, event | category | flops | bytes accessed | tf_op | source)
XLA Modules:
  0.0 1120.6 jit_solution(7984333453421324685)
XLA Ops:
  7.3 3.8 convert_reduce_fusion
  11.2 4.7 fusion.24
  16.5 6.3 fusion.19
  24.4 225.0 %all-gather.3.cloned.1.call-done = bf16[8,512,6144]{2,1,0:T(8,128)(2,1)} async-done(((bf16[8,64,6144]{2,1,0:T(8,128)(2,1)}), bf16[8,512,6144]{2,1,0:T(8,128)(2,1)}) %all-gather.3.cloned.1.call-update) | async-done | bytes 50331664 | tf_op jit(solution)/shard_map/all_gather | solution.py:46
  249.4 46.8 %add_convert_fusion = bf16[8,512,768]{2,1,0:T(8,128)(2,1)} fusion(f32[768]{0:T(1024)S(1)} %copy-done.12, bf16[8,512,6144]{2,1,0:T(8,128)(2,1)} %all-gather.3.cloned.1.call-done, bf16[6144,768]{1,0:T(8,128)(2,1)} %param.13), kind=kOutput, calls=%fused_computation.47 | convolution fusion | flops 38660997120 | bytes 66063360 | tf_op jit(solution)/shard_map/bsd,de->bse/dot_general | solution.py:52
  296.2 8.6 copy.35
  304.9 22.3 %add_convert_fusion.1 = bf16[8,512,256]{2,1,0:T(8,128)(2,1)} fusion(f32[256]{0:T(256)S(1)} %copy-done.13, bf16[8,512,6144]{2,1,0:T(8,128)(2,1)} %all-gather.3.cloned.1.call-done, bf16[6144,256]{1,0:T(8,128)(2,1)S(1)} %copy-done), kind=kOutput, calls=%fused_computation.60 | convolution fusion | flops 12886999040 | bytes 55575552 | tf_op jit(solution)/shard_map/bsd,dc->bsc/dot_general | solution.py:54
  327.1 26.4 %fusion.65 = (f32[8,6,512]{2,1,0:T(8,128)S(1)}, f32[8,6,512,512]{2,3,1,0:T(8,128)}) fusion(pred[512,512]{0,1:T(8,128)(4,1)S(1)} %iota_compare_fusion, bf16[8,512,6,128]{1,3,2,0:T(8,128)(2,1)} %bitcast.129, bf16[8,512,256]{2,1,0:T(8,128)(2,1)} %add_convert_fusion.1), kind=kOutput, calls=%fused_computation.86 | convolution fusion | flops 3271557632 | bytes 58032128 | tf_op jit(solution)/shard_map/sub | solution.py:25
  353.6 20.2 %fusion.46 = bf16[8,128,6,512]{3,1,2,0:T(8,128)(2,1)} fusion(bf16[8,512,256]{2,1,0:T(8,128)(2,1)} %add_convert_fusion.1, f32[8,6,512,512]{2,3,1,0:T(8,128)} %get-tuple-element.33, f32[8,6,512]{2,1,0:T(8,128)S(1)} %get-tuple-element.32), kind=kOutput, calls=%fused_computation.63 | convolution fusion | flops 3249537024 | bytes 57769984 | tf_op jit(solution)/shard_map/bhqk,bkc->bqhc/dot_general | solution.py:27
  373.7 47.4 %convolution_convert_fusion.1 = bf16[8,512,6144]{2,1,0:T(8,128)(2,1)} fusion(bf16[8,512,768]{1,2,0:T(8,128)(2,1)} %bitcast.136, bf16[768,6144]{1,0:T(8,128)(2,1)} %param.17), kind=kOutput, calls=%fused_computation.10 | convolution fusion | flops 38679871488 | bytes 66060288 | tf_op jit(solution)/shard_map/bse,ed->bsd/dot_general | solution.py:61
  421.2 53.2 %all-gather.5.cloned.1.call-done = bf16[8,512,6144]{2,1,0:T(8,128)(2,1)} async-done(((bf16[8,64,6144]{2,1,0:T(8,128)(2,1)}), bf16[8,512,6144]{2,1,0:T(8,128)(2,1)}) %all-gather.5.cloned.1.call-update) | async-done | bytes 50331664 | tf_op jit(solution)/shard_map/all_gather | solution.py:47
  474.5 47.3 %fusion.43 = bf16[8,512,768]{2,1,0:T(8,128)(2,1)} fusion(bf16[8,512,6144]{2,1,0:T(8,128)(2,1)} %all-gather.5.cloned.1.call-done, bf16[768,6144]{1,0:T(8,128)(2,1)} %param.17), kind=kOutput, calls=%fused_computation.62 | convolution fusion | flops 38657851392 | bytes 66060288 | tf_op jit(solution)/shard_map/bsd,ed->bse/dot_general | solution.py:65
  521.8 8.6 copy.40
  530.4 14.0 %convolution_convert_fusion.2 = bf16[8,512,512,6]{2,1,3,0:T(8,128)(2,1)} fusion(bf16[8,512,6,128]{1,3,2,0:T(8,128)(2,1)} %bitcast.127, bf16[8,512,256]{2,1,0:T(8,128)(2,1)} %add_convert_fusion.1), kind=kOutput, calls=%fused_computation.30 | convolution fusion | flops 3233808384 | bytes 32505856 | tf_op jit(solution)/shard_map/bqhc,bkc->bhqk/dot_general | solution.py:32
  544.4 50.7 %bitcast_convert_fusion.1 = bf16[8,512,128]{1,2,0:T(8,128)(2,1)} fusion(bf16[8,512,6,128]{1,3,2,0:T(8,128)(2,1)} %bitcast.130, bf16[8,512,512,6]{2,1,3,0:T(8,128)(2,1)} %convolution_convert_fusion.2, f32[8,6,512,512]{2,3,1,0:T(8,128)} %get-tuple-element.33, f32[8,6,512]{2,1,0:T(8,128)S(1)} %get-tuple-element.32), kind=kOutput, calls=%fused_computation.69 | convolution fusion | flops 3335021056 | bytes 82935808 | tf_op jit(solution)/shard_map/bhqk,bqhc->bkc/dot_general | solution.py:36
  595.1 21.7 %bitcast_convert_fusion = bf16[8,512,128]{1,2,0:T(8,128)(2,1)} fusion(bf16[8,512,6,128]{1,3,2,0:T(8,128)(2,1)} %bitcast.128, f32[8,6,512,512]{2,3,1,0:T(8,128)} %get-tuple-element.33, f32[8,6,512]{2,1,0:T(8,128)S(1)} %get-tuple-element.32), kind=kOutput, calls=%fused_computation.68 | convolution fusion | flops 3246915584 | bytes 57769984 | tf_op jit(solution)/shard_map/bhqk,bqhc->bkc/dot_general | solution.py:37
  616.9 3.0 pad_maximum_fusion
  619.8 50.6 %fusion.42 = bf16[8,128,6,512]{3,1,2,0:T(8,128)(2,1)} fusion(bf16[8,512,512,6]{2,1,3,0:T(8,128)(2,1)} %convolution_convert_fusion.2, bf16[8,512,256]{2,1,0:T(8,128)(2,1)} %add_convert_fusion.1, f32[8,6,512,512]{2,3,1,0:T(8,128)} %get-tuple-element.33, f32[8,6,512]{2,1,0:T(8,128)S(1)} %get-tuple-element.32), kind=kOutput, calls=%fused_computation.61 | convolution fusion | flops 3337642496 | bytes 158597120 | tf_op jit(solution)/shard_map/bhqk,bkc->bqhc/dot_general | solution.py:35
  670.6 47.6 %convolution_convert_fusion = bf16[8,512,6144]{2,1,0:T(8,128)(2,1)} fusion(bf16[8,512,768]{1,2,0:T(8,128)(2,1)} %bitcast.131, bf16[6144,768]{1,0:T(8,128)(2,1)} %param.13), kind=kOutput, calls=%fused_computation.9 | convolution fusion | flops 38679871488 | bytes 66060288 | tf_op jit(solution)/shard_map/bse,de->bsd/dot_general | solution.py:69
  718.2 3.6 reduce-scatter.3.cloned.1.call-done
  722.0 59.9 %all-reduce.4.cloned.1.call-done = bf16[8,512,256]{1,2,0:T(8,128)(2,1)} async-done(((bf16[8,512,256]{1,2,0:T(8,128)(2,1)}), bf16[8,512,256]{1,2,0:T(8,128)(2,1)}) %all-reduce.4.cloned.1.call-update) | async-done | bytes 2097168 | tf_op jit(solution)/shard_map/psum | solution.py:68
  781.9 2.5 convert_reduce_fusion.3
  784.4 25.3 %convolution_bitcast_fusion.2 = f32[6144,256]{1,0:T(8,128)} fusion(bf16[8,512,6144]{2,1,0:T(8,128)(2,1)} %all-gather.3.cloned.1.call-done, bf16[8,512,256]{1,2,0:T(8,128)(2,1)} %all-reduce.4.cloned.1.call-done), kind=kOutput, calls=%fused_computation.57 | convolution fusion | flops 12884901888 | bytes 58720256 | tf_op jit(solution)/shard_map/bsd,bsc->dc/dot_general | solution.py:77
  809.7 46.9 %convolution_bitcast_fusion.1 = f32[768,6144]{1,0:T(8,128)} fusion(bf16[8,512,768]{1,2,0:T(8,128)(2,1)} %bitcast.137, bf16[8,512,6144]{2,1,0:T(8,128)(2,1)} %all-gather.5.cloned.1.call-done), kind=kOutput, calls=%fused_computation.49 | convolution fusion | flops 38654705664 | bytes 75497472 | tf_op jit(solution)/shard_map/bse,bsd->ed/dot_general | solution.py:74
  856.7 46.0 %convolution_bitcast_fusion = f32[6144,768]{1,0:T(8,128)} fusion(bf16[8,512,6144]{2,1,0:T(8,128)(2,1)} %all-gather.3.cloned.1.call-done, bf16[8,512,768]{1,2,0:T(8,128)(2,1)S(1)} %bitcast.135), kind=kOutput, calls=%fused_computation.48 | convolution fusion | flops 38654705664 | bytes 75497472 | tf_op jit(solution)/shard_map/bsd,bse->de/dot_general | solution.py:75
  902.7 126.2 %reduce-scatter.5.cloned.1.call-done = bf16[8,64,6144]{2,1,0:T(8,128)(2,1)} async-done(((bf16[8,512,6144]{2,1,0:T(8,128)(2,1)}), bf16[8,64,6144]{2,1,0:T(8,128)(2,1)}) %reduce-scatter.5.cloned.1.call-update) | async-done | bytes 6291472 | tf_op jit(solution)/shard_map/reduce_scatter | solution.py:71
  1028.9 13.9 %fusion.23 = (f32[6144]{0:T(1024)}, f32[8,64]{1,0:T(8,128)S(1)}, f32[8,64]{1,0:T(8,128)S(1)}, f32[6144]{0:T(1024)}, f32[8,64,6144]{2,1,0:T(8,128)}) fusion(bf16[8,64,6144]{2,1,0:T(8,128)(2,1)} %param.10, f32[8,64]{1,0:T(8,128)S(1)} %copy-done.9, f32[8,64]{1,0:T(8,128)S(1)} %copy-done.7, f32[6144]{0:T(1024)S(1)} %copy-done.5, ...), kind=kOutput, calls=%fused_computation.36 | convolution fusion | flops 1648348160 | bytes 28917764 | tf_op jit(solution)/shard_map/bsc,dc->bsd/dot_general | solution.py:81
  1042.8 15.8 %convert_reduce_fusion.1 = (f32[6144]{0:T(1024)}, bf16[8,64,6144]{2,1,0:T(8,128)(2,1)}, bf16[8,64,6144]{2,1,0:T(8,128)(2,1)}) fusion(bf16[8,64,6144]{2,1,0:T(8,128)(2,1)S(1)} %copy-done.3, f32[8,64]{1,0:T(8,128)S(1)} %get-tuple-element.35, f32[8,64]{1,0:T(8,128)S(1)} %copy-done.7, bf16[8,64,6144]{2,1,0:T(8,128)(2,1)S(1)} %copy-done.2, ...), kind=kLoop, calls=%fused_computation.22 | loop fusion | flops 50325504 | bytes 44122112 | tf_op jit(solution)/shard_map/reduce_sum | solution.py:48
  1058.6 4.3 convert_reduce_fusion.2
  1062.9 46.2 %all-reduce.6.cloned.1.call-done = (f32[6144]{0:T(1024)}, f32[6144]{0:T(1024)}, f32[6144]{0:T(1024)}) async-done(((f32[6144]{0:T(1024)}, f32[6144]{0:T(1024)}, f32[6144]{0:T(1024)}), (f32[6144]{0:T(1024)}, f32[6144]{0:T(1024)}, f32[6144]{0:T(1024)})) %all-reduce.6.cloned.1.call-update) | async-done | bytes 73744 | tf_op jit(solution)/shard_map/psum | solution.py:83
  1109.2 1.3 copy.75
  1110.5 1.3 copy.76
  (50 shorter events, 4.0 us)
Async XLA Ops:
  7.2 297.7 %copy-start = (bf16[6144,256]{1,0:T(8,128)(2,1)S(1)}, bf16[6144,256]{1,0:T(8,128)(2,1)}, u32[]{:S(2)}) copy-start(bf16[6144,256]{1,0:T(8,128)(2,1)} %param.15) | copy-start | bytes 9437188
  7.2 9.3 copy-start.4
  7.2 9.3 copy-start.11
  7.2 242.2 %all-gather.3.cloned.1.call-start = ((), (), s32[]{:S(2)}) async-start(), calls=%async_computation.2 | async-start | bytes 56623104 | tf_op jit(solution)/shard_map/all_gather | solution.py:46
  7.3 9.2 copy-start.1
  11.2 4.7 copy-start.6
  15.9 0.6 copy-start.8
  16.5 232.9 %copy-start.12 = (f32[768]{0:T(1024)S(1)}, f32[768]{0:T(1024)}, u32[]{:S(2)}) copy-start(f32[768]{0:T(1024)} %param.14) | copy-start | bytes 9220
  22.9 451.4 %all-gather.5.cloned.1.call-start = ((), (), s32[]{:S(2)}) async-start(), calls=%async_computation.3 | async-start | bytes 56623104 | tf_op jit(solution)/shard_map/all_gather | solution.py:47
  23.7 698.1 %reduce-scatter.3.cloned.1.call-start = ((), (), s32[]{:S(2)}) async-start(), calls=%async_computation.4 | async-start | bytes 56623104 | tf_op jit(solution)/shard_map/reduce_scatter | solution.py:63
  296.2 8.6 copy-start.13
  474.4 307.5 %all-reduce.4.cloned.1.call-start = ((), (), s32[]{:S(2)}) async-start(), calls=%async_computation.6 | async-start | bytes 4194304 | tf_op jit(solution)/shard_map/psum | solution.py:68
  670.5 358.3 %reduce-scatter.5.cloned.1.call-start = ((), (), s32[]{:S(2)}) async-start(), calls=%async_computation.5 | async-start | bytes 56623104 | tf_op jit(solution)/shard_map/reduce_scatter | solution.py:71
  721.9 387.2 %all-reduce.6.cloned.1.call-start = ((), (), s32[]{:S(2)}) async-start(), calls=%async_computation.7 | async-start | bytes 147456 | tf_op jit(solution)/shard_map/psum | solution.py:83
  784.4 72.2 %slice-start = ((s8[6291456]{0:T(1024)(128)(4,1)}), s8[2097152]{0:T(1024)(128)(4,1)S(1)}, s32[]{:S(2)}) async-start(s8[6291456]{0:T(1024)(128)(4,1)} %bitcast.133), calls=%async_computation.8 | async-start | bytes 4194304
  809.7 46.9 %slice-start.1 = ((s8[6291456]{0:T(1024)(128)(4,1)}), s8[4194304]{0:T(1024)(128)(4,1)S(1)}, s32[]{:S(2)}) async-start(s8[6291456]{0:T(1024)(128)(4,1)} %bitcast.133), calls=%async_computation.9 | async-start | bytes 8388608
  856.7 172.2 %copy-start.5 = (f32[6144]{0:T(1024)S(1)}, f32[6144]{0:T(1024)}, u32[]{:S(2)}) copy-start(f32[6144]{0:T(1024)} %param.11) | copy-start | bytes 73732
  856.7 172.2 %copy-start.7 = (f32[8,64]{1,0:T(8,128)S(1)}, f32[8,64]{1,0:T(8,128)}, u32[]{:S(2)}) copy-start(f32[8,64]{1,0:T(8,128)} %copy-done.6) | copy-start | bytes 6148
  856.7 172.2 %copy-start.9 = (f32[8,64]{1,0:T(8,128)S(1)}, f32[8,64]{1,0:T(8,128)}, u32[]{:S(2)}) copy-start(f32[8,64]{1,0:T(8,128)} %copy-done.8) | copy-start | bytes 6148
  902.7 140.1 %copy-start.10 = (f32[6144]{0:T(1024)S(1)}, f32[6144]{0:T(1024)}, u32[]{:S(2)}) copy-start(f32[6144]{0:T(1024)} %param.18) | copy-start | bytes 73732
  1028.9 13.9 %copy-start.2 = (bf16[8,64,6144]{2,1,0:T(8,128)(2,1)S(1)}, bf16[8,64,6144]{2,1,0:T(8,128)(2,1)}, u32[]{:S(2)}) copy-start(bf16[8,64,6144]{2,1,0:T(8,128)(2,1)} %param.10) | copy-start | bytes 18874372
  1028.9 13.9 %copy-start.3 = (bf16[8,64,6144]{2,1,0:T(8,128)(2,1)S(1)}, bf16[8,64,6144]{2,1,0:T(8,128)(2,1)}, u32[]{:S(2)}) copy-start(bf16[8,64,6144]{2,1,0:T(8,128)(2,1)} %param.19) | copy-start | bytes 18874372
Sparse Core Ops, SparseCore 0:
  23.0 226.3 all-gather.2
  251.0 223.2 all-gather.4
  476.7 245.0 reduce-scatter.2
  724.7 57.1 all-reduce.3
  784.1 244.7 reduce-scatter.4
  1058.8 50.3 all-reduce.5

commit v2 on v1

v2 whole, which is shorter than its diff:
```python
import functools

import jax
import jax.numpy as jnp
from jax import lax
from jax.experimental import pallas as pl
from jax.experimental.pallas import tpu as pltpu
from jax.sharding import PartitionSpec as P

LN_EPS = 1e-5
VMEM_LIMIT = 60 * 1024 * 1024
BF16 = jnp.bfloat16
F32 = jnp.float32

RIGHT, LEFT, PART, FAR_R, FAR_L, PASS_L, PASS_R, PASS_F = range(8)


def norm_backward(grad_h, x_hat, inv_std, ln_gamma):
    grad_hat = grad_h * ln_gamma
    grad_in = inv_std * (grad_hat - jnp.mean(grad_hat, axis=-1, keepdims=True) - x_hat * jnp.mean(grad_hat * x_hat, axis=-1, keepdims=True))
    return grad_in, jnp.sum(grad_h * x_hat, axis=(0, 1)), jnp.sum(grad_h, axis=(0, 1))


def norm_stats(x_wide):
    centred = x_wide - jnp.mean(x_wide, axis=-1, keepdims=True)
    inv_std = lax.rsqrt(jnp.mean(centred * centred, axis=-1, keepdims=True) + LN_EPS)
    return centred * inv_std, inv_std


def block_probs(q_blk, keys, first_row, scale):
    scores = lax.dot_general(q_blk, keys, (((1,), (1,)), ((), ())), preferred_element_type=F32) * scale
    rows = lax.broadcasted_iota(jnp.int32, scores.shape, 0) + first_row
    cols = lax.broadcasted_iota(jnp.int32, scores.shape, 1)
    scores = jnp.where(rows >= cols, scores, -1e30)
    weights = jnp.exp(scores - jnp.max(scores, axis=-1, keepdims=True))
    return weights / jnp.sum(weights, axis=-1, keepdims=True)


def attend(qkv, out, heads, dim):
    rows = qkv.shape[0]
    width = heads * dim

    @pl.loop(0, heads)
    def _(h):
        lanes = pl.ds(pl.multiple_of(h * dim, dim), dim)
        for first in range(0, rows, dim):
            last = first + dim
            probs = block_probs(qkv[first:last, lanes], qkv[:last, width : width + dim], first, dim**-0.5).astype(BF16)
            out[first:last, lanes] = jnp.dot(probs, qkv[:last, width + dim :], preferred_element_type=F32).astype(BF16)


def attend_backward(qkv, grad_att, grad_q, grad_kv, probs_s, scores_s, q_s, att_s, heads, dim):
    rows = qkv.shape[0]
    width = heads * dim
    scale = dim**-0.5
    grad_kv[...] = jnp.zeros_like(grad_kv)
    for first in range(0, rows, dim):
        last = first + dim

        @pl.loop(0, heads)
        def _(h):
            lanes = pl.ds(pl.multiple_of(h * dim, dim), dim)
            stack = pl.ds(pl.multiple_of(h * dim, dim), dim)
            keys = qkv[:last, width : width + dim]
            q_blk = qkv[first:last, lanes]
            a_blk = grad_att[first:last, lanes]
            probs = block_probs(q_blk, keys, first, scale)
            grad_p = lax.dot_general(a_blk, qkv[:last, width + dim :], (((1,), (1,)), ((), ())), preferred_element_type=F32)
            grad_p = grad_p.astype(BF16).astype(F32)
            row_dot = jnp.sum(probs * grad_p, axis=-1, keepdims=True)
            grad_s = (probs * (grad_p - row_dot) * scale).astype(BF16)
            grad_q[first:last, lanes] = jnp.dot(grad_s, keys, preferred_element_type=F32).astype(BF16)
            probs_s[stack, :last] = probs.astype(BF16)
            scores_s[stack, :last] = grad_s
            q_s[stack, :] = q_blk
            att_s[stack, :] = a_blk

        over_rows = (((0,), (0,)), ((), ()))
        grad_kv[:last, :dim] += lax.dot_general(scores_s[:, :last], q_s[...], over_rows, preferred_element_type=F32)
        grad_kv[:last, dim:] += lax.dot_general(probs_s[:, :last], att_s[...], over_rows, preferred_element_type=F32)


def gather_kernel(heads, dim, x_hbm, dy_hbm, gamma, beta, wq_hbm, wkv_hbm, bias, h_full, dy_full, qkv_out, att_out,
                  own, x_buf, w_buf, h_buf, qkv_buf, att_buf, send, recv, x_sem, dy_sem, keep_sem, w_sem, h_sem, out_sem):
    batch, rows, width = x_hbm.shape
    half = rows // 2
    units = 2 * batch
    ring = h_full.shape[1] // rows
    qkv_width = qkv_buf.shape[1]
    me = lax.axis_index("tp")
    partner = me + 1 - 2 * lax.rem(me, 2)
    right, left, far = lax.rem(me + 2, ring), lax.rem(me + ring - 2, ring), lax.rem(me + ring // 2, ring)

    barrier = pltpu.get_barrier_semaphore()
    for other in (left, right, partner):
        pl.semaphore_signal(barrier, inc=1, device_id={"tp": other}, device_id_type=pl.DeviceIdType.MESH)
    pl.semaphore_wait(barrier, 3)

    def block(full, b, owner, first=0, count=rows):
        return full.at[b, pl.ds(pl.multiple_of(owner * rows + first, half), count)]

    def remote(src, dst, kind, u, to):
        return pltpu.make_async_remote_copy(
            src_ref=src, dst_ref=dst, send_sem=send.at[kind, u], recv_sem=recv.at[kind, u],
            device_id={"tp": to}, device_id_type=pl.DeviceIdType.MESH)

    def move(kind, full, b, u):
        if kind in (RIGHT, LEFT, PART):
            src, dst = own.at[u], block(full, b, me)
        elif kind in (FAR_R, FAR_L):
            src = dst = block(full, b, left, 0, half) if kind == FAR_R else block(full, b, right, half, half)
        else:
            src = dst = block(full, b, {PASS_L: left, PASS_R: right, PASS_F: far}[kind])
        to = {RIGHT: right, FAR_R: right, LEFT: left, FAR_L: left}.get(kind, partner)
        return remote(src, dst, kind, u, to)

    def keep(full, b, u):
        return pltpu.make_async_copy(own.at[u], block(full, b, me), keep_sem.at[u])

    def load_x(b):
        return pltpu.make_async_copy(x_hbm.at[b], x_buf.at[lax.rem(b, 2)], x_sem.at[lax.rem(b, 2)])

    def load_dy(b):
        return pltpu.make_async_copy(dy_hbm.at[b], own.at[batch + b], dy_sem.at[b])

    def unit(u, low, high, act):
        @pl.when(jnp.logical_and(u >= low, u < jnp.minimum(high, batch)))
        def _():
            act(h_full, u, u)

        @pl.when(jnp.logical_and(u >= jnp.maximum(low, batch), u < high))
        def _():
            act(dy_full, u - batch, u)

    def normalise(b):
        load_x(b).wait()
        slot = lax.rem(b, 2)

        @pl.loop(0, rows, step=16)
        def _(r):
            at = pl.ds(pl.multiple_of(r, 16), 16)
            x_hat, _ = norm_stats(x_buf[slot, at, :].astype(F32))
            own[b, at, :] = (x_hat * gamma[...] + beta[...]).astype(BF16)

        @pl.when(b + 2 < batch)
        def _():
            load_x(b + 2).start()

    def launch(u):
        @pl.when(u < batch)
        def _():
            normalise(u)

        @pl.when(jnp.logical_and(u >= batch, u < units))
        def _():
            load_dy(u - batch).wait()

        def act(full, b, u):
            for kind in (RIGHT, LEFT, PART):
                move(kind, full, b, u).start()
            keep(full, b, u).start()

        unit(u, 0, units, act)

    load_x(0).start()
    load_x(1).start()
    weights = (pltpu.make_async_copy(wq_hbm, w_buf.at[:, pl.ds(0, heads * dim)], w_sem.at[0]),
               pltpu.make_async_copy(wkv_hbm, w_buf.at[:, pl.ds(heads * dim, 2 * dim)], w_sem.at[1]))
    launch(0)
    launch(1)
    for copy in weights:
        copy.start()
    for b in range(batch):
        load_dy(b).start()
    for copy in weights:
        copy.wait()

    def project(b):
        load = pltpu.make_async_copy(h_full.at[b], h_buf, h_sem.at[0])
        load.start()
        load.wait()

        @pl.loop(0, qkv_width, step=256)
        def _(n):
            at = pl.ds(pl.multiple_of(n, 256), 256)
            qkv_buf[:, at] = (jnp.dot(h_buf[...], w_buf[:, at], preferred_element_type=F32) + bias[:, at]).astype(BF16)

    def results(b):
        return (pltpu.make_async_copy(qkv_buf, qkv_out.at[b], out_sem.at[0]),
                pltpu.make_async_copy(att_buf, att_out.at[b], out_sem.at[1]))

    @pl.loop(0, units + 2)
    def _(s):
        def forward(full, b, u):
            move(RIGHT, full, b, u).wait_recv()
            move(FAR_R, full, b, u).start()
            move(LEFT, full, b, u).wait_recv()
            move(FAR_L, full, b, u).start()

        unit(s, 0, units, forward)
        launch(s + 2)

        def share(full, b, u):
            move(PASS_L, full, b, u).start()
            move(PASS_R, full, b, u).start()

        unit(s, 0, units, share)

        def share_far(full, b, u):
            move(FAR_R, full, b, u).wait_recv()
            move(FAR_L, full, b, u).wait_recv()
            move(PASS_F, full, b, u).start()

        unit(s - 1, 0, units, share_far)

        def complete(full, b, u):
            for kind in (PART, PASS_L, PASS_R, PASS_F):
                move(kind, full, b, u).wait_recv()
            keep(full, b, u).wait()

        unit(s - 2, 0, units, complete)

        @pl.when(jnp.logical_and(s >= 2, s < batch + 2))
        def _():
            b = s - 2

            @pl.when(b > 0)
            def _():
                for copy in results(b - 1):
                    copy.wait()

            project(b)
            attend(qkv_buf, att_buf, heads, dim)
            for copy in results(b):
                copy.start()

    for copy in results(batch - 1):
        copy.wait()

    @pl.loop(0, units)
    def _(u):
        def act(full, b, u):
            for kind in range(8):
                move(kind, full, b, u).wait_send()

        unit(u, 0, units, act)


def gather_and_attend(x_loc, dy_loc, gamma, beta, w_q, w_kv, bias, ring, dim):
    batch, rows, width = x_loc.shape
    q_width = w_q.shape[1]
    qkv_width = q_width + w_kv.shape[1]
    seq = rows * ring
    units = 2 * batch
    hbm = pl.BlockSpec(memory_space=pl.ANY)
    vmem = pl.BlockSpec(memory_space=pltpu.VMEM)
    dma = pltpu.SemaphoreType.DMA
    return pl.pallas_call(
        functools.partial(gather_kernel, q_width // dim, dim),
        name="gather_and_attend",
        out_shape=(
            jax.ShapeDtypeStruct((batch, seq, width), BF16), jax.ShapeDtypeStruct((batch, seq, width), BF16),
            jax.ShapeDtypeStruct((batch, seq, qkv_width), BF16), jax.ShapeDtypeStruct((batch, seq, q_width), BF16)),
        in_specs=[hbm, hbm, vmem, vmem, hbm, hbm, vmem],
        out_specs=(hbm, hbm, hbm, hbm),
        scratch_shapes=[
            pltpu.VMEM((units, rows, width), BF16), pltpu.VMEM((2, rows, width), BF16), pltpu.VMEM((width, qkv_width), BF16),
            pltpu.VMEM((seq, width), BF16), pltpu.VMEM((seq, qkv_width), BF16), pltpu.VMEM((seq, q_width), BF16),
            dma((8, units)), dma((8, units)), dma((2,)), dma((batch,)), dma((units,)), dma((2,)), dma((1,)), dma((2,))],
        compiler_params=pltpu.CompilerParams(collective_id=0, has_side_effects=True, vmem_limit_bytes=VMEM_LIMIT),
        cost_estimate=pl.CostEstimate(flops=2 * batch * seq * width * qkv_width, bytes_accessed=6 * batch * seq * width, transcendentals=0),
    )(x_loc, dy_loc, gamma, beta, w_q, w_kv, bias)


def attend_backward_kernel(heads, dim, qkv, grad_att, grad_q, grad_kv, total, probs_s, scores_s, q_s, att_s):
    attend_backward(qkv.at[0], grad_att.at[0], grad_q.at[0], total, probs_s, scores_s, q_s, att_s, heads, dim)
    grad_kv[0] = total[...].astype(BF16)


def attention_gradients(qkv, grad_att, dim):
    batch, seq, qkv_width = qkv.shape
    q_width = grad_att.shape[2]
    heads = q_width // dim
    one = lambda w: pl.BlockSpec((1, seq, w), lambda b: (b, 0, 0))
    return pl.pallas_call(
        functools.partial(attend_backward_kernel, heads, dim),
        name="attention_gradients",
        grid=(batch,),
        out_shape=(jax.ShapeDtypeStruct((batch, seq, q_width), BF16), jax.ShapeDtypeStruct((batch, seq, 2 * dim), BF16)),
        in_specs=[one(qkv_width), one(q_width)],
        out_specs=(one(q_width), one(2 * dim)),
        scratch_shapes=[
            pltpu.VMEM((seq, 2 * dim), F32), pltpu.VMEM((q_width, seq), BF16), pltpu.VMEM((q_width, seq), BF16),
            pltpu.VMEM((q_width, dim), BF16), pltpu.VMEM((q_width, dim), BF16)],
        compiler_params=pltpu.CompilerParams(vmem_limit_bytes=VMEM_LIMIT // 2),
        cost_estimate=pl.CostEstimate(flops=batch * heads * seq * seq * dim * 12, bytes_accessed=batch * seq * qkv_width * 8, transcendentals=0),
    )(qkv, grad_att)


def solution(mesh):
    ring = mesh.shape["tp"]

    def device_block(x_loc, ln_gamma, ln_beta, w_q, b_q, w_kv, b_kv, w_o, b_o, dy_loc):
        head_dim = w_kv.shape[1] // 2
        bias = jnp.concatenate([b_q, b_kv])[None, :]
        normed_full, dy_full, qkv, merged = gather_and_attend(x_loc, dy_loc, ln_gamma[None, :], ln_beta[None, :], w_q, w_kv, bias, ring, head_dim)
        out_part = jnp.einsum("bse,ed->bsd", merged, w_o, preferred_element_type=jnp.float32).astype(jnp.bfloat16)
        out_part, dy_full = lax.optimization_barrier((out_part, dy_full))
        out_loc = lax.psum_scatter(out_part, "tp", scatter_dimension=1, tiled=True)

        grad_att = jnp.einsum("bsd,ed->bse", dy_full, w_o, preferred_element_type=jnp.float32).astype(jnp.bfloat16)
        grad_q, grad_kv = attention_gradients(qkv, grad_att, head_dim)
        grad_kv = lax.psum(grad_kv, "tp")
        grad_h_part = jnp.einsum("bse,de->bsd", grad_q, w_q, preferred_element_type=jnp.float32).astype(jnp.bfloat16)
        grad_h_part, grad_q, merged, out_loc = lax.optimization_barrier((grad_h_part, grad_q, merged, out_loc))
        grad_h = lax.psum_scatter(grad_h_part, "tp", scatter_dimension=1, tiled=True).astype(jnp.float32)

        grad_bo_part = jnp.sum(dy_loc, axis=(0, 1), dtype=jnp.float32)
        y_loc = (x_loc.astype(jnp.float32) + out_loc.astype(jnp.float32) + b_o).astype(jnp.bfloat16)
        grad_wo = jnp.einsum("bse,bsd->ed", merged, dy_full, preferred_element_type=jnp.float32)
        grad_wq = jnp.einsum("bsd,bse->de", normed_full, grad_q, preferred_element_type=jnp.float32)
        grad_bq = jnp.sum(grad_q, axis=(0, 1), dtype=jnp.float32)
        grad_wkv = jnp.einsum("bsd,bsc->dc", normed_full, grad_kv, preferred_element_type=jnp.float32)
        grad_bkv = jnp.sum(grad_kv, axis=(0, 1), dtype=jnp.float32)
        own_rows = x_loc.shape[1]
        kv_loc = lax.dynamic_slice_in_dim(grad_kv, lax.axis_index("tp") * own_rows, own_rows, axis=1)
        grad_h = grad_h + jnp.einsum("bsc,dc->bsd", kv_loc, w_kv, preferred_element_type=jnp.float32)
        x_hat, inv_std = norm_stats(x_loc.astype(jnp.float32))
        grad_in, gamma_part, beta_part = norm_backward(grad_h, x_hat, inv_std, ln_gamma)
        grad_gamma, grad_beta, grad_bo = lax.psum((gamma_part, beta_part, grad_bo_part), "tp")
        grad_x = (dy_loc.astype(jnp.float32) + grad_in).astype(jnp.bfloat16)
        return (y_loc, grad_x, grad_gamma, grad_beta, grad_wq, grad_bq, grad_wkv, grad_bkv, grad_wo, grad_bo)

    return jax.shard_map(
        device_block,
        mesh=mesh,
        in_specs=(P("dp", "tp", None), P(None), P(None), P(None, "tp"), P("tp"), P(None, None), P(None), P("tp", None), P(None), P("dp", "tp", None)),
        out_specs=(P("dp", "tp", None), P("dp", "tp", None), P("dp"), P("dp"), P("dp", "tp"), P(("dp", "tp")), P("dp", None), P("dp"), P(("dp", "tp"), None), P("dp")),
        check_vma=False,
    )
```

time: 1130 us -> 1120 us (level)
  Pallas kernels: 0 us -> 542 us
  waiting for transfers between devices: 515 us -> 238 us
  matrix products: 527 us -> 275 us
  local copies, waits for them, and re-layouts: 22 us -> 9.67 us
    pallas_call x0 -> x2, Pallas kernels: none -> 542 us  [the longest x1 418 us: gather_and_attend(): pl.pallas_call(functools.partial(gather_kernel, q_width // dim, dim), nam...]
    all_gather x2 -> x0, waiting for transfers between devices: 278 us -> none  [the longest x1 225 us: device_block(): normed_full = lax.all_gather(normed, 'tp', axis=1, tiled=True)]
    dot_general x7 -> x0, matrix products: 226 us -> none  [the longest x1 50.7 us: attn_backward(): jnp.einsum('bhqk,bqhc->bkc', grad_score, q_heads, preferred_element_type=...]
    sub x1 -> x0, matrix products: 26.4 us -> none  [attn_forward(): attn_prob = jax.nn.softmax(jnp.where(causal, scores, -1e+30), axis=-1)]
    reduce_scatter x1, waiting for transfers between devices: 3.65 us -> 22.5 us  [device_block(): out_loc = lax.psum_scatter(out_part, 'tp', scatter_dimension=1, tiled=True)]
    convert_element_type x2 -> x0, local copies, waits for them, and re-layouts: 17.3 us -> none  [the longest x1 8.64 us: device_block(): (jnp.einsum('bsd,de->bse', normed_full, w_q, preferred_element_type=jnp.f...]
  transfers between devices with their start and end apart: 6 -> 4, of which waited for: 6 -> 4; matrix products, arithmetic and copies ran while one was open for 48% -> 21% of each run, Pallas kernels for 0% -> 11%
where the time goes in v2:
time: 1120 us; the launch traced here: 1110 us
  Pallas kernels  542 us (48%)
  matrix products  275 us (25%)
  waiting for transfers between devices  238 us (21%)
  other arithmetic  32.1 us (3%)
  between operations  14 us (1%)
    pallas_call x1, Pallas kernels, gather_and_attend(): pl.pallas_call(functools.partial(gather_kernel, q_width // dim, dim), nam...  418 us
    pallas_call x1, Pallas kernels, attention_gradients(): pl.pallas_call(functools.partial(attend_backward_kernel, heads, dim), nam...  124 us
    reduce_scatter x1, waiting for transfers between devices, device_block(): lax.psum_scatter(grad_h_part, 'tp', scatter_dimension=1, tiled=True)  122 us
    psum x1, waiting for transfers between devices, device_block(): grad_kv = lax.psum(grad_kv, 'tp')  51.6 us
    dot_general x1, matrix products, device_block(): jnp.einsum('bse,ed->bsd', merged, w_o, preferred_element_type=jnp.float32)  48.3 us
    dot_general x1, matrix products, device_block(): jnp.einsum('bsd,bse->de', normed_full, grad_q, preferred_element_type=jnp...  48.2 us
    dot_general x1, matrix products, device_block(): jnp.einsum('bse,bsd->ed', merged, dy_full, preferred_element_type=jnp.flo...  47.8 us
    dot_general x1, matrix products, device_block(): jnp.einsum('bse,de->bsd', grad_q, w_q, preferred_element_type=jnp.float32)  47.3 us
  transfers between devices with their start and end apart: 4, of which 4 were waited for; matrix products, arithmetic and copies ran while one was open for 21% of the time, Pallas kernels for 11%

profile of v2, /device:TPU:112, one launch (start us, length us, event | category | flops | bytes accessed | tf_op | source)
XLA Modules:
  0.0 1112.0 jit_solution(18194269564405672566)
XLA Ops:
  7.2 0.1 reduce-scatter.3.cloned.1.call-start
  7.3 1.3 pad_maximum_fusion
  8.6 417.9 %gather_and_attend.1 = (bf16[8,512,6144]{2,1,0:T(8,128)(2,1)}, bf16[8,512,6144]{2,1,0:T(8,128)(2,1)}, bf16[8,512,1024]{2,1,0:T(8,128)(2,1)}, bf16[8,512,768]{2,1,0:T(8,128)(2,1)}) custom-call(bf16[8,64,6144]{2,1,0:T(8,128)(2,1)} %x_hbm.1, bf16[8,64,6144]{2,1,0:T(8,128)(2,1)} %dy_hbm.1, f32[1,6144]{1,0:T(1,128)} %bitcast.35, f32[1,6144]{1,0:T(1,128)} %bitcast.37, ...), custom_call_target="tpu_custom_call" | custom-call | flops 51539607552 | bytes 150994944 | tf_op jit(solution)/shard_map/gather_and_attend/pallas_call | solution.py:258
  426.5 48.3 %convolution_convert_fusion.1 = bf16[8,512,6144]{2,1,0:T(8,128)(2,1)} fusion(bf16[8,512,768]{2,1,0:T(8,128)(2,1)} %get-tuple-element.33, bf16[768,6144]{1,0:T(8,128)(2,1)} %param.17), kind=kOutput, calls=%fused_computation.1 | convolution fusion | flops 38679871488 | bytes 66060288 | tf_op jit(solution)/shard_map/bse,ed->bsd/dot_general | solution.py:307
  474.8 0.1 reduce-scatter.3.cloned.1.call-update
  474.8 0.2 all-reduce.4.cloned.1.call-start
  475.1 47.2 %fusion.17.grad_att = bf16[8,512,768]{2,1,0:T(8,128)(2,1)} fusion(bf16[8,512,6144]{2,1,0:T(8,128)(2,1)} %get-tuple-element.25, bf16[768,6144]{1,0:T(8,128)(2,1)} %param.17), kind=kOutput, calls=%fused_computation.31 | convolution fusion | flops 38657851392 | bytes 66060288 | tf_op jit(solution)/shard_map/bsd,ed->bse/dot_general | solution.py:311
  522.3 2.9 copy-done.2
  525.2 123.9 %attention_gradients.1 = (bf16[8,512,768]{2,1,0:T(8,128)(2,1)S(1)}, bf16[8,512,256]{2,1,0:T(8,128)(2,1)}) custom-call(bf16[8,512,1024]{2,1,0:T(8,128)(2,1)S(1)} %copy-done.1, bf16[8,512,768]{2,1,0:T(8,128)(2,1)S(1)} %copy-done.2), custom_call_target="tpu_custom_call" | custom-call | flops 19327352832 | bytes 33554432 | tf_op jit(solution)/shard_map/attention_gradients/pallas_call | solution.py:285
  649.2 2.7 copy-done
  651.8 0.1 all-reduce.4.cloned.1.call-update
  651.9 0.3 reduce-scatter.5.cloned.1.call-start
  652.2 47.3 %convolution_convert_fusion = bf16[8,512,6144]{2,1,0:T(8,128)(2,1)} fusion(bf16[8,512,768]{2,1,0:T(8,128)(2,1)} %copy-done, bf16[6144,768]{1,0:T(8,128)(2,1)} %wq_hbm.1), kind=kOutput, calls=%fused_computation | convolution fusion | flops 38679871488 | bytes 66060288 | tf_op jit(solution)/shard_map/bse,de->bsd/dot_general | solution.py:314
  699.5 22.5 %reduce-scatter.3.cloned.1.call-done = bf16[8,64,6144]{2,1,0:T(8,128)(2,1)} async-done(((bf16[8,512,6144]{2,1,0:T(8,128)(2,1)}), bf16[8,64,6144]{2,1,0:T(8,128)(2,1)}) %reduce-scatter.3.cloned.1.call-update) | async-done | bytes 6291472 | tf_op jit(solution)/shard_map/reduce_scatter | solution.py:309
  721.9 0.1 reduce-scatter.5.cloned.1.call-update
  722.0 0.1 all-reduce.6.cloned.1.call-start
  722.1 3.7 convert_reduce_fusion
  725.8 4.7 fusion.9
  730.4 51.6 %all-reduce.4.cloned.1.call-done = bf16[8,512,256]{2,1,0:T(8,128)(2,1)} async-done(((bf16[8,512,256]{2,1,0:T(8,128)(2,1)}), bf16[8,512,256]{2,1,0:T(8,128)(2,1)}) %all-reduce.4.cloned.1.call-update) | async-done | bytes 2097168 | tf_op jit(solution)/shard_map/psum | solution.py:313
  782.0 2.7 convert_reduce_fusion.3
  784.7 26.9 %convolution_bitcast_fusion.2 = f32[6144,256]{1,0:T(8,128)} fusion(bf16[8,512,6144]{2,1,0:T(8,128)(2,1)} %get-tuple-element.31, bf16[8,512,256]{2,1,0:T(8,128)(2,1)} %all-reduce.4.cloned.1.call-done), kind=kOutput, calls=%fused_computation.29 | convolution fusion | flops 12884901888 | bytes 58720256 | tf_op jit(solution)/shard_map/bsd,bsc->dc/dot_general | solution.py:323
  811.6 47.8 %convolution_bitcast_fusion.1 = f32[768,6144]{1,0:T(8,128)} fusion(bf16[8,512,768]{2,1,0:T(8,128)(2,1)} %get-tuple-element.33, bf16[8,512,6144]{2,1,0:T(8,128)(2,1)} %get-tuple-element.25), kind=kOutput, calls=%fused_computation.23 | convolution fusion | flops 38654705664 | bytes 75497472 | tf_op jit(solution)/shard_map/bse,bsd->ed/dot_general | solution.py:320
  859.5 48.2 %convolution_bitcast_fusion = f32[6144,768]{1,0:T(8,128)} fusion(bf16[8,512,6144]{2,1,0:T(8,128)(2,1)} %get-tuple-element.31, bf16[8,512,768]{2,1,0:T(8,128)(2,1)S(1)} %bitcast.34), kind=kOutput, calls=%fused_computation.22 | convolution fusion | flops 38654705664 | bytes 75497472 | tf_op jit(solution)/shard_map/bsd,bse->de/dot_general | solution.py:321
  907.7 121.6 %reduce-scatter.5.cloned.1.call-done = bf16[8,64,6144]{2,1,0:T(8,128)(2,1)} async-done(((bf16[8,512,6144]{2,1,0:T(8,128)(2,1)}), bf16[8,64,6144]{2,1,0:T(8,128)(2,1)}) %reduce-scatter.5.cloned.1.call-update) | async-done | bytes 6291472 | tf_op jit(solution)/shard_map/reduce_scatter | solution.py:316
  1029.3 9.8 fusion.8
  1039.1 15.4 %convert_reduce_fusion.1 = (f32[6144]{0:T(1024)}, bf16[8,64,6144]{2,1,0:T(8,128)(2,1)}, bf16[8,64,6144]{2,1,0:T(8,128)(2,1)}) fusion(bf16[8,64,6144]{2,1,0:T(8,128)(2,1)} %dy_hbm.1, f32[8,64]{1,0:T(8,128)S(1)} %get-tuple-element.45, f32[8,64]{1,0:T(8,128)S(1)} %broadcast_multiply_fusion.2, bf16[8,64,6144]{2,1,0:T(8,128)(2,1)} %x_hbm.1, ...), kind=kLoop, calls=%fused_computation.5 | loop fusion | flops 50325504 | bytes 44122112 | tf_op jit(solution)/shard_map/reduce_sum | solution.py:318
  1054.5 0.1 all-reduce.6.cloned.1.call-update
  1054.5 4.3 convert_reduce_fusion.2
  1058.8 42.4 %all-reduce.6.cloned.1.call-done = (f32[6144]{0:T(1024)}, f32[6144]{0:T(1024)}, f32[6144]{0:T(1024)}) async-done(((f32[6144]{0:T(1024)}, f32[6144]{0:T(1024)}, f32[6144]{0:T(1024)}), (f32[6144]{0:T(1024)}, f32[6144]{0:T(1024)}, f32[6144]{0:T(1024)})) %all-reduce.6.cloned.1.call-update) | async-done | bytes 73744 | tf_op jit(solution)/shard_map/psum | solution.py:330
  1101.3 1.3 copy.30
  1102.6 1.3 copy.31
  1104.0 1.3 copy.32
  (18 shorter events, 0.0 us)
Async XLA Ops:
  7.2 714.7 %reduce-scatter.3.cloned.1.call-start = ((), (), s32[]{:S(2)}) async-start(), calls=%async_computation.2 | async-start | bytes 56623104 | tf_op jit(solution)/shard_map/reduce_scatter | solution.py:309
  474.8 307.1 %all-reduce.4.cloned.1.call-start = ((), (), s32[]{:S(2)}) async-start(), calls=%async_computation.4 | async-start | bytes 4194304 | tf_op jit(solution)/shard_map/psum | solution.py:313
  475.1 47.2 %copy-start.1 = (bf16[8,512,1024]{2,1,0:T(8,128)(2,1)S(1)}, bf16[8,512,1024]{2,1,0:T(8,128)(2,1)}, u32[]{:S(2)}) copy-start(bf16[8,512,1024]{2,1,0:T(8,128)(2,1)} %get-tuple-element.22.qkv) | copy-start | bytes 25165828
  522.3 2.9 copy-start.2
  649.2 2.7 copy-start
  651.9 377.4 %reduce-scatter.5.cloned.1.call-start = ((), (), s32[]{:S(2)}) async-start(), calls=%async_computation.3 | async-start | bytes 56623104 | tf_op jit(solution)/shard_map/reduce_scatter | solution.py:316
  722.0 379.3 %all-reduce.6.cloned.1.call-start = ((), (), s32[]{:S(2)}) async-start(), calls=%async_computation.5 | async-start | bytes 147456 | tf_op jit(solution)/shard_map/psum | solution.py:330
  784.7 74.7 %slice-start = ((s8[6291456]{0:T(1024)(128)(4,1)}), s8[2097152]{0:T(1024)(128)(4,1)S(1)}, s32[]{:S(2)}) async-start(s8[6291456]{0:T(1024)(128)(4,1)} %bitcast.33), calls=%async_computation.6 | async-start | bytes 4194304
  811.6 47.8 %slice-start.1 = ((s8[6291456]{0:T(1024)(128)(4,1)}), s8[4194304]{0:T(1024)(128)(4,1)S(1)}, s32[]{:S(2)}) async-start(s8[6291456]{0:T(1024)(128)(4,1)} %bitcast.33), calls=%async_computation.7 | async-start | bytes 8388608
  859.4 169.8 %copy-start.3 = (f32[6144]{0:T(1024)S(1)}, f32[6144]{0:T(1024)}, u32[]{:S(2)}) copy-start(f32[6144]{0:T(1024)} %param.11) | copy-start | bytes 73732
  859.5 169.8 %copy-start.5 = (bf16[6144,256]{1,0:T(8,128)(2,1)S(1)}, bf16[6144,256]{1,0:T(8,128)(2,1)}, u32[]{:S(2)}) copy-start(bf16[6144,256]{1,0:T(8,128)(2,1)} %wkv_hbm.1) | copy-start | bytes 9437188
  907.7 131.4 %copy-start.4 = (f32[6144]{0:T(1024)S(1)}, f32[6144]{0:T(1024)}, u32[]{:S(2)}) copy-start(f32[6144]{0:T(1024)} %param.18) | copy-start | bytes 73732
Sparse Core Ops, SparseCore 0:
  475.0 246.9 reduce-scatter.2
  724.9 57.0 all-reduce.3
  784.4 244.8 reduce-scatter.4
  1054.7 46.5 all-reduce.5

commit v3 on v2

v3 whole, which is shorter than its diff:
```python
import functools

import jax
import jax.numpy as jnp
from jax import lax
from jax.experimental import pallas as pl
from jax.experimental.pallas import tpu as pltpu
from jax.sharding import PartitionSpec as P

LN_EPS = 1e-5
VMEM_LIMIT = 60 * 1024 * 1024
BF16 = jnp.bfloat16
F32 = jnp.float32

RIGHT, LEFT, PART, FAR_R, FAR_L, PASS_L, PASS_R, PASS_F = range(8)


def norm_stats(x_wide):
    centred = x_wide - jnp.mean(x_wide, axis=-1, keepdims=True)
    inv_std = lax.rsqrt(jnp.mean(centred * centred, axis=-1, keepdims=True) + LN_EPS)
    return centred * inv_std, inv_std


def causal_softmax(scores, first_row):
    rows = lax.broadcasted_iota(jnp.int32, scores.shape, 0) + first_row
    cols = lax.broadcasted_iota(jnp.int32, scores.shape, 1)
    scores = jnp.where(rows >= cols, scores, -1e30)
    weights = jnp.exp(scores - jnp.max(scores, axis=-1, keepdims=True))
    return weights / jnp.sum(weights, axis=-1, keepdims=True)


def attend(qkv, out, heads, dim):
    rows = qkv.shape[0]
    width = heads * dim

    @pl.loop(0, heads)
    def _(h):
        lanes = pl.ds(pl.multiple_of(h * dim, dim), dim)
        for first in range(0, rows, dim):
            last = first + dim
            scores = lax.dot_general(qkv[first:last, lanes], qkv[:last, width : width + dim], (((1,), (1,)), ((), ())), preferred_element_type=F32)
            probs = causal_softmax(scores * dim**-0.5, first).astype(BF16)
            out[first:last, lanes] = jnp.dot(probs, qkv[:last, width + dim :], preferred_element_type=F32).astype(BF16)


def attend_backward(qkv, grad_att, grad_q, grad_kv, scores_s, grad_p_s, probs_s, grad_s_s, q_s, att_s, heads, dim):
    rows = qkv.shape[0]
    width = heads * dim
    scale = dim**-0.5
    across = (((1,), (1,)), ((), ()))
    over_rows = (((0,), (0,)), ((), ()))
    chunk = dim // 2
    grad_kv[...] = jnp.zeros_like(grad_kv)
    for first in range(0, rows, dim):
        last = first + dim
        for h in range(heads):
            q_s[h * dim : (h + 1) * dim, :] = qkv[first:last, h * dim : (h + 1) * dim]
            att_s[h * dim : (h + 1) * dim, :] = grad_att[first:last, h * dim : (h + 1) * dim]
        keys = qkv[:last, width : width + dim]
        scores_s[:, :last] = lax.dot_general(q_s[...], keys, across, preferred_element_type=F32)
        grad_p_s[:, :last] = lax.dot_general(att_s[...], qkv[:last, width + dim :], across, preferred_element_type=F32)

        @pl.loop(0, width, step=chunk)
        def _(r):
            at = pl.ds(pl.multiple_of(r, chunk), chunk)
            row = first + lax.rem(r, dim)
            probs = causal_softmax(scores_s[at, :last] * scale, row)
            grad_p = grad_p_s[at, :last].astype(BF16).astype(F32)
            row_dot = jnp.sum(probs * grad_p, axis=-1, keepdims=True)
            grad_s_s[at, :last] = (probs * (grad_p - row_dot) * scale).astype(BF16)
            probs_s[at, :last] = probs.astype(BF16)

        stacked = jnp.dot(grad_s_s[:, :last], keys, preferred_element_type=F32).astype(BF16)
        for h in range(heads):
            grad_q[first:last, h * dim : (h + 1) * dim] = stacked[h * dim : (h + 1) * dim, :]
        grad_kv[:last, :dim] += lax.dot_general(grad_s_s[:, :last], q_s[...], over_rows, preferred_element_type=F32)
        grad_kv[:last, dim:] += lax.dot_general(probs_s[:, :last], att_s[...], over_rows, preferred_element_type=F32)


def gather_kernel(heads, dim, x_hbm, dy_hbm, gamma, beta, wq_hbm, wkv_hbm, bias, wo_hbm,
                  h_full, dy_full, qkv_out, att_out, dq_out, dkv_out, dbo,
                  own, x_buf, w_buf, wo_buf, h_buf, qkv_buf, att_buf, dq_buf, dkv_buf, total, scores_s, grad_p_s, probs_s, grad_s_s, q_s, att_s,
                  send, recv, x_sem, dy_sem, keep_sem, w_sem, h_sem, out_sem, back_sem):
    batch, rows, width = x_hbm.shape
    half = rows // 2
    units = 2 * batch
    ring = h_full.shape[1] // rows
    qkv_width = qkv_buf.shape[1]
    me = lax.axis_index("tp")
    partner = me + 1 - 2 * lax.rem(me, 2)
    right, left, far = lax.rem(me + 2, ring), lax.rem(me + ring - 2, ring), lax.rem(me + ring // 2, ring)

    barrier = pltpu.get_barrier_semaphore()
    for other in (left, right, partner):
        pl.semaphore_signal(barrier, inc=1, device_id={"tp": other}, device_id_type=pl.DeviceIdType.MESH)
    pl.semaphore_wait(barrier, 3)

    def block(full, b, owner, first=0, count=rows):
        return full.at[b, pl.ds(pl.multiple_of(owner * rows + first, half), count)]

    def remote(src, dst, kind, u, to):
        return pltpu.make_async_remote_copy(
            src_ref=src, dst_ref=dst, send_sem=send.at[kind, u], recv_sem=recv.at[kind, u],
            device_id={"tp": to}, device_id_type=pl.DeviceIdType.MESH)

    def move(kind, full, b, u):
        if kind in (RIGHT, LEFT, PART):
            src, dst = own.at[u], block(full, b, me)
        elif kind in (FAR_R, FAR_L):
            src = dst = block(full, b, left, 0, half) if kind == FAR_R else block(full, b, right, half, half)
        else:
            src = dst = block(full, b, {PASS_L: left, PASS_R: right, PASS_F: far}[kind])
        to = {RIGHT: right, FAR_R: right, LEFT: left, FAR_L: left}.get(kind, partner)
        return remote(src, dst, kind, u, to)

    def keep(full, b, u):
        return pltpu.make_async_copy(own.at[u], block(full, b, me), keep_sem.at[u])

    def load_x(b):
        return pltpu.make_async_copy(x_hbm.at[b], x_buf.at[lax.rem(b, 2)], x_sem.at[lax.rem(b, 2)])

    def load_dy(b):
        return pltpu.make_async_copy(dy_hbm.at[b], own.at[batch + b], dy_sem.at[b])

    def unit(u, low, high, act):
        @pl.when(jnp.logical_and(u >= low, u < jnp.minimum(high, batch)))
        def _():
            act(h_full, u, u)

        @pl.when(jnp.logical_and(u >= jnp.maximum(low, batch), u < high))
        def _():
            act(dy_full, u - batch, u)

    def normalise(b):
        load_x(b).wait()
        slot = lax.rem(b, 2)

        @pl.loop(0, rows, step=16)
        def _(r):
            at = pl.ds(pl.multiple_of(r, 16), 16)
            x_hat, _ = norm_stats(x_buf[slot, at, :].astype(F32))
            own[b, at, :] = (x_hat * gamma[...] + beta[...]).astype(BF16)

        @pl.when(b + 2 < batch)
        def _():
            load_x(b + 2).start()

    def launch(u):
        @pl.when(u < batch)
        def _():
            normalise(u)

        @pl.when(jnp.logical_and(u >= batch, u < units))
        def _():
            load_dy(u - batch).wait()

        def act(full, b, u):
            for kind in (RIGHT, LEFT, PART):
                move(kind, full, b, u).start()
            keep(full, b, u).start()

        unit(u, 0, units, act)

    load_x(0).start()
    load_x(1).start()
    weights = (pltpu.make_async_copy(wq_hbm, w_buf.at[:, pl.ds(0, heads * dim)], w_sem.at[0]),
               pltpu.make_async_copy(wkv_hbm, w_buf.at[:, pl.ds(heads * dim, 2 * dim)], w_sem.at[1]),
               pltpu.make_async_copy(wo_hbm, wo_buf, w_sem.at[2]))
    dbo[...] = jnp.zeros_like(dbo)
    launch(0)
    launch(1)
    for copy in weights:
        copy.start()
    for b in range(batch):
        load_dy(b).start()
    for copy in weights:
        copy.wait()

    def project(b):
        load = pltpu.make_async_copy(h_full.at[b], h_buf, h_sem.at[0])
        load.start()
        load.wait()

        @pl.loop(0, qkv_width, step=256)
        def _(n):
            at = pl.ds(pl.multiple_of(n, 256), 256)
            qkv_buf[:, at] = (jnp.dot(h_buf[...], w_buf[:, at], preferred_element_type=F32) + bias[:, at]).astype(BF16)

    def results(b):
        return (pltpu.make_async_copy(qkv_buf, qkv_out.at[b], out_sem.at[0]),
                pltpu.make_async_copy(att_buf, att_out.at[b], out_sem.at[1]))

    def back_results(b):
        return (pltpu.make_async_copy(dq_buf, dq_out.at[b], back_sem.at[0]),
                pltpu.make_async_copy(dkv_buf, dkv_out.at[b], back_sem.at[1]))

    def differentiate(b):
        load = pltpu.make_async_copy(dy_full.at[b], h_buf, h_sem.at[0])
        again = pltpu.make_async_copy(qkv_out.at[b], qkv_buf, h_sem.at[1])
        load.start()
        again.start()
        load.wait()

        @pl.loop(0, heads * dim, step=256)
        def _(n):
            at = pl.ds(pl.multiple_of(n, 256), 256)
            att_buf[:, at] = lax.dot_general(h_buf[...], wo_buf[at, :], (((1,), (1,)), ((), ())), preferred_element_type=F32).astype(BF16)

        @pl.loop(0, width, step=512)
        def _(n):
            at = pl.ds(pl.multiple_of(n, 512), 512)
            dbo[:, at] += jnp.sum(h_buf[:, at].astype(F32).reshape(-1, 8, 512), axis=0)

        again.wait()
        attend_backward(qkv_buf, att_buf, dq_buf, total, scores_s, grad_p_s, probs_s, grad_s_s, q_s, att_s, heads, dim)
        dkv_buf[...] = total[...].astype(BF16)

    @pl.loop(0, units + 2)
    def _(s):
        def forward(full, b, u):
            move(RIGHT, full, b, u).wait_recv()
            move(FAR_R, full, b, u).start()
            move(LEFT, full, b, u).wait_recv()
            move(FAR_L, full, b, u).start()

        unit(s, 0, units, forward)
        launch(s + 2)

        def share(full, b, u):
            move(PASS_L, full, b, u).start()
            move(PASS_R, full, b, u).start()

        unit(s, 0, units, share)

        def share_far(full, b, u):
            move(FAR_R, full, b, u).wait_recv()
            move(FAR_L, full, b, u).wait_recv()
            move(PASS_F, full, b, u).start()

        unit(s - 1, 0, units, share_far)

        def complete(full, b, u):
            for kind in (PART, PASS_L, PASS_R, PASS_F):
                move(kind, full, b, u).wait_recv()
            keep(full, b, u).wait()

        unit(s - 2, 0, units, complete)

        @pl.when(jnp.logical_and(s >= 2, s < batch + 2))
        def _():
            b = s - 2

            @pl.when(b > 0)
            def _():
                for copy in results(b - 1):
                    copy.wait()

            project(b)
            attend(qkv_buf, att_buf, heads, dim)
            for copy in results(b):
                copy.start()

        @pl.when(s >= batch + 2)
        def _():
            b = s - 2 - batch

            @pl.when(b == 0)
            def _():
                for copy in results(batch - 1):
                    copy.wait()

            @pl.when(b > 0)
            def _():
                for copy in back_results(b - 1):
                    copy.wait()

            differentiate(b)
            for copy in back_results(b):
                copy.start()

    for copy in back_results(batch - 1):
        copy.wait()

    @pl.loop(0, units)
    def _(u):
        def act(full, b, u):
            for kind in range(8):
                move(kind, full, b, u).wait_send()

        unit(u, 0, units, act)


def gather_and_attend(x_loc, dy_loc, gamma, beta, w_q, w_kv, bias, w_o, ring, dim):
    batch, rows, width = x_loc.shape
    q_width = w_q.shape[1]
    qkv_width = q_width + w_kv.shape[1]
    seq = rows * ring
    units = 2 * batch
    hbm = pl.BlockSpec(memory_space=pl.ANY)
    vmem = pl.BlockSpec(memory_space=pltpu.VMEM)
    dma = pltpu.SemaphoreType.DMA
    whole = lambda w: jax.ShapeDtypeStruct((batch, seq, w), BF16)
    return pl.pallas_call(
        functools.partial(gather_kernel, q_width // dim, dim),
        name="gather_and_attend",
        out_shape=(whole(width), whole(width), whole(qkv_width), whole(q_width), whole(q_width), whole(2 * dim), jax.ShapeDtypeStruct((8, width), F32)),
        in_specs=[hbm, hbm, vmem, vmem, hbm, hbm, vmem, hbm],
        out_specs=(hbm, hbm, hbm, hbm, hbm, hbm, vmem),
        scratch_shapes=[
            pltpu.VMEM((units, rows, width), BF16), pltpu.VMEM((2, rows, width), BF16), pltpu.VMEM((width, qkv_width), BF16),
            pltpu.VMEM((q_width, width), BF16), pltpu.VMEM((seq, width), BF16), pltpu.VMEM((seq, qkv_width), BF16), pltpu.VMEM((seq, q_width), BF16),
            pltpu.VMEM((seq, q_width), BF16), pltpu.VMEM((seq, 2 * dim), BF16), pltpu.VMEM((seq, 2 * dim), F32),
            pltpu.VMEM((q_width, seq), F32), pltpu.VMEM((q_width, seq), F32), pltpu.VMEM((q_width, seq), BF16), pltpu.VMEM((q_width, seq), BF16),
            pltpu.VMEM((q_width, dim), BF16), pltpu.VMEM((q_width, dim), BF16),
            dma((8, units)), dma((8, units)), dma((2,)), dma((batch,)), dma((units,)), dma((3,)), dma((2,)), dma((2,)), dma((2,))],
        compiler_params=pltpu.CompilerParams(collective_id=0, has_side_effects=True, vmem_limit_bytes=VMEM_LIMIT),
        cost_estimate=pl.CostEstimate(flops=4 * batch * seq * width * qkv_width, bytes_accessed=6 * batch * seq * width, transcendentals=0),
    )(x_loc, dy_loc, gamma, beta, w_q, w_kv, bias, w_o)


def scatter_kernel(att_hbm, dq_hbm, wo_hbm, wq_hbm, x_hbm, b_o, y_out, dh_out,
                   att_buf, dq_buf, wo_buf, wq_buf, stage, dh_buf, theirs, far_sum, near_sum, own_sum, far_in, near_in, x_buf, y_buf,
                   pair_send, pair_recv, far_send, far_recv, near_send, near_recv, free, load_sem, w_sem, dh_sem):
    batch, rows, width = x_hbm.shape
    ring = stage.shape[0] // rows
    half = width // 2
    tile = 512
    me = lax.axis_index("tp")
    partner = me + 1 - 2 * lax.rem(me, 2)
    right, left = lax.rem(me + 2, ring), lax.rem(me + ring - 2, ring)
    chips = ring // 2

    barrier = pltpu.get_barrier_semaphore()
    for other in (left, right, partner):
        pl.semaphore_signal(barrier, inc=1, device_id={"tp": other}, device_id_type=pl.DeviceIdType.MESH)
    pl.semaphore_wait(barrier, 3)

    def load(src, dst, n):
        return pltpu.make_async_copy(src, dst, load_sem.at[n])

    load_att = lambda b: load(att_hbm.at[b], att_buf, 0)
    load_dq = lambda b: load(dq_hbm.at[b], dq_buf, 1)
    load_x = lambda b: load(x_hbm.at[b], x_buf, 2)
    store_y = lambda b: load(y_buf, y_out.at[b], 3)
    load_wo = pltpu.make_async_copy(wo_hbm, wo_buf, w_sem.at[0])
    load_wq = pltpu.make_async_copy(wq_hbm, wq_buf, w_sem.at[1])

    def remote(src, dst, sems, to):
        return pltpu.make_async_remote_copy(
            src_ref=src, dst_ref=dst, send_sem=sems[0], recv_sem=sems[1], device_id={"tp": to}, device_id_type=pl.DeviceIdType.MESH)

    def block(owner):
        return pl.ds(pl.multiple_of(owner * rows, rows), rows)

    def pair(r):
        return remote(stage.at[block(lax.rem(partner + 2 * r, ring))], theirs.at[r], (pair_send.at[r], pair_recv.at[r]), partner)

    def far(u, way):
        cols = pl.ds(way * half, half)
        return remote(far_sum.at[lax.rem(u, 2), :, cols], far_in.at[lax.rem(u, 3), :, cols],
                      (far_send.at[lax.rem(u, 2), way], far_recv.at[lax.rem(u, 3), way]), (right, left)[way])

    def near(u, way):
        slot = lax.rem(u, 3)
        return remote(near_sum.at[slot, way], near_in.at[slot, way], (near_send.at[slot, way], near_recv.at[slot, way]), (right, left)[way])

    def columns(low, high, act):
        @pl.loop(low, high, step=tile)
        def _(n):
            act(pl.ds(pl.multiple_of(n, tile), tile))

    def part(u):
        load_att(u).wait()

        @pl.when(u > 0)
        def _():
            for r in range(chips):
                pair(r).wait_send()

        def act(at):
            stage[:, at] = jnp.dot(att_buf[...], wo_buf[:, at], preferred_element_type=F32).astype(BF16)

        columns(0, width, act)

        @pl.when(u + 1 < batch)
        def _():
            load_att(u + 1).start()

        @pl.when(u > 0)
        def _():
            pl.semaphore_wait(free, 1)

        for r in range(chips):
            pair(r).start()

    def combine(u):
        slot2, slot3 = lax.rem(u, 2), lax.rem(u, 3)
        for r in range(chips):
            pair(r).wait_recv()

        @pl.when(u >= 2)
        def _():
            for way in range(2):
                far(u - 2, way).wait_send()

        @pl.when(u >= 3)
        def _():
            for way in range(2):
                near(u - 3, way).wait_send()

        def chip_sum(r, at):
            return stage[block(lax.rem(me + 2 * r, ring)), at].astype(F32) + theirs[r, :, at].astype(F32)

        def act_far(at):
            far_sum[slot2, :, at] = chip_sum(chips // 2, at).astype(BF16)

        columns(0, width, act_far)
        for way in range(2):
            far(u, way).start()

        def act(at):
            near_sum[slot3, 0, :, at] = chip_sum(1, at).astype(BF16)
            near_sum[slot3, 1, :, at] = chip_sum(chips - 1, at).astype(BF16)
            own_sum[slot3, :, at] = chip_sum(0, at)

        columns(0, width, act)

        @pl.when(u + 1 < batch)
        def _():
            pl.semaphore_signal(free, inc=1, device_id={"tp": partner}, device_id_type=pl.DeviceIdType.MESH)

    def relay(u):
        slot = lax.rem(u, 3)
        for way in range(2):
            far(u, way).wait_recv()
        for way in range(2):
            def act(at):
                near_sum[slot, way, :, at] = (near_sum[slot, way, :, at].astype(F32) + far_in[slot, :, at].astype(F32)).astype(BF16)

            columns(way * half, way * half + half, act)
        for way in range(2):
            near(u, way).start()

    def finish(u):
        slot = lax.rem(u, 3)
        for way in range(2):
            near(u, way).wait_recv()
        load_x(u).wait()

        @pl.when(u > 0)
        def _():
            store_y(u - 1).wait()

        def act(at):
            total = own_sum[slot, :, at] + near_in[slot, 0, :, at].astype(F32) + near_in[slot, 1, :, at].astype(F32)
            y_buf[:, at] = (x_buf[:, at].astype(F32) + total + b_o[:, at]).astype(BF16)

        columns(0, width, act)
        store_y(u).start()

        @pl.when(u + 1 < batch)
        def _():
            load_x(u + 1).start()

    def store_dh(b, n):
        at = pl.ds(pl.multiple_of(n, tile), tile)
        slot = lax.rem(lax.div(n, tile), 2)
        return pltpu.make_async_copy(dh_buf.at[slot], dh_out.at[b, :, at], dh_sem.at[slot])

    def grad_part(b):
        load_dq(b).wait()

        @pl.loop(0, width, step=tile)
        def _(n):
            @pl.when(n >= 2 * tile)
            def _():
                store_dh(b, n - 2 * tile).wait()

            at = pl.ds(pl.multiple_of(n, tile), tile)
            dh_buf[lax.rem(lax.div(n, tile), 2)] = lax.dot_general(
                dq_buf[...], wq_buf[at, :], (((1,), (1,)), ((), ())), preferred_element_type=F32).astype(BF16)
            store_dh(b, n).start()

        @pl.when(b + 1 < batch)
        def _():
            load_dq(b + 1).start()

        for n in (width - 2 * tile, width - tile):
            store_dh(b, n).wait()

    load_att(0).start()
    load_wo.start()
    load_wq.start()
    load_dq(0).start()
    load_x(0).start()
    load_wo.wait()

    @pl.loop(0, batch + 3)
    def _(t):
        @pl.when(jnp.logical_and(t >= 1, t < batch + 1))
        def _():
            combine(t - 1)

        @pl.when(jnp.logical_and(t >= 2, t < batch + 2))
        def _():
            relay(t - 2)

        @pl.when(t >= 3)
        def _():
            finish(t - 3)

        @pl.when(t < batch)
        def _():
            part(t)

        @pl.when(t == 2)
        def _():
            load_wq.wait()

        @pl.when(jnp.logical_and(t >= 2, t < batch + 2))
        def _():
            grad_part(t - 2)

    for r in range(chips):
        pair(r).wait_send()
    for way in range(2):
        for u in (batch - 2, batch - 1):
            far(u, way).wait_send()
        for u in (batch - 3, batch - 2, batch - 1):
            near(u, way).wait_send()
    store_y(batch - 1).wait()


def project_and_scatter(merged, grad_q, w_o, w_q, x_loc, b_o, ring):
    batch, rows, width = x_loc.shape
    seq, q_width = merged.shape[1:]
    hbm = pl.BlockSpec(memory_space=pl.ANY)
    vmem = pl.BlockSpec(memory_space=pltpu.VMEM)
    dma = pltpu.SemaphoreType.DMA
    return pl.pallas_call(
        scatter_kernel,
        name="project_and_scatter",
        out_shape=(jax.ShapeDtypeStruct(x_loc.shape, BF16), jax.ShapeDtypeStruct((batch, seq, width), BF16)),
        in_specs=[hbm, hbm, hbm, hbm, hbm, vmem],
        out_specs=(hbm, hbm),
        scratch_shapes=[
            pltpu.VMEM((seq, q_width), BF16), pltpu.VMEM((seq, q_width), BF16), pltpu.VMEM((q_width, width), BF16), pltpu.VMEM((width, q_width), BF16),
            pltpu.VMEM((seq, width), BF16), pltpu.VMEM((2, seq, 512), BF16), pltpu.VMEM((ring // 2, rows, width), BF16),
            pltpu.VMEM((2, rows, width), BF16), pltpu.VMEM((3, 2, rows, width), BF16), pltpu.VMEM((3, rows, width), F32),
            pltpu.VMEM((3, rows, width), BF16), pltpu.VMEM((3, 2, rows, width), BF16), pltpu.VMEM((rows, width), BF16), pltpu.VMEM((rows, width), BF16),
            dma((ring // 2,)), dma((ring // 2,)), dma((2, 2)), dma((3, 2)), dma((3, 2)), dma((3, 2)), pltpu.SemaphoreType.REGULAR,
            dma((4,)), dma((2,)), dma((2,))],
        compiler_params=pltpu.CompilerParams(collective_id=1, has_side_effects=True, vmem_limit_bytes=VMEM_LIMIT),
        cost_estimate=pl.CostEstimate(flops=4 * batch * seq * width * q_width, bytes_accessed=4 * batch * seq * width, transcendentals=0),
    )(merged, grad_q, w_o, w_q, x_loc, b_o)


def norm_backward_kernel(dh, dkv, w_kv, x, dy, gamma, dx, sums):
    rows = x.shape[1]

    @pl.when(pl.program_id(0) == 0)
    def _():
        sums[...] = jnp.zeros_like(sums)

    @pl.loop(0, rows, step=16)
    def _(r):
        at = pl.ds(pl.multiple_of(r, 16), 16)
        from_kv = lax.dot_general(dkv[0, at, :], w_kv[...], (((1,), (1,)), ((), ())), preferred_element_type=F32)
        grad_h = dh[0, at, :].astype(F32) + from_kv
        x_hat, inv_std = norm_stats(x[0, at, :].astype(F32))
        grad_hat = grad_h * gamma[...]
        mean = jnp.mean(grad_hat, axis=-1, keepdims=True)
        along = jnp.mean(grad_hat * x_hat, axis=-1, keepdims=True)
        dx[0, at, :] = (dy[0, at, :].astype(F32) + inv_std * (grad_hat - mean - x_hat * along)).astype(BF16)
        by_sublane = lambda v: jnp.sum(v.reshape(-1, 8, v.shape[-1]), axis=0)
        sums[0] += by_sublane(grad_h * x_hat)
        sums[1] += by_sublane(grad_h)


def norm_backward(grad_h, grad_kv, w_kv, x_loc, dy_loc, gamma):
    batch, rows, width = x_loc.shape
    one = pl.BlockSpec((1, rows, width), lambda b: (b, 0, 0))
    still = lambda shape: pl.BlockSpec(shape, lambda b: (0,) * len(shape))
    return pl.pallas_call(
        norm_backward_kernel,
        name="norm_backward",
        grid=(batch,),
        out_shape=(jax.ShapeDtypeStruct(x_loc.shape, BF16), jax.ShapeDtypeStruct((2, 8, width), F32)),
        in_specs=[one, pl.BlockSpec((1, rows, grad_kv.shape[-1]), lambda b: (b, 0, 0)), still(w_kv.shape), one, one, still(gamma.shape)],
        out_specs=(one, still((2, 8, width))),
        compiler_params=pltpu.CompilerParams(vmem_limit_bytes=VMEM_LIMIT // 2),
        cost_estimate=pl.CostEstimate(flops=2 * batch * rows * width * 256, bytes_accessed=8 * batch * rows * width, transcendentals=0),
    )(grad_h, grad_kv, w_kv, x_loc, dy_loc, gamma)


def settle(values):
    block = pl.BlockSpec((1,) + values.shape[1:], lambda b: (b, 0, 0))

    def body(src, dst):
        dst[...] = src[...]

    return pl.pallas_call(
        body, name="settle", grid=(values.shape[0],), out_shape=jax.ShapeDtypeStruct(values.shape, values.dtype), in_specs=[block], out_specs=block,
        cost_estimate=pl.CostEstimate(flops=values.size * 100, bytes_accessed=values.size * 4, transcendentals=0))(values)


def sum_kernel(ring, parts, out, gathered, send, recv):
    me = lax.axis_index("tp")
    barrier = pltpu.get_barrier_semaphore()
    others = [lax.rem(me + k, ring) for k in range(1, ring)]
    for other in others:
        pl.semaphore_signal(barrier, inc=1, device_id={"tp": other}, device_id_type=pl.DeviceIdType.MESH)
    pl.semaphore_wait(barrier, ring - 1)

    def copy(k):
        return pltpu.make_async_remote_copy(
            src_ref=parts, dst_ref=gathered.at[me], send_sem=send.at[k], recv_sem=recv.at[k],
            device_id={"tp": lax.rem(me + k, ring)}, device_id_type=pl.DeviceIdType.MESH)

    for k in range(1, ring):
        copy(k).start()
    gathered[me] = parts[...]
    for k in range(1, ring):
        copy(k).wait_recv()
    total = gathered[0]
    for k in range(1, ring):
        total = total + gathered[k]
    out[...] = total
    for k in range(1, ring):
        copy(k).wait_send()


def sum_over_ring(parts, ring):
    vmem = pl.BlockSpec(memory_space=pltpu.VMEM)
    return pl.pallas_call(
        functools.partial(sum_kernel, ring),
        name="sum_over_ring",
        out_shape=jax.ShapeDtypeStruct(parts.shape, F32),
        in_specs=[vmem],
        out_specs=vmem,
        scratch_shapes=[pltpu.VMEM((ring,) + parts.shape, F32), pltpu.SemaphoreType.DMA((ring,)), pltpu.SemaphoreType.DMA((ring,))],
        compiler_params=pltpu.CompilerParams(collective_id=2, has_side_effects=True),
    )(parts)


def solution(mesh):
    ring = mesh.shape["tp"]

    def device_block(x_loc, ln_gamma, ln_beta, w_q, b_q, w_kv, b_kv, w_o, b_o, dy_loc):
        head_dim = w_kv.shape[1] // 2
        own_rows, width = x_loc.shape[1:]
        bias = jnp.concatenate([b_q, b_kv])[None, :]
        normed_full, dy_full, _, merged, grad_q, grad_kv, bo_rows = gather_and_attend(
            x_loc, dy_loc, ln_gamma[None, :], ln_beta[None, :], w_q, w_kv, bias, w_o, ring, head_dim)
        grad_kv = lax.psum(grad_kv, "tp")
        y_loc, grad_h_part = project_and_scatter(merged, grad_q, w_o, w_q, x_loc, b_o[None, :], ring)
        grad_h = lax.psum_scatter(grad_h_part, "tp", scatter_dimension=1, tiled=True)

        grad_h_part, grad_q, merged, y_loc, bo_rows = lax.optimization_barrier((grad_h_part, grad_q, merged, y_loc, bo_rows))
        y_loc = settle(y_loc)
        grad_bo = jnp.sum(bo_rows, axis=0)
        grad_wo = jnp.einsum("bse,bsd->ed", merged, dy_full, preferred_element_type=jnp.float32)
        grad_wq = jnp.einsum("bsd,bse->de", normed_full, grad_q, preferred_element_type=jnp.float32)
        grad_bq = jnp.sum(grad_q, axis=(0, 1), dtype=jnp.float32)
        grad_wkv = jnp.einsum("bsd,bsc->dc", normed_full, grad_kv, preferred_element_type=jnp.float32)
        grad_bkv = jnp.sum(grad_kv, axis=(0, 1), dtype=jnp.float32)
        kv_loc = lax.dynamic_slice_in_dim(grad_kv, lax.axis_index("tp") * own_rows, own_rows, axis=1)
        grad_x, parts = norm_backward(grad_h, kv_loc, w_kv, x_loc, dy_loc, ln_gamma[None, :])
        sums = sum_over_ring(jnp.sum(parts, axis=1).reshape(-1, 128), ring).reshape(2, width)
        return (y_loc, grad_x, sums[0], sums[1], grad_wq, grad_bq, grad_wkv, grad_bkv, grad_wo, grad_bo)

    return jax.shard_map(
        device_block,
        mesh=mesh,
        in_specs=(P("dp", "tp", None), P(None), P(None), P(None, "tp"), P("tp"), P(None, None), P(None), P("tp", None), P(None), P("dp", "tp", None)),
        out_specs=(P("dp", "tp", None), P("dp", "tp", None), P("dp"), P("dp"), P("dp", "tp"), P(("dp", "tp")), P("dp", None), P("dp"), P(("dp", "tp"), None), P("dp")),
        check_vma=False,
    )
```

time: 1120 us -> 1060 us (0.946)
  Pallas kernels: 542 us -> 795 us
  matrix products: 275 us -> 123 us
  waiting for transfers between devices: 238 us -> 106 us
  other arithmetic: 32.1 us -> 10.3 us
    pallas_call x1 -> x4, Pallas kernels: 124 us -> 295 us  [the longest x1 240 us: project_and_scatter(): pl.pallas_call(scatter_kernel, name='project_and_scatter', out_shape=(jax...]
    dot_general x4 -> x0, matrix products: 153 us -> none  [the longest x1 48.3 us: device_block(): jnp.einsum('bse,ed->bsd', merged, w_o, preferred_element_type=jnp.float32)]
    pallas_call x1, Pallas kernels: 418 us -> 499 us  [gather_and_attend(): pl.pallas_call(functools.partial(gather_kernel, q_width // dim, dim), nam...]
    psum x1, waiting for transfers between devices: 51.6 us -> 0.01 us  [device_block(): grad_kv = lax.psum(grad_kv, 'tp')]
    psum x1 -> x0, waiting for transfers between devices: 42.4 us -> none  [device_block(): lax.psum((gamma_part, beta_part, grad_bo_part), 'tp')]
    reduce_scatter x1 -> x0, waiting for transfers between devices: 22.5 us -> none  [device_block(): out_loc = lax.psum_scatter(out_part, 'tp', scatter_dimension=1, tiled=True)]
    reduce_sum x3 -> x2, other arithmetic: 23.7 us -> 1.78 us  [the longest x1 1.12 us: device_block(): jnp.sum(parts, axis=1).reshape(-1, 128)]
    reduce_scatter x1, waiting for transfers between devices: 122 us -> 106 us  [device_block(): lax.psum_scatter(grad_h_part, 'tp', scatter_dimension=1, tiled=True)]
  transfers between devices with their start and end apart: 4 -> 2, of which waited for: 4 -> 1; matrix products, arithmetic and copies ran while one was open for 21% -> 12% of each run, Pallas kernels for 11% -> 23%
where the time goes in v3:
time: 1060 us
  Pallas kernels  795 us (75%)
  matrix products  123 us (12%)
  waiting for transfers between devices  106 us (10%)
  between operations  14.1 us (1%)
  local copies, waits for them, and re-layouts  13 us (1%)
    pallas_call x1, Pallas kernels, gather_and_attend(): pl.pallas_call(functools.partial(gather_kernel, q_width // dim, dim), nam...  499 us
    pallas_call x1, Pallas kernels, project_and_scatter(): pl.pallas_call(scatter_kernel, name='project_and_scatter', out_shape=(jax...  240 us
    reduce_scatter x1, waiting for transfers between devices, device_block(): lax.psum_scatter(grad_h_part, 'tp', scatter_dimension=1, tiled=True)  106 us
    dot_general x1, matrix products, device_block(): jnp.einsum('bsd,bse->de', normed_full, grad_q, preferred_element_type=jnp...  48.6 us
    dot_general x1, matrix products, device_block(): jnp.einsum('bse,bsd->ed', merged, dy_full, preferred_element_type=jnp.flo...  47.8 us
    pallas_call x1, Pallas kernels, norm_backward(): pl.pallas_call(norm_backward_kernel, name='norm_backward', grid=(batch,),...  37.3 us
    dot_general x1, matrix products, device_block(): jnp.einsum('bsd,bsc->dc', normed_full, grad_kv, preferred_element_type=jn...  26.9 us
  transfers between devices with their start and end apart: 2, of which 1 were waited for; matrix products, arithmetic and copies ran while one was open for 12% of the time, Pallas kernels for 23%

profile of v3, /device:TPU:112, one launch (start us, length us, event | category | flops | bytes accessed | tf_op | source)
XLA Modules:
  0.0 1061.3 jit_solution(3887405493038622389)
XLA Ops:
  7.2 0.1 all-reduce.2.cloned.1.call-start
  7.3 1.3 pad_maximum_fusion
  8.6 499.3 %gather_and_attend.1 = (bf16[8,512,6144]{2,1,0:T(8,128)(2,1)}, bf16[8,512,6144]{2,1,0:T(8,128)(2,1)}, bf16[8,512,1024]{2,1,0:T(8,128)(2,1)}, bf16[8,512,768]{2,1...) custom-call(bf16[8,64,6144]{2,1,0:T(8,128)(2,1)} %x.1, ...), custom_call_target="tpu_custom_call" | custom-call | flops 103079215104 | bytes 150994944 | tf_op jit(solution)/shard_map/gather_and_attend/pallas_call | solution.py:303
  507.9 0.1 all-reduce.2.cloned.1.call-update
  507.9 0.2 reduce-scatter.2.cloned.1.call-start
  508.2 240.3 %project_and_scatter.1 = (bf16[8,64,6144]{2,1,0:T(8,128)(2,1)}, bf16[8,512,6144]{2,1,0:T(8,128)(2,1)}) custom-call(bf16[8,512,768]{2,1,0:T(8,128)(2,1)} %get-tuple-element.35.att_hbm, bf16[8,512,768]{2,1,0:T(8,128)(2,1)} %get-tuple-element.34.dq_hbm, bf16[768,6144]{1,0:T(8,128)(2,1)} %wo_hbm.3, bf16[6144,768]{1,0:T(8,128)(2,1)} %wq_hbm.3, ...), custom_call_target="tpu_custom_call" | custom-call | flops 77309411328 | bytes 100663296 | tf_op jit(solution)/shard_map/project_and_scatter/pallas_call | solution.py:540
  748.5 0.0 copy-start.6
  748.5 0.1 reduce-scatter.2.cloned.1.call-update
  748.6 0.9 copy-done.6
  749.4 0.7 reduce_sum.39
  750.1 7.9 settle.1
  758.0 0.0 slice-start
  758.0 4.4 convert_reduce_fusion
  762.4 47.8 %convolution_bitcast_fusion.1 = f32[768,6144]{1,0:T(8,128)} fusion(bf16[8,512,768]{2,1,0:T(8,128)(2,1)} %get-tuple-element.35.att_hbm, bf16[8,512,6144]{2,1,0:T(8,128)(2,1)} %get-tuple-element.36), kind=kOutput, calls=%fused_computation.2 | convolution fusion | flops 38654705664 | bytes 75497472 | tf_op jit(solution)/shard_map/bse,bsd->ed/dot_general | solution.py:662
  810.2 0.0 slice-done
  810.2 0.0 slice-done.1
  810.2 48.6 %convolution_bitcast_fusion = f32[6144,768]{1,0:T(8,128)} fusion(bf16[8,512,6144]{2,1,0:T(8,128)(2,1)} %get-tuple-element.33, bf16[8,512,768]{2,1,0:T(8,128)(2,1)S(1)} %bitcast.23), kind=kOutput, calls=%fused_computation.1 | convolution fusion | flops 38654705664 | bytes 75497472 | tf_op jit(solution)/shard_map/bsd,bse->de/dot_general | solution.py:663
  858.8 1.0 constant_dynamic-slice_fusion.dkv
  859.8 2.8 convert_reduce_fusion.1
  862.6 26.9 %convolution_bitcast_fusion.2 = f32[6144,256]{1,0:T(8,128)} fusion(bf16[8,512,6144]{2,1,0:T(8,128)(2,1)} %get-tuple-element.33, bf16[8,512,256]{2,1,0:T(8,128)(2,1)} %all-reduce.2.cloned.1.call-done), kind=kOutput, calls=%fused_computation.3 | convolution fusion | flops 12884901888 | bytes 58720256 | tf_op jit(solution)/shard_map/bsd,bsc->dc/dot_general | solution.py:665
  889.5 105.6 %reduce-scatter.2.cloned.1.call-done.dh = bf16[8,64,6144]{2,1,0:T(8,128)(2,1)} async-done(((bf16[8,512,6144]{2,1,0:T(8,128)(2,1)}), bf16[8,64,6144]{2,1,0:T(8,128)(2,1)}) %reduce-scatter.2.cloned.1.call-update) | async-done | bytes 6291472 | tf_op jit(solution)/shard_map/reduce_scatter | solution.py:657
  995.1 0.0 copy-done.3
  995.1 0.0 copy-done.5
  995.1 2.8 copy-done
  997.9 2.8 copy-done.1
  1000.7 2.8 copy-done.2
  1003.5 37.3 %norm_backward.1 = (bf16[8,64,6144]{2,1,0:T(8,128)(2,1)}, f32[2,8,6144]{2,1,0:T(8,128)S(1)}) custom-call(bf16[8,64,6144]{2,1,0:T(8,128)(2,1)S(1)} %copy-done.2, bf16[8,64,256]{2,1,0:T(8,128)(2,1)S(1)} %constant_dynamic-slice_fusion.dkv, bf16[6144,256]{1,0:T(8,128)(2,1)S(1)} %copy-done.3, bf16[8,64,6144]{2,1,0:T(8,128)(2,1)S(1)} %copy-done, ...), custom_call_target="tpu_custom_call" | custom-call | flops 1610612736 | bytes 25165824 | tf_op jit(solution)/shard_map/norm_backward/pallas_call | solution.py:584
  1040.8 0.8 copy-done.4
  1041.5 1.1 reduce_sum.36
  1042.7 0.6 reshape.28.parts
  1043.3 9.8 sum_over_ring.1
  1053.1 1.4 slice_bitcast_fusion
  (9 shorter events, 0.0 us)
Async XLA Ops:
  7.2 851.6 %all-reduce.2.cloned.1.call-start = ((), (), s32[]{:S(2)}) async-start(), calls=%async_computation.2 | async-start | bytes 4194304 | tf_op jit(solution)/shard_map/psum | solution.py:655
  507.9 487.2 %reduce-scatter.2.cloned.1.call-start = ((), (), s32[]{:S(2)}) async-start(), calls=%async_computation.1 | async-start | bytes 56623104 | tf_op jit(solution)/shard_map/reduce_scatter | solution.py:657
  748.5 0.9 copy-start.6
  758.0 52.3 %slice-start = ((s8[6291456]{0:T(1024)(128)(4,1)}), s8[4194304]{0:T(1024)(128)(4,1)S(1)}, s32[]{:S(2)}) async-start(s8[6291456]{0:T(1024)(128)(4,1)} %bitcast.22), calls=%async_computation.3 | async-start | bytes 8388608
  762.4 47.8 %slice-start.1 = ((s8[6291456]{0:T(1024)(128)(4,1)}), s8[2097152]{0:T(1024)(128)(4,1)S(1)}, s32[]{:S(2)}) async-start(s8[6291456]{0:T(1024)(128)(4,1)} %bitcast.22), calls=%async_computation.4 | async-start | bytes 4194304
  862.6 132.5 %copy-start.3 = (bf16[6144,256]{1,0:T(8,128)(2,1)S(1)}, bf16[6144,256]{1,0:T(8,128)(2,1)}, u32[]{:S(2)}) copy-start(bf16[6144,256]{1,0:T(8,128)(2,1)} %w_kv.1) | copy-start | bytes 9437188
  862.6 132.5 %copy-start.5 = (f32[6144]{0:T(1024)S(1)}, f32[6144]{0:T(1024)}, u32[]{:S(2)}) copy-start(f32[6144]{0:T(1024)} %param.11) | copy-start | bytes 73732
  995.1 2.8 copy-start
  997.9 2.8 copy-start.1
  1000.7 2.8 copy-start.2
  1040.8 0.8 copy-start.4
Sparse Core Ops, SparseCore 0:
  508.0 71.6 all-reduce.1
  748.7 246.3 reduce-scatter.1

commit v4 on v3

--- a/solution.py
+++ b/solution.py
@@ -7,6 +7,7 @@
 from jax.experimental.pallas import tpu as pltpu
 from jax.sharding import PartitionSpec as P
 
+
 LN_EPS = 1e-5
 VMEM_LIMIT = 60 * 1024 * 1024
 BF16 = jnp.bfloat16
@@ -15,77 +16,82 @@
 RIGHT, LEFT, PART, FAR_R, FAR_L, PASS_L, PASS_R, PASS_F = range(8)
 
 
-def norm_stats(x_wide):
-    centred = x_wide - jnp.mean(x_wide, axis=-1, keepdims=True)
-    inv_std = lax.rsqrt(jnp.mean(centred * centred, axis=-1, keepdims=True) + LN_EPS)
-    return centred * inv_std, inv_std
-
-
-def causal_softmax(scores, first_row):
-    rows = lax.broadcasted_iota(jnp.int32, scores.shape, 0) + first_row
-    cols = lax.broadcasted_iota(jnp.int32, scores.shape, 1)
-    scores = jnp.where(rows >= cols, scores, -1e30)
-    weights = jnp.exp(scores - jnp.max(scores, axis=-1, keepdims=True))
-    return weights / jnp.sum(weights, axis=-1, keepdims=True)
-
-
-def attend(qkv, out, heads, dim):
+def stack_heads(rows, dst, first, heads, dim):
+    for h in range(heads):
+        dst[h * dim : (h + 1) * dim, :] = rows[first : first + dim, h * dim : (h + 1) * dim]
+
+
+def scaled_scores(scores_s, lanes, first, dim):
+    scores = scores_s[: first + dim, lanes] * dim**-0.5
+    keys = lax.broadcasted_iota(jnp.int32, scores.shape, 0)
+    queries = lax.broadcasted_iota(jnp.int32, scores.shape, 1) + first
+    return jnp.where(keys <= queries, scores, -1e30)
+
+
+ACROSS = (((1,), (1,)), ((), ()))
+DOWN = (((0,), (0,)), ((), ()))
+
+
+def attend(qkv, out, stats, scores_s, probs_s, q_s, heads, dim):
     rows = qkv.shape[0]
     width = heads * dim
-
-    @pl.loop(0, heads)
-    def _(h):
-        lanes = pl.ds(pl.multiple_of(h * dim, dim), dim)
-        for first in range(0, rows, dim):
-            last = first + dim
-            scores = lax.dot_general(qkv[first:last, lanes], qkv[:last, width : width + dim], (((1,), (1,)), ((), ())), preferred_element_type=F32)
-            probs = causal_softmax(scores * dim**-0.5, first).astype(BF16)
-            out[first:last, lanes] = jnp.dot(probs, qkv[:last, width + dim :], preferred_element_type=F32).astype(BF16)
-
-
-def attend_backward(qkv, grad_att, grad_q, grad_kv, scores_s, grad_p_s, probs_s, grad_s_s, q_s, att_s, heads, dim):
+    for first in range(0, rows, dim):
+        last = first + dim
+        stack_heads(qkv, q_s, first, heads, dim)
+        scores_s[:last, :] = lax.dot_general(qkv[:last, width : width + dim], q_s[...], ACROSS, preferred_element_type=F32)
+
+        @pl.loop(0, heads, unroll=2)
+        def _(h):
+            lanes = pl.ds(pl.multiple_of(h * dim, dim), dim)
+            scores = scaled_scores(scores_s, lanes, first, dim)
+            top = jnp.max(scores, axis=0, keepdims=True)
+            weights = jnp.exp(scores - top)
+            share = 1.0 / jnp.sum(weights, axis=0, keepdims=True)
+            probs_s[:last, lanes] = (weights * share).astype(BF16)
+            stats[h, 0:1, first:last] = top
+            stats[h, 1:2, first:last] = share
+
+        turned = lax.dot_general(qkv[:last, width + dim :], probs_s[:last, :], DOWN, preferred_element_type=F32)
+        for h in range(heads):
+            out[first:last, h * dim : (h + 1) * dim] = turned[:, h * dim : (h + 1) * dim].T.astype(BF16)
+
+
+def attend_backward(qkv, grad_att, grad_q, grad_kv, stats, scores_s, grad_p_s, probs_s, grad_s_s, q_s, att_s, heads, dim):
     rows = qkv.shape[0]
     width = heads * dim
-    scale = dim**-0.5
-    across = (((1,), (1,)), ((), ()))
-    over_rows = (((0,), (0,)), ((), ()))
-    chunk = dim // 2
     grad_kv[...] = jnp.zeros_like(grad_kv)
     for first in range(0, rows, dim):
         last = first + dim
+        stack_heads(qkv, q_s, first, heads, dim)
+        stack_heads(grad_att, att_s, first, heads, dim)
+        scores_s[:last, :] = lax.dot_general(qkv[:last, width : width + dim], q_s[...], ACROSS, preferred_element_type=F32)
+        grad_p_s[:last, :] = lax.dot_general(qkv[:last, width + dim :], att_s[...], ACROSS, preferred_element_type=F32)
+
+        @pl.loop(0, heads, unroll=2)
+        def _(h):
+            lanes = pl.ds(pl.multiple_of(h * dim, dim), dim)
+            scores = scaled_scores(scores_s, lanes, first, dim)
+            probs = jnp.exp(scores - stats[h, 0:1, first:last]) * stats[h, 1:2, first:last]
+            grad_p = grad_p_s[:last, lanes].astype(BF16).astype(F32)
+            row_dot = jnp.sum(probs * grad_p, axis=0, keepdims=True)
+            grad_s_s[:last, lanes] = (probs * (grad_p - row_dot) * dim**-0.5).astype(BF16)
+            probs_s[:last, lanes] = probs.astype(BF16)
+
+        turned = lax.dot_general(qkv[:last, width : width + dim], grad_s_s[:last, :], DOWN, preferred_element_type=F32)
         for h in range(heads):
-            q_s[h * dim : (h + 1) * dim, :] = qkv[first:last, h * dim : (h + 1) * dim]
-            att_s[h * dim : (h + 1) * dim, :] = grad_att[first:last, h * dim : (h + 1) * dim]
-        keys = qkv[:last, width : width + dim]
-        scores_s[:, :last] = lax.dot_general(q_s[...], keys, across, preferred_element_type=F32)
-        grad_p_s[:, :last] = lax.dot_general(att_s[...], qkv[:last, width + dim :], across, preferred_element_type=F32)
-
-        @pl.loop(0, width, step=chunk)
-        def _(r):
-            at = pl.ds(pl.multiple_of(r, chunk), chunk)
-            row = first + lax.rem(r, dim)
-            probs = causal_softmax(scores_s[at, :last] * scale, row)
-            grad_p = grad_p_s[at, :last].astype(BF16).astype(F32)
-            row_dot = jnp.sum(probs * grad_p, axis=-1, keepdims=True)
-            grad_s_s[at, :last] = (probs * (grad_p - row_dot) * scale).astype(BF16)
-            probs_s[at, :last] = probs.astype(BF16)
-
-        stacked = jnp.dot(grad_s_s[:, :last], keys, preferred_element_type=F32).astype(BF16)
-        for h in range(heads):
-            grad_q[first:last, h * dim : (h + 1) * dim] = stacked[h * dim : (h + 1) * dim, :]
-        grad_kv[:last, :dim] += lax.dot_general(grad_s_s[:, :last], q_s[...], over_rows, preferred_element_type=F32)
-        grad_kv[:last, dim:] += lax.dot_general(probs_s[:, :last], att_s[...], over_rows, preferred_element_type=F32)
-
-
-def gather_kernel(heads, dim, x_hbm, dy_hbm, gamma, beta, wq_hbm, wkv_hbm, bias, wo_hbm,
-                  h_full, dy_full, qkv_out, att_out, dq_out, dkv_out, dbo,
-                  own, x_buf, w_buf, wo_buf, h_buf, qkv_buf, att_buf, dq_buf, dkv_buf, total, scores_s, grad_p_s, probs_s, grad_s_s, q_s, att_s,
+            grad_q[first:last, h * dim : (h + 1) * dim] = turned[:, h * dim : (h + 1) * dim].T.astype(BF16)
+        grad_kv[:last, :dim] += jnp.dot(grad_s_s[:last, :], q_s[...], preferred_element_type=F32)
+        grad_kv[:last, dim:] += jnp.dot(probs_s[:last, :], att_s[...], preferred_element_type=F32)
+
+
+def gather_kernel(heads, dim, x_hbm, dy_hbm, gamma, beta, wq_hbm, wkv_hbm, b_q, b_kv, wo_hbm,
+                  h_full, dy_full, qkv_out, att_out, dq_out, dkv_out, dkv_twin, dbo, ln_stats,
+                  own, x_buf, w_buf, wo_buf, h_buf, qkv_buf, att_buf, dq_buf, dkv_buf, total, stats, scores_s, grad_p_s, probs_s, grad_s_s, q_s, att_s,
                   send, recv, x_sem, dy_sem, keep_sem, w_sem, h_sem, out_sem, back_sem):
     batch, rows, width = x_hbm.shape
     half = rows // 2
     units = 2 * batch
     ring = h_full.shape[1] // rows
-    qkv_width = qkv_buf.shape[1]
     me = lax.axis_index("tp")
     partner = me + 1 - 2 * lax.rem(me, 2)
     right, left, far = lax.rem(me + 2, ring), lax.rem(me + ring - 2, ring), lax.rem(me + ring // 2, ring)
@@ -138,8 +144,13 @@
         @pl.loop(0, rows, step=16)
         def _(r):
             at = pl.ds(pl.multiple_of(r, 16), 16)
-            x_hat, _ = norm_stats(x_buf[slot, at, :].astype(F32))
-            own[b, at, :] = (x_hat * gamma[...] + beta[...]).astype(BF16)
+            x_wide = x_buf[slot, at, :].astype(F32)
+            mean = jnp.mean(x_wide, axis=-1, keepdims=True)
+            centred = x_wide - mean
+            inv_std = lax.rsqrt(jnp.mean(centred * centred, axis=-1, keepdims=True) + LN_EPS)
+            own[b, at, :] = (centred * inv_std * gamma[...] + beta[...]).astype(BF16)
+            ln_stats[0, b, at, :] = jnp.broadcast_to(mean, (16, 128))
+            ln_stats[1, b, at, :] = jnp.broadcast_to(inv_std, (16, 128))
 
         @pl.when(b + 2 < batch)
         def _():
@@ -181,10 +192,13 @@
         load.start()
         load.wait()
 
-        @pl.loop(0, qkv_width, step=256)
+        @pl.loop(0, heads * dim, step=256)
         def _(n):
             at = pl.ds(pl.multiple_of(n, 256), 256)
-            qkv_buf[:, at] = (jnp.dot(h_buf[...], w_buf[:, at], preferred_element_type=F32) + bias[:, at]).astype(BF16)
+            qkv_buf[:, at] = (jnp.dot(h_buf[...], w_buf[:, at], preferred_element_type=F32) + b_q[:, at]).astype(BF16)
+
+        at = pl.ds(heads * dim, 2 * dim)
+        qkv_buf[:, at] = (jnp.dot(h_buf[...], w_buf[:, at], preferred_element_type=F32) + b_kv[...]).astype(BF16)
 
     def results(b):
         return (pltpu.make_async_copy(qkv_buf, qkv_out.at[b], out_sem.at[0]),
@@ -192,7 +206,8 @@
 
     def back_results(b):
         return (pltpu.make_async_copy(dq_buf, dq_out.at[b], back_sem.at[0]),
-                pltpu.make_async_copy(dkv_buf, dkv_out.at[b], back_sem.at[1]))
+                pltpu.make_async_copy(dkv_buf, dkv_out.at[b], back_sem.at[1]),
+                pltpu.make_async_copy(dkv_buf, dkv_twin.at[b], back_sem.at[2]))
 
     def differentiate(b):
         load = pltpu.make_async_copy(dy_full.at[b], h_buf, h_sem.at[0])
@@ -212,7 +227,7 @@
             dbo[:, at] += jnp.sum(h_buf[:, at].astype(F32).reshape(-1, 8, 512), axis=0)
 
         again.wait()
-        attend_backward(qkv_buf, att_buf, dq_buf, total, scores_s, grad_p_s, probs_s, grad_s_s, q_s, att_s, heads, dim)
+        attend_backward(qkv_buf, att_buf, dq_buf, total, stats.at[b], scores_s, grad_p_s, probs_s, grad_s_s, q_s, att_s, heads, dim)
         dkv_buf[...] = total[...].astype(BF16)
 
     @pl.loop(0, units + 2)
@@ -256,7 +271,7 @@
                     copy.wait()
 
             project(b)
-            attend(qkv_buf, att_buf, heads, dim)
+            attend(qkv_buf, att_buf, stats.at[b], scores_s, probs_s, q_s, heads, dim)
             for copy in results(b):
                 copy.start()
 
@@ -290,7 +305,7 @@
         unit(u, 0, units, act)
 
 
-def gather_and_attend(x_loc, dy_loc, gamma, beta, w_q, w_kv, bias, w_o, ring, dim):
+def gather_and_attend(x_loc, dy_loc, gamma, beta, w_q, w_kv, b_q, b_kv, w_o, ring, dim):
     batch, rows, width = x_loc.shape
     q_width = w_q.shape[1]
     qkv_width = q_width + w_kv.shape[1]
@@ -303,22 +318,24 @@
     return pl.pallas_call(
         functools.partial(gather_kernel, q_width // dim, dim),
         name="gather_and_attend",
-        out_shape=(whole(width), whole(width), whole(qkv_width), whole(q_width), whole(q_width), whole(2 * dim), jax.ShapeDtypeStruct((8, width), F32)),
-        in_specs=[hbm, hbm, vmem, vmem, hbm, hbm, vmem, hbm],
-        out_specs=(hbm, hbm, hbm, hbm, hbm, hbm, vmem),
+        out_shape=(whole(width), whole(width), whole(qkv_width), whole(q_width), whole(q_width), whole(2 * dim), whole(2 * dim), jax.ShapeDtypeStruct((8, width), F32),
+                   jax.ShapeDtypeStruct((2, batch, rows, 128), F32)),
+        in_specs=[hbm, hbm, vmem, vmem, hbm, hbm, vmem, vmem, hbm],
+        out_specs=(hbm, hbm, hbm, hbm, hbm, hbm, hbm, vmem, vmem),
         scratch_shapes=[
             pltpu.VMEM((units, rows, width), BF16), pltpu.VMEM((2, rows, width), BF16), pltpu.VMEM((width, qkv_width), BF16),
             pltpu.VMEM((q_width, width), BF16), pltpu.VMEM((seq, width), BF16), pltpu.VMEM((seq, qkv_width), BF16), pltpu.VMEM((seq, q_width), BF16),
             pltpu.VMEM((seq, q_width), BF16), pltpu.VMEM((seq, 2 * dim), BF16), pltpu.VMEM((seq, 2 * dim), F32),
-            pltpu.VMEM((q_width, seq), F32), pltpu.VMEM((q_width, seq), F32), pltpu.VMEM((q_width, seq), BF16), pltpu.VMEM((q_width, seq), BF16),
+            pltpu.VMEM((batch, q_width // dim, 8, seq), F32),
+            pltpu.VMEM((seq, q_width), F32), pltpu.VMEM((seq, q_width), F32), pltpu.VMEM((seq, q_width), BF16), pltpu.VMEM((seq, q_width), BF16),
             pltpu.VMEM((q_width, dim), BF16), pltpu.VMEM((q_width, dim), BF16),
-            dma((8, units)), dma((8, units)), dma((2,)), dma((batch,)), dma((units,)), dma((3,)), dma((2,)), dma((2,)), dma((2,))],
+            dma((8, units)), dma((8, units)), dma((2,)), dma((batch,)), dma((units,)), dma((3,)), dma((2,)), dma((2,)), dma((3,))],
         compiler_params=pltpu.CompilerParams(collective_id=0, has_side_effects=True, vmem_limit_bytes=VMEM_LIMIT),
         cost_estimate=pl.CostEstimate(flops=4 * batch * seq * width * qkv_width, bytes_accessed=6 * batch * seq * width, transcendentals=0),
-    )(x_loc, dy_loc, gamma, beta, w_q, w_kv, bias, w_o)
-
-
-def scatter_kernel(att_hbm, dq_hbm, wo_hbm, wq_hbm, x_hbm, b_o, y_out, dh_out,
+    )(x_loc, dy_loc, gamma, beta, w_q, w_kv, b_q, b_kv, w_o)
+
+
+def scatter_kernel(att_hbm, dq_hbm, dkv_hbm, wo_hbm, wq_hbm, wkv_hbm, x_hbm, b_o, y_out, dh_early, dh_late,
                    att_buf, dq_buf, wo_buf, wq_buf, stage, dh_buf, theirs, far_sum, near_sum, own_sum, far_in, near_in, x_buf, y_buf,
                    pair_send, pair_recv, far_send, far_recv, near_send, near_recv, free, load_sem, w_sem, dh_sem):
     batch, rows, width = x_hbm.shape
@@ -339,11 +356,15 @@
         return pltpu.make_async_copy(src, dst, load_sem.at[n])
 
     load_att = lambda b: load(att_hbm.at[b], att_buf, 0)
-    load_dq = lambda b: load(dq_hbm.at[b], dq_buf, 1)
+    q_width = dq_hbm.shape[2]
+    q_cols, kv_cols = pl.ds(0, q_width), pl.ds(q_width, dkv_hbm.shape[2])
     load_x = lambda b: load(x_hbm.at[b], x_buf, 2)
     store_y = lambda b: load(y_buf, y_out.at[b], 3)
     load_wo = pltpu.make_async_copy(wo_hbm, wo_buf, w_sem.at[0])
-    load_wq = pltpu.make_async_copy(wq_hbm, wq_buf, w_sem.at[1])
+    load_back = (pltpu.make_async_copy(wq_hbm, wq_buf.at[:, q_cols], w_sem.at[1]), pltpu.make_async_copy(wkv_hbm, wq_buf.at[:, kv_cols], w_sem.at[2]))
+
+    def load_grads(b):
+        return load(dq_hbm.at[b], dq_buf.at[:, q_cols], 1), load(dkv_hbm.at[b], dq_buf.at[:, kv_cols], 4)
 
     def remote(src, dst, sems, to):
         return pltpu.make_async_remote_copy(
@@ -462,36 +483,37 @@
         def _():
             load_x(u + 1).start()
 
-    def store_dh(b, n):
+    def store_dh(dh_out, b, n):
         at = pl.ds(pl.multiple_of(n, tile), tile)
         slot = lax.rem(lax.div(n, tile), 2)
         return pltpu.make_async_copy(dh_buf.at[slot], dh_out.at[b, :, at], dh_sem.at[slot])
 
-    def grad_part(b):
-        load_dq(b).wait()
+    def grad_part(dh_out, b, place):
+        for copy in load_grads(b):
+            copy.wait()
 
         @pl.loop(0, width, step=tile)
         def _(n):
             @pl.when(n >= 2 * tile)
             def _():
-                store_dh(b, n - 2 * tile).wait()
+                store_dh(dh_out, place, n - 2 * tile).wait()
 
             at = pl.ds(pl.multiple_of(n, tile), tile)
-            dh_buf[lax.rem(lax.div(n, tile), 2)] = lax.dot_general(
-                dq_buf[...], wq_buf[at, :], (((1,), (1,)), ((), ())), preferred_element_type=F32).astype(BF16)
-            store_dh(b, n).start()
+            dh_buf[lax.rem(lax.div(n, tile), 2)] = lax.dot_general(dq_buf[...], wq_buf[at, :], ACROSS, preferred_element_type=F32).astype(BF16)
+            store_dh(dh_out, place, n).start()
 
         @pl.when(b + 1 < batch)
         def _():
-            load_dq(b + 1).start()
+            for copy in load_grads(b + 1):
+                copy.start()
 
         for n in (width - 2 * tile, width - tile):
-            store_dh(b, n).wait()
+            store_dh(dh_out, place, n).wait()
 
     load_att(0).start()
     load_wo.start()
-    load_wq.start()
-    load_dq(0).start()
+    for copy in load_back + load_grads(0):
+        copy.start()
     load_x(0).start()
     load_wo.wait()
 
@@ -515,11 +537,16 @@
 
         @pl.when(t == 2)
         def _():
-            load_wq.wait()
-
-        @pl.when(jnp.logical_and(t >= 2, t < batch + 2))
-        def _():
-            grad_part(t - 2)
+            for copy in load_back:
+                copy.wait()
+
+        @pl.when(jnp.logical_and(t >= 2, t < batch // 2 + 2))
+        def _():
+            grad_part(dh_early, t - 2, t - 2)
+
+        @pl.when(jnp.logical_and(t >= batch // 2 + 2, t < batch + 2))
+        def _():
+            grad_part(dh_late, t - 2, t - 2 - batch // 2)
 
     for r in range(chips):
         pair(r).wait_send()
@@ -531,66 +558,81 @@
     store_y(batch - 1).wait()
 
 
-def project_and_scatter(merged, grad_q, w_o, w_q, x_loc, b_o, ring):
+def project_and_scatter(merged, grad_q, grad_kv, w_o, w_q, w_kv, x_loc, b_o, ring):
     batch, rows, width = x_loc.shape
     seq, q_width = merged.shape[1:]
+    qkv_width = q_width + w_kv.shape[1]
+    part = jax.ShapeDtypeStruct((batch // 2, seq, width), BF16)
     hbm = pl.BlockSpec(memory_space=pl.ANY)
     vmem = pl.BlockSpec(memory_space=pltpu.VMEM)
     dma = pltpu.SemaphoreType.DMA
     return pl.pallas_call(
         scatter_kernel,
         name="project_and_scatter",
-        out_shape=(jax.ShapeDtypeStruct(x_loc.shape, BF16), jax.ShapeDtypeStruct((batch, seq, width), BF16)),
-        in_specs=[hbm, hbm, hbm, hbm, hbm, vmem],
-        out_specs=(hbm, hbm),
+        out_shape=(jax.ShapeDtypeStruct(x_loc.shape, BF16), part, part),
+        in_specs=[hbm, hbm, hbm, hbm, hbm, hbm, hbm, vmem],
+        out_specs=(hbm, hbm, hbm),
         scratch_shapes=[
-            pltpu.VMEM((seq, q_width), BF16), pltpu.VMEM((seq, q_width), BF16), pltpu.VMEM((q_width, width), BF16), pltpu.VMEM((width, q_width), BF16),
+            pltpu.VMEM((seq, q_width), BF16), pltpu.VMEM((seq, qkv_width), BF16), pltpu.VMEM((q_width, width), BF16), pltpu.VMEM((width, qkv_width), BF16),
             pltpu.VMEM((seq, width), BF16), pltpu.VMEM((2, seq, 512), BF16), pltpu.VMEM((ring // 2, rows, width), BF16),
             pltpu.VMEM((2, rows, width), BF16), pltpu.VMEM((3, 2, rows, width), BF16), pltpu.VMEM((3, rows, width), F32),
             pltpu.VMEM((3, rows, width), BF16), pltpu.VMEM((3, 2, rows, width), BF16), pltpu.VMEM((rows, width), BF16), pltpu.VMEM((rows, width), BF16),
             dma((ring // 2,)), dma((ring // 2,)), dma((2, 2)), dma((3, 2)), dma((3, 2)), dma((3, 2)), pltpu.SemaphoreType.REGULAR,
-            dma((4,)), dma((2,)), dma((2,))],
+            dma((5,)), dma((3,)), dma((2,))],
         compiler_params=pltpu.CompilerParams(collective_id=1, has_side_effects=True, vmem_limit_bytes=VMEM_LIMIT),
         cost_estimate=pl.CostEstimate(flops=4 * batch * seq * width * q_width, bytes_accessed=4 * batch * seq * width, transcendentals=0),
-    )(merged, grad_q, w_o, w_q, x_loc, b_o)
-
-
-def norm_backward_kernel(dh, dkv, w_kv, x, dy, gamma, dx, sums):
-    rows = x.shape[1]
+    )(merged, grad_q, grad_kv, w_o, w_q, w_kv, x_loc, b_o)
+
+
+def norm_backward_kernel(dh, x, dy, ln_stats, gamma, *refs):
+    dx, sums = refs[-2:]
+    rows, width = x.shape[1:]
+    tile = 512
 
     @pl.when(pl.program_id(0) == 0)
     def _():
         sums[...] = jnp.zeros_like(sums)
 
-    @pl.loop(0, rows, step=16)
-    def _(r):
-        at = pl.ds(pl.multiple_of(r, 16), 16)
-        from_kv = lax.dot_general(dkv[0, at, :], w_kv[...], (((1,), (1,)), ((), ())), preferred_element_type=F32)
-        grad_h = dh[0, at, :].astype(F32) + from_kv
-        x_hat, inv_std = norm_stats(x[0, at, :].astype(F32))
-        grad_hat = grad_h * gamma[...]
-        mean = jnp.mean(grad_hat, axis=-1, keepdims=True)
-        along = jnp.mean(grad_hat * x_hat, axis=-1, keepdims=True)
-        dx[0, at, :] = (dy[0, at, :].astype(F32) + inv_std * (grad_hat - mean - x_hat * along)).astype(BF16)
-        by_sublane = lambda v: jnp.sum(v.reshape(-1, 8, v.shape[-1]), axis=0)
-        sums[0] += by_sublane(grad_h * x_hat)
-        sums[1] += by_sublane(grad_h)
-
-
-def norm_backward(grad_h, grad_kv, w_kv, x_loc, dy_loc, gamma):
-    batch, rows, width = x_loc.shape
-    one = pl.BlockSpec((1, rows, width), lambda b: (b, 0, 0))
+    mean, inv_std = ln_stats[0, 0, :, :1], ln_stats[1, 0, :, :1]
+    by_lane = lambda v: sum(v[:, n : n + 128] for n in range(0, tile, 128))
+    by_sublane = lambda v: jnp.sum(v.reshape(-1, 8, tile), axis=0)
+    plain = along = jnp.zeros((rows, 128), F32)
+    for n in range(0, width, tile):
+        at = slice(n, n + tile)
+        grad_h = dh[0, :, at].astype(F32)
+        x_hat = (x[0, :, at].astype(F32) - mean) * inv_std
+        both = grad_h * x_hat
+        plain = plain + by_lane(grad_h * gamma[:, at])
+        along = along + by_lane(both * gamma[:, at])
+        sums[0, :, at] += by_sublane(both)
+        sums[1, :, at] += by_sublane(grad_h)
+    plain = jnp.sum(plain, axis=-1, keepdims=True) / width
+    along = jnp.sum(along, axis=-1, keepdims=True) / width
+    for n in range(0, width, tile):
+        at = slice(n, n + tile)
+        x_hat = (x[0, :, at].astype(F32) - mean) * inv_std
+        grad_in = inv_std * (dh[0, :, at].astype(F32) * gamma[:, at] - plain - x_hat * along)
+        dx[0, :, at] = (dy[0, :, at].astype(F32) + grad_in).astype(BF16)
+
+
+def norm_backward(grad_h, x_loc, dy_loc, ln_stats, gamma, first, started):
+    rows, width = x_loc.shape[1:]
+    count = grad_h.shape[0]
+    block = lambda skip: pl.BlockSpec((1, rows, width), lambda b: (b + skip, 0, 0))
     still = lambda shape: pl.BlockSpec(shape, lambda b: (0,) * len(shape))
+    extra = [] if started is None else [started]
     return pl.pallas_call(
         norm_backward_kernel,
         name="norm_backward",
-        grid=(batch,),
+        grid=(count,),
         out_shape=(jax.ShapeDtypeStruct(x_loc.shape, BF16), jax.ShapeDtypeStruct((2, 8, width), F32)),
-        in_specs=[one, pl.BlockSpec((1, rows, grad_kv.shape[-1]), lambda b: (b, 0, 0)), still(w_kv.shape), one, one, still(gamma.shape)],
-        out_specs=(one, still((2, 8, width))),
-        compiler_params=pltpu.CompilerParams(vmem_limit_bytes=VMEM_LIMIT // 2),
-        cost_estimate=pl.CostEstimate(flops=2 * batch * rows * width * 256, bytes_accessed=8 * batch * rows * width, transcendentals=0),
-    )(grad_h, grad_kv, w_kv, x_loc, dy_loc, gamma)
+        in_specs=[block(0), block(first), block(first), pl.BlockSpec((2, 1, rows, 128), lambda b: (0, b + first, 0, 0)), still(gamma.shape)]
+        + [pl.BlockSpec(memory_space=pl.ANY)] * len(extra),
+        out_specs=(block(first), still((2, 8, width))),
+        input_output_aliases={5: 0} if extra else {},
+        compiler_params=pltpu.CompilerParams(vmem_limit_bytes=VMEM_LIMIT),
+        cost_estimate=pl.CostEstimate(flops=60 * count * rows * width, bytes_accessed=8 * count * rows * width, transcendentals=0),
+    )(grad_h, x_loc, dy_loc, ln_stats, gamma, *extra)
 
 
 def settle(values):
@@ -648,15 +690,16 @@
 
     def device_block(x_loc, ln_gamma, ln_beta, w_q, b_q, w_kv, b_kv, w_o, b_o, dy_loc):
         head_dim = w_kv.shape[1] // 2
-        own_rows, width = x_loc.shape[1:]
-        bias = jnp.concatenate([b_q, b_kv])[None, :]
-        normed_full, dy_full, _, merged, grad_q, grad_kv, bo_rows = gather_and_attend(
-            x_loc, dy_loc, ln_gamma[None, :], ln_beta[None, :], w_q, w_kv, bias, w_o, ring, head_dim)
-        grad_kv = lax.psum(grad_kv, "tp")
-        y_loc, grad_h_part = project_and_scatter(merged, grad_q, w_o, w_q, x_loc, b_o[None, :], ring)
-        grad_h = lax.psum_scatter(grad_h_part, "tp", scatter_dimension=1, tiled=True)
-
-        grad_h_part, grad_q, merged, y_loc, bo_rows = lax.optimization_barrier((grad_h_part, grad_q, merged, y_loc, bo_rows))
+        batch, _, width = x_loc.shape
+        normed_full, dy_full, _, merged, grad_q, kv_part, kv_twin, bo_rows, ln_stats = gather_and_attend(
+            x_loc, dy_loc, ln_gamma[None, :], ln_beta[None, :], w_q, w_kv, b_q[None, :], b_kv[None, :], w_o, ring, head_dim)
+        grad_kv = lax.psum(kv_twin, "tp")
+        y_loc, dh_early, dh_late = project_and_scatter(merged, grad_q, kv_part, w_o, w_q, w_kv, x_loc, b_o[None, :], ring)
+        scatter = lambda part: lax.psum_scatter(part, "tp", scatter_dimension=1, tiled=True)
+        dh_early_loc = scatter(dh_early)
+        dh_late_loc = scatter(dh_late)
+
+        grad_q, merged, y_loc, bo_rows = lax.optimization_barrier((grad_q, merged, y_loc, bo_rows))
         y_loc = settle(y_loc)
         grad_bo = jnp.sum(bo_rows, axis=0)
         grad_wo = jnp.einsum("bse,bsd->ed", merged, dy_full, preferred_element_type=jnp.float32)
@@ -664,9 +707,10 @@
         grad_bq = jnp.sum(grad_q, axis=(0, 1), dtype=jnp.float32)
         grad_wkv = jnp.einsum("bsd,bsc->dc", normed_full, grad_kv, preferred_element_type=jnp.float32)
         grad_bkv = jnp.sum(grad_kv, axis=(0, 1), dtype=jnp.float32)
-        kv_loc = lax.dynamic_slice_in_dim(grad_kv, lax.axis_index("tp") * own_rows, own_rows, axis=1)
-        grad_x, parts = norm_backward(grad_h, kv_loc, w_kv, x_loc, dy_loc, ln_gamma[None, :])
-        sums = sum_over_ring(jnp.sum(parts, axis=1).reshape(-1, 128), ring).reshape(2, width)
+        gamma = ln_gamma[None, :]
+        started, parts_early = norm_backward(dh_early_loc, x_loc, dy_loc, ln_stats, gamma, 0, None)
+        grad_x, parts_late = norm_backward(dh_late_loc, x_loc, dy_loc, ln_stats, gamma, batch // 2, started)
+        sums = sum_over_ring(jnp.sum(parts_early + parts_late, axis=1).reshape(-1, 128), ring).reshape(2, width)
         return (y_loc, grad_x, sums[0], sums[1], grad_wq, grad_bq, grad_wkv, grad_bkv, grad_wo, grad_bo)
 
     return jax.shard_map(

time: 1060 us -> 1000 us (0.943)
  Pallas kernels: 795 us -> 735 us
    pallas_call x1, Pallas kernels: 499 us -> 459 us  [gather_and_attend(): pl.pallas_call(functools.partial(gather_kernel, q_width // dim, dim), nam...]
    pallas_call x1 -> x2, Pallas kernels: 37.3 us -> 17.5 us  [norm_backward(): pl.pallas_call(norm_backward_kernel, name='norm_backward', grid=(count,),...]
    reduce_scatter x1 -> x2, waiting for transfers between devices: 106 us -> 110 us  [device_block(): lax.psum_scatter(part, 'tp', scatter_dimension=1, tiled=True)]
  transfers between devices with their start and end apart: 2 -> 3, of which waited for: 1 -> 1; matrix products, arithmetic and copies ran while one was open for 12% -> 13% of each run, Pallas kernels for 23% -> 26%
where the time goes in v4:
time: 1000 us; the launch traced here: 995 us
  Pallas kernels  735 us (74%)
  matrix products  122 us (12%)
  waiting for transfers between devices  111 us (11%)
  between operations  14.1 us (1%)
    pallas_call x1, Pallas kernels, gather_and_attend(): pl.pallas_call(functools.partial(gather_kernel, q_width // dim, dim), nam...  459 us
    pallas_call x1, Pallas kernels, project_and_scatter(): pl.pallas_call(scatter_kernel, name='project_and_scatter', out_shape=(jax...  240 us
    reduce_scatter x2, waiting for transfers between devices, device_block(): lax.psum_scatter(part, 'tp', scatter_dimension=1, tiled=True)  110 us
    dot_general x1, matrix products, device_block(): jnp.einsum('bsd,bse->de', normed_full, grad_q, preferred_element_type=jnp...  48.5 us
    dot_general x1, matrix products, device_block(): jnp.einsum('bse,bsd->ed', merged, dy_full, preferred_element_type=jnp.flo...  47.8 us
    dot_general x1, matrix products, device_block(): jnp.einsum('bsd,bsc->dc', normed_full, grad_kv, preferred_element_type=jn...  25.7 us
  transfers between devices with their start and end apart: 3, of which 1 were waited for; matrix products, arithmetic and copies ran while one was open for 13% of the time, Pallas kernels for 26%

profile of v4, /device:TPU:112, one launch (start us, length us, event | category | flops | bytes accessed | tf_op | source)
XLA Modules:
  0.0 994.7 jit_solution(11408898239987253532)
XLA Ops:
  7.2 0.1 all-reduce.2.cloned.1.call-start
  7.3 1.3 broadcast_in_dim.18.b_q
  8.5 459.3 %gather_and_attend.1 = (bf16[8,512,6144]{2,1,0:T(8,128)(2,1)}, bf16[8,512,6144]{2,1,0:T(8,128)(2,1)}, bf16[8,512,1024]{2,1,0:T(8,128)(2,1)}, bf16[8,512,768]{2,1...) custom-call(bf16[8,64,6144]{2,1,0:T(8,128)(2,1)} %x.3, ...), custom_call_target="tpu_custom_call" | custom-call | flops 103079215104 | bytes 150994944 | tf_op jit(solution)/shard_map/gather_and_attend/pallas_call | solution.py:318
  467.8 0.1 all-reduce.2.cloned.1.call-update
  467.9 0.1 reduce-scatter.5.cloned.1.call-start
  468.0 240.3 %project_and_scatter.1 = (bf16[8,64,6144]{2,1,0:T(8,128)(2,1)}, bf16[4,512,6144]{2,1,0:T(8,128)(2,1)}, bf16[4,512,6144]{2,1,0:T(8,128)(2,1)}) custom-call(bf16[8,512,768]{2,1,0:T(8,128)(2,1)} %get-tuple-element.45.att_hbm, bf16[8,512,768]{2,1,0:T(8,128)(2,1)} %get-tuple-element.43.dq_hbm, bf16[8,512,256]{2,1,0:T(8,128)(2,1)} %get-tuple-element.31.dkv_hbm, ...), custom_call_target="tpu_custom_call" | custom-call | flops 77309411328 | bytes 100663296 | tf_op jit(solution)/shard_map/project_and_scatter/pallas_call | solution.py:569
  708.3 0.1 reduce-scatter.5.cloned.1.call-update
  708.4 0.1 reduce-scatter.3.cloned.1.call-start
  708.4 0.0 copy-start.1
  708.4 0.7 reduce-scatter.3.cloned.1.call-update
  709.2 0.2 copy-done.1
  709.4 0.7 reduce_sum.39
  710.0 7.9 settle.1
  717.9 0.0 slice-start
  717.9 4.4 convert_reduce_fusion
  722.4 0.0 slice-start.1
  722.4 47.8 %convolution_bitcast_fusion.1 = f32[768,6144]{1,0:T(8,128)} fusion(bf16[8,512,768]{2,1,0:T(8,128)(2,1)} %get-tuple-element.45.att_hbm, bf16[8,512,6144]{2,1,0:T(8,128)(2,1)} %get-tuple-element.46), kind=kOutput, calls=%fused_computation.2 | convolution fusion | flops 38654705664 | bytes 75497472 | tf_op jit(solution)/shard_map/bse,bsd->ed/dot_general | solution.py:705
  770.2 0.0 slice-done
  770.2 0.0 slice-done.1
  770.2 48.5 %convolution_bitcast_fusion = f32[6144,768]{1,0:T(8,128)} fusion(bf16[8,512,6144]{2,1,0:T(8,128)(2,1)} %get-tuple-element.42, bf16[8,512,768]{2,1,0:T(8,128)(2,1)S(1)} %bitcast.21), kind=kOutput, calls=%fused_computation.1 | convolution fusion | flops 38654705664 | bytes 75497472 | tf_op jit(solution)/shard_map/bsd,bse->de/dot_general | solution.py:706
  818.7 0.0 all-reduce.2.cloned.1.call-done
  818.7 2.7 convert_reduce_fusion.1
  821.4 25.7 %convolution_bitcast_fusion.2 = f32[6144,256]{1,0:T(8,128)} fusion(bf16[8,512,6144]{2,1,0:T(8,128)(2,1)} %get-tuple-element.42, bf16[8,512,256]{2,1,0:T(8,128)(2,1)} %all-reduce.2.cloned.1.call-done), kind=kOutput, calls=%fused_computation.3 | convolution fusion | flops 12884901888 | bytes 58720256 | tf_op jit(solution)/shard_map/bsd,bsc->dc/dot_general | solution.py:708
  847.1 0.0 reduce-scatter.5.cloned.1.call-done.dh
  847.1 8.8 norm_backward.2
  855.9 110.4 %reduce-scatter.3.cloned.1.call-done.dh = bf16[4,64,6144]{2,1,0:T(8,128)(2,1)} async-done(((bf16[4,512,6144]{2,1,0:T(8,128)(2,1)}), bf16[4,64,6144]{2,1,0:T(8,128)(2,1)}) %reduce-scatter.3.cloned.1.call-update) | async-done | bytes 3145744 | tf_op jit(solution)/shard_map/reduce_scatter | solution.py:698
  966.2 8.7 norm_backward.3
  975.0 0.0 copy-done
  975.0 1.1 add_reduce_fusion
  976.1 0.7 reshape.28.parts
  976.8 9.8 sum_over_ring.1
  986.6 1.4 slice_bitcast_fusion
  (2 shorter events, 0.0 us)
Async XLA Ops:
  7.2 811.5 %all-reduce.2.cloned.1.call-start = ((), (), s32[]{:S(2)}) async-start(), calls=%async_computation.4 | async-start | bytes 4194304 | tf_op jit(solution)/shard_map/psum | solution.py:696
  467.9 379.2 %reduce-scatter.5.cloned.1.call-start = ((), (), s32[]{:S(2)}) async-start(), calls=%async_computation.3 | async-start | bytes 28311552 | tf_op jit(solution)/shard_map/reduce_scatter | solution.py:698
  708.4 257.9 %reduce-scatter.3.cloned.1.call-start = ((), (), s32[]{:S(2)}) async-start(), calls=%async_computation.2 | async-start | bytes 28311552 | tf_op jit(solution)/shard_map/reduce_scatter | solution.py:698
  708.4 0.9 copy-start.1
  717.9 52.3 %slice-start = ((s8[6291456]{0:T(1024)(128)(4,1)}), s8[4194304]{0:T(1024)(128)(4,1)S(1)}, s32[]{:S(2)}) async-start(s8[6291456]{0:T(1024)(128)(4,1)} %bitcast.20), calls=%async_computation.5 | async-start | bytes 8388608
  722.4 47.8 %slice-start.1 = ((s8[6291456]{0:T(1024)(128)(4,1)}), s8[2097152]{0:T(1024)(128)(4,1)S(1)}, s32[]{:S(2)}) async-start(s8[6291456]{0:T(1024)(128)(4,1)} %bitcast.20), calls=%async_computation.6 | async-start | bytes 4194304
  966.2 8.7 copy-start
Sparse Core Ops, SparseCore 0:
  468.0 71.7 all-reduce.1
  708.5 128.4 reduce-scatter.4
  839.3 126.8 reduce-scatter.2

commit v5 on v4

--- a/solution.py
+++ b/solution.py
@@ -85,13 +85,15 @@
 
 
 def gather_kernel(heads, dim, x_hbm, dy_hbm, gamma, beta, wq_hbm, wkv_hbm, b_q, b_kv, wo_hbm,
-                  h_full, dy_full, qkv_out, att_out, dq_out, dkv_out, dkv_twin, dbo, ln_stats,
-                  own, x_buf, w_buf, wo_buf, h_buf, qkv_buf, att_buf, dq_buf, dkv_buf, total, stats, scores_s, grad_p_s, probs_s, grad_s_s, q_s, att_s,
-                  send, recv, x_sem, dy_sem, keep_sem, w_sem, h_sem, out_sem, back_sem):
+                  h_full, dy_full, att_out, o_part, dq_out, dkv_out, dkv_twin, dbo, ln_stats,
+                  own, x_buf, w_buf, wo_buf, h_buf, qkv_buf, att_buf, da_buf, dq_buf, dkv_buf, o_buf, total, stats,
+                  scores_s, grad_p_s, probs_s, grad_s_s, q_s, att_s,
+                  send, recv, x_sem, dy_sem, keep_sem, w_sem, h_sem, att_sem, back_sem, o_sem):
     batch, rows, width = x_hbm.shape
     half = rows // 2
     units = 2 * batch
     ring = h_full.shape[1] // rows
+    tile = 512
     me = lax.axis_index("tp")
     partner = me + 1 - 2 * lax.rem(me, 2)
     right, left, far = lax.rem(me + 2, ring), lax.rem(me + ring - 2, ring), lax.rem(me + ring // 2, ring)
@@ -126,16 +128,22 @@
         return pltpu.make_async_copy(x_hbm.at[b], x_buf.at[lax.rem(b, 2)], x_sem.at[lax.rem(b, 2)])
 
     def load_dy(b):
-        return pltpu.make_async_copy(dy_hbm.at[b], own.at[batch + b], dy_sem.at[b])
+        return pltpu.make_async_copy(dy_hbm.at[b], own.at[2 * b + 1], dy_sem.at[b])
+
+    def turn(u, low, high, h_act, dy_act):
+        b = lax.div(u, 2)
+        inside = jnp.logical_and(u >= low, u < high)
+
+        @pl.when(jnp.logical_and(inside, lax.rem(u, 2) == 0))
+        def _():
+            h_act(b)
+
+        @pl.when(jnp.logical_and(inside, lax.rem(u, 2) == 1))
+        def _():
+            dy_act(b)
 
     def unit(u, low, high, act):
-        @pl.when(jnp.logical_and(u >= low, u < jnp.minimum(high, batch)))
-        def _():
-            act(h_full, u, u)
-
-        @pl.when(jnp.logical_and(u >= jnp.maximum(low, batch), u < high))
-        def _():
-            act(dy_full, u - batch, u)
+        turn(u, low, high, lambda b: act(h_full, b, u), lambda b: act(dy_full, b, u))
 
     def normalise(b):
         load_x(b).wait()
@@ -148,7 +156,7 @@
             mean = jnp.mean(x_wide, axis=-1, keepdims=True)
             centred = x_wide - mean
             inv_std = lax.rsqrt(jnp.mean(centred * centred, axis=-1, keepdims=True) + LN_EPS)
-            own[b, at, :] = (centred * inv_std * gamma[...] + beta[...]).astype(BF16)
+            own[2 * b, at, :] = (centred * inv_std * gamma[...] + beta[...]).astype(BF16)
             ln_stats[0, b, at, :] = jnp.broadcast_to(mean, (16, 128))
             ln_stats[1, b, at, :] = jnp.broadcast_to(inv_std, (16, 128))
 
@@ -157,13 +165,7 @@
             load_x(b + 2).start()
 
     def launch(u):
-        @pl.when(u < batch)
-        def _():
-            normalise(u)
-
-        @pl.when(jnp.logical_and(u >= batch, u < units))
-        def _():
-            load_dy(u - batch).wait()
+        turn(u, 0, units, normalise, lambda b: load_dy(b).wait())
 
         def act(full, b, u):
             for kind in (RIGHT, LEFT, PART):
@@ -173,24 +175,28 @@
         unit(u, 0, units, act)
 
     load_x(0).start()
+    load_dy(0).start()
     load_x(1).start()
     weights = (pltpu.make_async_copy(wq_hbm, w_buf.at[:, pl.ds(0, heads * dim)], w_sem.at[0]),
                pltpu.make_async_copy(wkv_hbm, w_buf.at[:, pl.ds(heads * dim, 2 * dim)], w_sem.at[1]),
                pltpu.make_async_copy(wo_hbm, wo_buf, w_sem.at[2]))
-    dbo[...] = jnp.zeros_like(dbo)
     launch(0)
     launch(1)
     for copy in weights:
         copy.start()
-    for b in range(batch):
+    for b in range(1, batch):
         load_dy(b).start()
+    dbo[...] = jnp.zeros_like(dbo)
     for copy in weights:
         copy.wait()
 
-    def project(b):
-        load = pltpu.make_async_copy(h_full.at[b], h_buf, h_sem.at[0])
+    def load_block(full, b):
+        load = pltpu.make_async_copy(full.at[b], h_buf, h_sem.at[0])
         load.start()
         load.wait()
+
+    def project(b):
+        load_block(h_full, b)
 
         @pl.loop(0, heads * dim, step=256)
         def _(n):
@@ -200,9 +206,47 @@
         at = pl.ds(heads * dim, 2 * dim)
         qkv_buf[:, at] = (jnp.dot(h_buf[...], w_buf[:, at], preferred_element_type=F32) + b_kv[...]).astype(BF16)
 
-    def results(b):
-        return (pltpu.make_async_copy(qkv_buf, qkv_out.at[b], out_sem.at[0]),
-                pltpu.make_async_copy(att_buf, att_out.at[b], out_sem.at[1]))
+    def store_att(b):
+        return pltpu.make_async_copy(att_buf, att_out.at[b], att_sem.at[0])
+
+    def store_o(b, n):
+        at = pl.ds(pl.multiple_of(n, tile), tile)
+        slot = lax.rem(lax.div(n, tile), 2)
+        return pltpu.make_async_copy(o_buf.at[slot], o_part.at[b, :, at], o_sem.at[slot])
+
+    def attend_and_project(b):
+        @pl.when(b > 0)
+        def _():
+            store_att(b - 1).wait()
+
+        attend(qkv_buf, att_buf, stats, scores_s, probs_s, q_s, heads, dim)
+        store_att(b).start()
+
+        @pl.loop(0, width, step=tile)
+        def _(n):
+            @pl.when(n >= 2 * tile)
+            def _():
+                store_o(b, n - 2 * tile).wait()
+
+            at = pl.ds(pl.multiple_of(n, tile), tile)
+            o_buf[lax.rem(lax.div(n, tile), 2)] = jnp.dot(att_buf[...], wo_buf[:, at], preferred_element_type=F32).astype(BF16)
+            store_o(b, n).start()
+
+        for n in (width - 2 * tile, width - tile):
+            store_o(b, n).wait()
+
+    def grad_attended(b):
+        load_block(dy_full, b)
+
+        @pl.loop(0, heads * dim, step=256)
+        def _(n):
+            at = pl.ds(pl.multiple_of(n, 256), 256)
+            da_buf[:, at] = lax.dot_general(h_buf[...], wo_buf[at, :], ACROSS, preferred_element_type=F32).astype(BF16)
+
+        @pl.loop(0, width, step=tile)
+        def _(n):
+            at = pl.ds(pl.multiple_of(n, tile), tile)
+            dbo[:, at] += jnp.sum(h_buf[:, at].astype(F32).reshape(-1, 8, tile), axis=0)
 
     def back_results(b):
         return (pltpu.make_async_copy(dq_buf, dq_out.at[b], back_sem.at[0]),
@@ -210,25 +254,15 @@
                 pltpu.make_async_copy(dkv_buf, dkv_twin.at[b], back_sem.at[2]))
 
     def differentiate(b):
-        load = pltpu.make_async_copy(dy_full.at[b], h_buf, h_sem.at[0])
-        again = pltpu.make_async_copy(qkv_out.at[b], qkv_buf, h_sem.at[1])
-        load.start()
-        again.start()
-        load.wait()
-
-        @pl.loop(0, heads * dim, step=256)
-        def _(n):
-            at = pl.ds(pl.multiple_of(n, 256), 256)
-            att_buf[:, at] = lax.dot_general(h_buf[...], wo_buf[at, :], (((1,), (1,)), ((), ())), preferred_element_type=F32).astype(BF16)
-
-        @pl.loop(0, width, step=512)
-        def _(n):
-            at = pl.ds(pl.multiple_of(n, 512), 512)
-            dbo[:, at] += jnp.sum(h_buf[:, at].astype(F32).reshape(-1, 8, 512), axis=0)
-
-        again.wait()
-        attend_backward(qkv_buf, att_buf, dq_buf, total, stats.at[b], scores_s, grad_p_s, probs_s, grad_s_s, q_s, att_s, heads, dim)
+        @pl.when(b > 0)
+        def _():
+            for copy in back_results(b - 1):
+                copy.wait()
+
+        attend_backward(qkv_buf, da_buf, dq_buf, total, stats, scores_s, grad_p_s, probs_s, grad_s_s, q_s, att_s, heads, dim)
         dkv_buf[...] = total[...].astype(BF16)
+        for copy in back_results(b):
+            copy.start()
 
     @pl.loop(0, units + 2)
     def _(s):
@@ -246,6 +280,7 @@
             move(PASS_R, full, b, u).start()
 
         unit(s, 0, units, share)
+        turn(s - 2, 0, units, attend_and_project, differentiate)
 
         def share_far(full, b, u):
             move(FAR_R, full, b, u).wait_recv()
@@ -259,40 +294,10 @@
                 move(kind, full, b, u).wait_recv()
             keep(full, b, u).wait()
 
-        unit(s - 2, 0, units, complete)
-
-        @pl.when(jnp.logical_and(s >= 2, s < batch + 2))
-        def _():
-            b = s - 2
-
-            @pl.when(b > 0)
-            def _():
-                for copy in results(b - 1):
-                    copy.wait()
-
-            project(b)
-            attend(qkv_buf, att_buf, stats.at[b], scores_s, probs_s, q_s, heads, dim)
-            for copy in results(b):
-                copy.start()
-
-        @pl.when(s >= batch + 2)
-        def _():
-            b = s - 2 - batch
-
-            @pl.when(b == 0)
-            def _():
-                for copy in results(batch - 1):
-                    copy.wait()
-
-            @pl.when(b > 0)
-            def _():
-                for copy in back_results(b - 1):
-                    copy.wait()
-
-            differentiate(b)
-            for copy in back_results(b):
-                copy.start()
-
+        unit(s - 1, 0, units, complete)
+        turn(s - 1, 0, units, project, grad_attended)
+
+    store_att(batch - 1).wait()
     for copy in back_results(batch - 1):
         copy.wait()
 
@@ -311,35 +316,38 @@
     qkv_width = q_width + w_kv.shape[1]
     seq = rows * ring
     units = 2 * batch
+    heads = q_width // dim
     hbm = pl.BlockSpec(memory_space=pl.ANY)
     vmem = pl.BlockSpec(memory_space=pltpu.VMEM)
     dma = pltpu.SemaphoreType.DMA
     whole = lambda w: jax.ShapeDtypeStruct((batch, seq, w), BF16)
     return pl.pallas_call(
-        functools.partial(gather_kernel, q_width // dim, dim),
+        functools.partial(gather_kernel, heads, dim),
         name="gather_and_attend",
-        out_shape=(whole(width), whole(width), whole(qkv_width), whole(q_width), whole(q_width), whole(2 * dim), whole(2 * dim), jax.ShapeDtypeStruct((8, width), F32),
-                   jax.ShapeDtypeStruct((2, batch, rows, 128), F32)),
+        out_shape=(whole(width), whole(width), whole(q_width), whole(width), whole(q_width), whole(2 * dim), whole(2 * dim),
+                   jax.ShapeDtypeStruct((8, width), F32), jax.ShapeDtypeStruct((2, batch, rows, 128), F32)),
         in_specs=[hbm, hbm, vmem, vmem, hbm, hbm, vmem, vmem, hbm],
-        out_specs=(hbm, hbm, hbm, hbm, hbm, hbm, hbm, vmem, vmem),
+        out_specs=(hbm,) * 7 + (vmem, vmem),
         scratch_shapes=[
             pltpu.VMEM((units, rows, width), BF16), pltpu.VMEM((2, rows, width), BF16), pltpu.VMEM((width, qkv_width), BF16),
             pltpu.VMEM((q_width, width), BF16), pltpu.VMEM((seq, width), BF16), pltpu.VMEM((seq, qkv_width), BF16), pltpu.VMEM((seq, q_width), BF16),
-            pltpu.VMEM((seq, q_width), BF16), pltpu.VMEM((seq, 2 * dim), BF16), pltpu.VMEM((seq, 2 * dim), F32),
-            pltpu.VMEM((batch, q_width // dim, 8, seq), F32),
+            pltpu.VMEM((seq, q_width), BF16), pltpu.VMEM((seq, q_width), BF16), pltpu.VMEM((seq, 2 * dim), BF16), pltpu.VMEM((2, seq, 512), BF16),
+            pltpu.VMEM((seq, 2 * dim), F32), pltpu.VMEM((heads, 8, seq), F32),
             pltpu.VMEM((seq, q_width), F32), pltpu.VMEM((seq, q_width), F32), pltpu.VMEM((seq, q_width), BF16), pltpu.VMEM((seq, q_width), BF16),
             pltpu.VMEM((q_width, dim), BF16), pltpu.VMEM((q_width, dim), BF16),
-            dma((8, units)), dma((8, units)), dma((2,)), dma((batch,)), dma((units,)), dma((3,)), dma((2,)), dma((2,)), dma((3,))],
+            dma((8, units)), dma((8, units)), dma((2,)), dma((batch,)), dma((units,)), dma((3,)), dma((1,)), dma((1,)), dma((3,)), dma((2,))],
         compiler_params=pltpu.CompilerParams(collective_id=0, has_side_effects=True, vmem_limit_bytes=VMEM_LIMIT),
-        cost_estimate=pl.CostEstimate(flops=4 * batch * seq * width * qkv_width, bytes_accessed=6 * batch * seq * width, transcendentals=0),
+        cost_estimate=pl.CostEstimate(flops=6 * batch * seq * width * qkv_width, bytes_accessed=6 * batch * seq * width, transcendentals=0),
     )(x_loc, dy_loc, gamma, beta, w_q, w_kv, b_q, b_kv, w_o)
 
 
-def scatter_kernel(att_hbm, dq_hbm, dkv_hbm, wo_hbm, wq_hbm, wkv_hbm, x_hbm, b_o, y_out, dh_early, dh_late,
-                   att_buf, dq_buf, wo_buf, wq_buf, stage, dh_buf, theirs, far_sum, near_sum, own_sum, far_in, near_in, x_buf, y_buf,
-                   pair_send, pair_recv, far_send, far_recv, near_send, near_recv, free, load_sem, w_sem, dh_sem):
+def scatter_kernel(o_part, dq_hbm, dkv_hbm, wq_hbm, wkv_hbm, x_hbm, b_o, y_out, dh_early, dh_late, dh_sum,
+                   dq_buf, w_buf, ours, dh_buf, theirs, far_sum, near_sum, own_sum, far_in, near_in, x_buf, y_buf,
+                   ours_sem, pair_send, pair_recv, far_send, far_recv, near_send, near_recv, free, load_sem, w_sem, dh_sem):
     batch, rows, width = x_hbm.shape
-    ring = stage.shape[0] // rows
+    early = dh_early.shape[0]
+    units = batch + early
+    ring = o_part.shape[1] // rows
     half = width // 2
     tile = 512
     me = lax.axis_index("tp")
@@ -355,16 +363,15 @@
     def load(src, dst, n):
         return pltpu.make_async_copy(src, dst, load_sem.at[n])
 
-    load_att = lambda b: load(att_hbm.at[b], att_buf, 0)
     q_width = dq_hbm.shape[2]
     q_cols, kv_cols = pl.ds(0, q_width), pl.ds(q_width, dkv_hbm.shape[2])
-    load_x = lambda b: load(x_hbm.at[b], x_buf, 2)
-    store_y = lambda b: load(y_buf, y_out.at[b], 3)
-    load_wo = pltpu.make_async_copy(wo_hbm, wo_buf, w_sem.at[0])
-    load_back = (pltpu.make_async_copy(wq_hbm, wq_buf.at[:, q_cols], w_sem.at[1]), pltpu.make_async_copy(wkv_hbm, wq_buf.at[:, kv_cols], w_sem.at[2]))
+    load_x = lambda b: load(x_hbm.at[b], x_buf, 0)
+    store_y = lambda u: load(y_buf, y_out.at[u], 1)
+    store_sum = lambda u: load(y_buf, dh_sum.at[u - batch], 1)
+    load_w = (pltpu.make_async_copy(wq_hbm, w_buf.at[:, q_cols], w_sem.at[0]), pltpu.make_async_copy(wkv_hbm, w_buf.at[:, kv_cols], w_sem.at[1]))
 
     def load_grads(b):
-        return load(dq_hbm.at[b], dq_buf.at[:, q_cols], 1), load(dkv_hbm.at[b], dq_buf.at[:, kv_cols], 4)
+        return load(dq_hbm.at[b], dq_buf.at[:, q_cols], 2), load(dkv_hbm.at[b], dq_buf.at[:, kv_cols], 3)
 
     def remote(src, dst, sems, to):
         return pltpu.make_async_remote_copy(
@@ -373,8 +380,22 @@
     def block(owner):
         return pl.ds(pl.multiple_of(owner * rows, rows), rows)
 
-    def pair(r):
-        return remote(stage.at[block(lax.rem(partner + 2 * r, ring))], theirs.at[r], (pair_send.at[r], pair_recv.at[r]), partner)
+    def sourced(u, act):
+        @pl.when(u < batch)
+        def _():
+            act(o_part.at[u])
+
+        @pl.when(u >= batch)
+        def _():
+            act(dh_early.at[u - batch])
+
+    def mine(part, u, r):
+        slot = lax.rem(u, 2)
+        return pltpu.make_async_copy(part.at[block(lax.rem(me + 2 * r, ring))], ours.at[slot, r], ours_sem.at[slot, r])
+
+    def pair(part, u, r):
+        slot = lax.rem(u, 2)
+        return remote(part.at[block(lax.rem(partner + 2 * r, ring))], theirs.at[slot, r], (pair_send.at[slot, r], pair_recv.at[slot, r]), partner)
 
     def far(u, way):
         cols = pl.ds(way * half, half)
@@ -390,34 +411,26 @@
         def _(n):
             act(pl.ds(pl.multiple_of(n, tile), tile))
 
-    def part(u):
-        load_att(u).wait()
-
-        @pl.when(u > 0)
-        def _():
+    def fetch(u):
+        @pl.when(u >= 2)
+        def _():
+            pl.semaphore_wait(free, 1)
             for r in range(chips):
-                pair(r).wait_send()
-
-        def act(at):
-            stage[:, at] = jnp.dot(att_buf[...], wo_buf[:, at], preferred_element_type=F32).astype(BF16)
-
-        columns(0, width, act)
-
-        @pl.when(u + 1 < batch)
-        def _():
-            load_att(u + 1).start()
-
-        @pl.when(u > 0)
-        def _():
-            pl.semaphore_wait(free, 1)
-
-        for r in range(chips):
-            pair(r).start()
+                pair(o_part.at[0], u, r).wait_send()
+
+        def act(part):
+            for r in range(chips):
+                pair(part, u, r).start()
+            for r in range(chips):
+                mine(part, u, r).start()
+
+        sourced(u, act)
 
     def combine(u):
         slot2, slot3 = lax.rem(u, 2), lax.rem(u, 3)
         for r in range(chips):
-            pair(r).wait_recv()
+            mine(o_part.at[0], u, r).wait()
+            pair(o_part.at[0], u, r).wait_recv()
 
         @pl.when(u >= 2)
         def _():
@@ -430,7 +443,7 @@
                 near(u - 3, way).wait_send()
 
         def chip_sum(r, at):
-            return stage[block(lax.rem(me + 2 * r, ring)), at].astype(F32) + theirs[r, :, at].astype(F32)
+            return ours[slot2, r, :, at].astype(F32) + theirs[slot2, r, :, at].astype(F32)
 
         def act_far(at):
             far_sum[slot2, :, at] = chip_sum(chips // 2, at).astype(BF16)
@@ -446,7 +459,7 @@
 
         columns(0, width, act)
 
-        @pl.when(u + 1 < batch)
+        @pl.when(u + 2 < units)
         def _():
             pl.semaphore_signal(free, inc=1, device_id={"tp": partner}, device_id_type=pl.DeviceIdType.MESH)
 
@@ -466,18 +479,31 @@
         slot = lax.rem(u, 3)
         for way in range(2):
             near(u, way).wait_recv()
-        load_x(u).wait()
 
         @pl.when(u > 0)
         def _():
-            store_y(u - 1).wait()
-
-        def act(at):
-            total = own_sum[slot, :, at] + near_in[slot, 0, :, at].astype(F32) + near_in[slot, 1, :, at].astype(F32)
-            y_buf[:, at] = (x_buf[:, at].astype(F32) + total + b_o[:, at]).astype(BF16)
-
-        columns(0, width, act)
-        store_y(u).start()
+            store_y(0).wait()
+
+        def total(at):
+            return own_sum[slot, :, at] + near_in[slot, 0, :, at].astype(F32) + near_in[slot, 1, :, at].astype(F32)
+
+        @pl.when(u < batch)
+        def _():
+            load_x(u).wait()
+
+            def act(at):
+                y_buf[:, at] = (x_buf[:, at].astype(F32) + total(at) + b_o[:, at]).astype(BF16)
+
+            columns(0, width, act)
+            store_y(u).start()
+
+        @pl.when(u >= batch)
+        def _():
+            def act(at):
+                y_buf[:, at] = total(at).astype(BF16)
+
+            columns(0, width, act)
+            store_sum(u).start()
 
         @pl.when(u + 1 < batch)
         def _():
@@ -488,7 +514,7 @@
         slot = lax.rem(lax.div(n, tile), 2)
         return pltpu.make_async_copy(dh_buf.at[slot], dh_out.at[b, :, at], dh_sem.at[slot])
 
-    def grad_part(dh_out, b, place):
+    def grad_part(b):
         for copy in load_grads(b):
             copy.wait()
 
@@ -496,11 +522,18 @@
         def _(n):
             @pl.when(n >= 2 * tile)
             def _():
-                store_dh(dh_out, place, n - 2 * tile).wait()
+                store_dh(dh_late, 0, n - 2 * tile).wait()
 
             at = pl.ds(pl.multiple_of(n, tile), tile)
-            dh_buf[lax.rem(lax.div(n, tile), 2)] = lax.dot_general(dq_buf[...], wq_buf[at, :], ACROSS, preferred_element_type=F32).astype(BF16)
-            store_dh(dh_out, place, n).start()
+            dh_buf[lax.rem(lax.div(n, tile), 2)] = lax.dot_general(dq_buf[...], w_buf[at, :], ACROSS, preferred_element_type=F32).astype(BF16)
+
+            @pl.when(b < early)
+            def _():
+                store_dh(dh_early, b, n).start()
+
+            @pl.when(b >= early)
+            def _():
+                store_dh(dh_late, b - early, n).start()
 
         @pl.when(b + 1 < batch)
         def _():
@@ -508,80 +541,76 @@
                 copy.start()
 
         for n in (width - 2 * tile, width - tile):
-            store_dh(dh_out, place, n).wait()
-
-    load_att(0).start()
-    load_wo.start()
-    for copy in load_back + load_grads(0):
+            store_dh(dh_late, 0, n).wait()
+
+    fetch(0)
+    for copy in load_w + load_grads(0):
         copy.start()
     load_x(0).start()
-    load_wo.wait()
-
-    @pl.loop(0, batch + 3)
+
+    @pl.loop(0, units + 3)
     def _(t):
-        @pl.when(jnp.logical_and(t >= 1, t < batch + 1))
+        @pl.when(jnp.logical_and(t >= 1, t < units + 1))
         def _():
             combine(t - 1)
 
+        @pl.when(jnp.logical_and(t >= 2, t < units + 2))
+        def _():
+            relay(t - 2)
+
+        @pl.when(t >= 3)
+        def _():
+            finish(t - 3)
+
+        @pl.when(t + 1 < units)
+        def _():
+            fetch(t + 1)
+
+        @pl.when(t == 2)
+        def _():
+            for copy in load_w:
+                copy.wait()
+
         @pl.when(jnp.logical_and(t >= 2, t < batch + 2))
         def _():
-            relay(t - 2)
-
-        @pl.when(t >= 3)
-        def _():
-            finish(t - 3)
-
-        @pl.when(t < batch)
-        def _():
-            part(t)
-
-        @pl.when(t == 2)
-        def _():
-            for copy in load_back:
-                copy.wait()
-
-        @pl.when(jnp.logical_and(t >= 2, t < batch // 2 + 2))
-        def _():
-            grad_part(dh_early, t - 2, t - 2)
-
-        @pl.when(jnp.logical_and(t >= batch // 2 + 2, t < batch + 2))
-        def _():
-            grad_part(dh_late, t - 2, t - 2 - batch // 2)
-
-    for r in range(chips):
-        pair(r).wait_send()
+            grad_part(t - 2)
+
     for way in range(2):
-        for u in (batch - 2, batch - 1):
+        for u in (units - 2, units - 1):
             far(u, way).wait_send()
-        for u in (batch - 3, batch - 2, batch - 1):
+        for u in (units - 3, units - 2, units - 1):
             near(u, way).wait_send()
-    store_y(batch - 1).wait()
-
-
-def project_and_scatter(merged, grad_q, grad_kv, w_o, w_q, w_kv, x_loc, b_o, ring):
+    for u in (units - 2, units - 1):
+        for r in range(chips):
+            pair(o_part.at[0], u, r).wait_send()
+    store_y(0).wait()
+
+
+def project_and_scatter(o_part, grad_q, grad_kv, w_q, w_kv, x_loc, b_o, early, ring):
     batch, rows, width = x_loc.shape
-    seq, q_width = merged.shape[1:]
+    seq, q_width = grad_q.shape[1:]
     qkv_width = q_width + w_kv.shape[1]
-    part = jax.ShapeDtypeStruct((batch // 2, seq, width), BF16)
+    chips = ring // 2
+    part = lambda n: jax.ShapeDtypeStruct((n, seq, width), BF16)
     hbm = pl.BlockSpec(memory_space=pl.ANY)
     vmem = pl.BlockSpec(memory_space=pltpu.VMEM)
     dma = pltpu.SemaphoreType.DMA
     return pl.pallas_call(
         scatter_kernel,
         name="project_and_scatter",
-        out_shape=(jax.ShapeDtypeStruct(x_loc.shape, BF16), part, part),
-        in_specs=[hbm, hbm, hbm, hbm, hbm, hbm, hbm, vmem],
-        out_specs=(hbm, hbm, hbm),
+        out_shape=(jax.ShapeDtypeStruct(x_loc.shape, BF16), part(early), part(batch - early), jax.ShapeDtypeStruct((early, rows, width), BF16)),
+        in_specs=[hbm] * 6 + [vmem],
+        out_specs=(hbm,) * 4,
         scratch_shapes=[
-            pltpu.VMEM((seq, q_width), BF16), pltpu.VMEM((seq, qkv_width), BF16), pltpu.VMEM((q_width, width), BF16), pltpu.VMEM((width, qkv_width), BF16),
-            pltpu.VMEM((seq, width), BF16), pltpu.VMEM((2, seq, 512), BF16), pltpu.VMEM((ring // 2, rows, width), BF16),
+            pltpu.VMEM((seq, qkv_width), BF16), pltpu.VMEM((width, qkv_width), BF16), pltpu.VMEM((2, chips, rows, width), BF16),
+            pltpu.VMEM((2, seq, 512), BF16), pltpu.VMEM((2, chips, rows, width), BF16),
             pltpu.VMEM((2, rows, width), BF16), pltpu.VMEM((3, 2, rows, width), BF16), pltpu.VMEM((3, rows, width), F32),
             pltpu.VMEM((3, rows, width), BF16), pltpu.VMEM((3, 2, rows, width), BF16), pltpu.VMEM((rows, width), BF16), pltpu.VMEM((rows, width), BF16),
-            dma((ring // 2,)), dma((ring // 2,)), dma((2, 2)), dma((3, 2)), dma((3, 2)), dma((3, 2)), pltpu.SemaphoreType.REGULAR,
-            dma((5,)), dma((3,)), dma((2,))],
+            dma((2, chips)), dma((2, chips)), dma((2, chips)), dma((2, 2)), dma((3, 2)), dma((3, 2)), dma((3, 2)), pltpu.SemaphoreType.REGULAR,
+            dma((4,)), dma((2,)), dma((2,))],
         compiler_params=pltpu.CompilerParams(collective_id=1, has_side_effects=True, vmem_limit_bytes=VMEM_LIMIT),
-        cost_estimate=pl.CostEstimate(flops=4 * batch * seq * width * q_width, bytes_accessed=4 * batch * seq * width, transcendentals=0),
-    )(merged, grad_q, grad_kv, w_o, w_q, w_kv, x_loc, b_o)
+        cost_estimate=pl.CostEstimate(flops=4 * batch * seq * width * q_width, bytes_accessed=6 * batch * seq * width, transcendentals=0),
+    )(o_part, grad_q, grad_kv, w_q, w_kv, x_loc, b_o)
 
 
 def norm_backward_kernel(dh, x, dy, ln_stats, gamma, *refs):
@@ -691,13 +720,12 @@
     def device_block(x_loc, ln_gamma, ln_beta, w_q, b_q, w_kv, b_kv, w_o, b_o, dy_loc):
         head_dim = w_kv.shape[1] // 2
         batch, _, width = x_loc.shape
-        normed_full, dy_full, _, merged, grad_q, kv_part, kv_twin, bo_rows, ln_stats = gather_and_attend(
+        normed_full, dy_full, merged, o_part, grad_q, kv_part, kv_twin, bo_rows, ln_stats = gather_and_attend(
             x_loc, dy_loc, ln_gamma[None, :], ln_beta[None, :], w_q, w_kv, b_q[None, :], b_kv[None, :], w_o, ring, head_dim)
+        early = 3 * batch // 8
         grad_kv = lax.psum(kv_twin, "tp")
-        y_loc, dh_early, dh_late = project_and_scatter(merged, grad_q, kv_part, w_o, w_q, w_kv, x_loc, b_o[None, :], ring)
-        scatter = lambda part: lax.psum_scatter(part, "tp", scatter_dimension=1, tiled=True)
-        dh_early_loc = scatter(dh_early)
-        dh_late_loc = scatter(dh_late)
+        y_loc, _, dh_part, dh_early = project_and_scatter(o_part, grad_q, kv_part, w_q, w_kv, x_loc, b_o[None, :], early, ring)
+        dh_late = lax.psum_scatter(dh_part, "tp", scatter_dimension=1, tiled=True)
 
         grad_q, merged, y_loc, bo_rows = lax.optimization_barrier((grad_q, merged, y_loc, bo_rows))
         y_loc = settle(y_loc)
@@ -708,8 +736,8 @@
         grad_wkv = jnp.einsum("bsd,bsc->dc", normed_full, grad_kv, preferred_element_type=jnp.float32)
         grad_bkv = jnp.sum(grad_kv, axis=(0, 1), dtype=jnp.float32)
         gamma = ln_gamma[None, :]
-        started, parts_early = norm_backward(dh_early_loc, x_loc, dy_loc, ln_stats, gamma, 0, None)
-        grad_x, parts_late = norm_backward(dh_late_loc, x_loc, dy_loc, ln_stats, gamma, batch // 2, started)
+        started, parts_early = norm_backward(dh_early, x_loc, dy_loc, ln_stats, gamma, 0, None)
+        grad_x, parts_late = norm_backward(dh_late, x_loc, dy_loc, ln_stats, gamma, early, started)
         sums = sum_over_ring(jnp.sum(parts_early + parts_late, axis=1).reshape(-1, 128), ring).reshape(2, width)
         return (y_loc, grad_x, sums[0], sums[1], grad_wq, grad_bq, grad_wkv, grad_bkv, grad_wo, grad_bo)
 

time: 1000 us -> 971 us (0.971)
  waiting for transfers between devices: 111 us -> 12.5 us
  Pallas kernels: 735 us -> 798 us
    reduce_scatter x2 -> x1, waiting for transfers between devices: 110 us -> 12.4 us  [device_block(): dh_late = lax.psum_scatter(dh_part, 'tp', scatter_dimension=1, tiled=True)]
    pallas_call x1, Pallas kernels: 240 us -> 308 us  [project_and_scatter(): pl.pallas_call(scatter_kernel, name='project_and_scatter', out_shape=(jax...]
  transfers between devices with their start and end apart: 3 -> 2, of which waited for: 1 -> 1; matrix products, arithmetic and copies ran while one was open for 13% -> 14% of each run, Pallas kernels for 26% -> 34%
where the time goes in v5:
time: 971 us; the launch traced here: 960 us
  Pallas kernels  798 us (82%)
  matrix products  122 us (13%)
  between operations  14.3 us (1%)
  waiting for transfers between devices  12.5 us (1%)
    pallas_call x1, Pallas kernels, gather_and_attend(): pl.pallas_call(functools.partial(gather_kernel, heads, dim), name='gather...  454 us
    pallas_call x1, Pallas kernels, project_and_scatter(): pl.pallas_call(scatter_kernel, name='project_and_scatter', out_shape=(jax...  308 us
    dot_general x1, matrix products, device_block(): jnp.einsum('bsd,bse->de', normed_full, grad_q, preferred_element_type=jnp...  48 us
    dot_general x1, matrix products, device_block(): jnp.einsum('bse,bsd->ed', merged, dy_full, preferred_element_type=jnp.flo...  47.8 us
    dot_general x1, matrix products, device_block(): jnp.einsum('bsd,bsc->dc', normed_full, grad_kv, preferred_element_type=jn...  25.9 us
  transfers between devices with their start and end apart: 2, of which 1 were waited for; matrix products, arithmetic and copies ran while one was open for 14% of the time, Pallas kernels for 34%

profile of v5, /device:TPU:112, one launch (start us, length us, event | category | flops | bytes accessed | tf_op | source)
XLA Modules:
  0.0 960.3 jit_solution(5206894607772892877)
XLA Ops:
  7.2 0.1 all-reduce.2.cloned.1.call-start
  7.3 1.3 broadcast_in_dim.18.b_q
  8.5 453.9 %gather_and_attend.1 = (bf16[8,512,6144]{2,1,0:T(8,128)(2,1)}, bf16[8,512,6144]{2,1,0:T(8,128)(2,1)}, bf16[8,512,768]{2,1,0:T(8,128)(2,1)}, bf16[8,512,6144]{2,1...) custom-call(bf16[8,64,6144]{2,1,0:T(8,128)(2,1)} %x.3, ...), custom_call_target="tpu_custom_call" | custom-call | flops 154618822656 | bytes 150994944 | tf_op jit(solution)/shard_map/gather_and_attend/pallas_call | solution.py:324
  462.5 0.1 all-reduce.2.cloned.1.call-update
  462.5 0.5 reduce-scatter.2.cloned.1.call-start
  463.1 308.0 %project_and_scatter.1 = (bf16[8,64,6144]{2,1,0:T(8,128)(2,1)}, bf16[3,512,6144]{2,1,0:T(8,128)(2,1)}, bf16[5,512,6144]{2,1,0:T(8,128)(2,1)}, bf16[3,64,6144]{2,1,0:T(8,128)(2,1)}) custom-call(bf16[8,512,6144]{2,1,0:T(8,128)(2,1)} %get-tuple-element.32.o_part, bf16[8,512,768]{2,1,0:T(8,128)(2,1)} %get-tuple-element.45.dq_hbm, ...), custom_call_target="tpu_custom_call" | custom-call | flops 77309411328 | bytes 150994944 | tf_op jit(solution)/shard_map/project_and_scatter/pallas_call | solution.py:598
  771.1 0.0 copy-start.1
  771.1 0.1 reduce-scatter.2.cloned.1.call-update
  771.2 0.9 copy-done.1
  772.0 0.7 reduce_sum.39
  772.7 7.8 norm_backward.2
  780.5 7.8 settle.1
  788.3 0.0 slice-start
  788.3 4.6 convert_reduce_fusion
  793.0 0.0 slice-start.1
  793.0 47.8 %convolution_bitcast_fusion.1 = f32[768,6144]{1,0:T(8,128)} fusion(bf16[8,512,768]{2,1,0:T(8,128)(2,1)} %get-tuple-element.47, bf16[8,512,6144]{2,1,0:T(8,128)(2,1)} %get-tuple-element.48), kind=kOutput, calls=%fused_computation.2 | convolution fusion | flops 38654705664 | bytes 75497472 | tf_op jit(solution)/shard_map/bse,bsd->ed/dot_general | solution.py:733
  840.7 0.0 slice-done
  840.7 0.0 slice-done.1
  840.7 48.0 %convolution_bitcast_fusion = f32[6144,768]{1,0:T(8,128)} fusion(bf16[8,512,6144]{2,1,0:T(8,128)(2,1)} %get-tuple-element.44, bf16[8,512,768]{2,1,0:T(8,128)(2,1)S(1)} %bitcast.21), kind=kOutput, calls=%fused_computation.1 | convolution fusion | flops 38654705664 | bytes 75497472 | tf_op jit(solution)/shard_map/bsd,bse->de/dot_general | solution.py:734
  888.7 0.0 all-reduce.2.cloned.1.call-done
  888.7 2.7 convert_reduce_fusion.1
  891.5 25.9 %convolution_bitcast_fusion.2 = f32[6144,256]{1,0:T(8,128)} fusion(bf16[8,512,6144]{2,1,0:T(8,128)(2,1)} %get-tuple-element.44, bf16[8,512,256]{2,1,0:T(8,128)(2,1)} %all-reduce.2.cloned.1.call-done), kind=kOutput, calls=%fused_computation.3 | convolution fusion | flops 12884901888 | bytes 58720256 | tf_op jit(solution)/shard_map/bsd,bsc->dc/dot_general | solution.py:736
  917.4 12.4 %reduce-scatter.2.cloned.1.call-done.dh = bf16[5,64,6144]{2,1,0:T(8,128)(2,1)} async-done(((bf16[5,512,6144]{2,1,0:T(8,128)(2,1)}), bf16[5,64,6144]{2,1,0:T(8,128)(2,1)}) %reduce-scatter.2.cloned.1.call-update) | async-done | bytes 3932176 | tf_op jit(solution)/shard_map/reduce_scatter | solution.py:728
  929.8 0.0 copy-start
  929.8 10.5 %norm_backward.3 = (bf16[8,64,6144]{2,1,0:T(8,128)(2,1)}, f32[2,8,6144]{2,1,0:T(8,128)}) custom-call(bf16[5,64,6144]{2,1,0:T(8,128)(2,1)} %reduce-scatter.2.cloned.1.call-done.dh, bf16[8,64,6144]{2,1,0:T(8,128)(2,1)} %x.3, bf16[8,64,6144]{2,1,0:T(8,128)(2,1)} %dy.3, f32[2,8,64,128]{3,2,1,0:T(8,128)} %get-tuple-element.38.ln_stats, ...), custom_call_target="tpu_custom_call", output_to_operand_aliasing={{0}: (5, {})} | custom-call | flops 117964800 | bytes 15728640 | tf_op jit(solution)/shard_map/norm_backward/pallas_call | solution.py:653
  940.3 0.0 copy-done
  940.3 1.1 add_reduce_fusion
  941.5 0.7 reshape.28.parts
  942.1 9.8 %sum_over_ring.1 = f32[96,128]{1,0:T(8,128)} custom-call(f32[96,128]{1,0:T(8,128)} %reshape.28.parts), custom_call_target="tpu_custom_call" | custom-call | tf_op jit(solution)/shard_map/sum_over_ring/pallas_call | solution.py:706
  951.9 1.4 slice_bitcast_fusion
  (1 shorter events, 0.0 us)
Async XLA Ops:
  7.2 881.5 %all-reduce.2.cloned.1.call-start = ((), (), s32[]{:S(2)}) async-start(), calls=%async_computation.2 | async-start | bytes 4194304 | tf_op jit(solution)/shard_map/psum | solution.py:726
  462.5 467.3 %reduce-scatter.2.cloned.1.call-start = ((), (), s32[]{:S(2)}) async-start(), calls=%async_computation.1 | async-start | bytes 35389440 | tf_op jit(solution)/shard_map/reduce_scatter | solution.py:728
  771.1 0.9 copy-start.1
  788.3 52.4 %slice-start = ((s8[6291456]{0:T(1024)(128)(4,1)}), s8[4194304]{0:T(1024)(128)(4,1)S(1)}, s32[]{:S(2)}) async-start(s8[6291456]{0:T(1024)(128)(4,1)} %bitcast.20), calls=%async_computation.3 | async-start | bytes 8388608
  793.0 47.8 %slice-start.1 = ((s8[6291456]{0:T(1024)(128)(4,1)}), s8[2097152]{0:T(1024)(128)(4,1)S(1)}, s32[]{:S(2)}) async-start(s8[6291456]{0:T(1024)(128)(4,1)} %bitcast.20), calls=%async_computation.4 | async-start | bytes 4194304
  929.8 10.5 %copy-start = (f32[2,8,6144]{2,1,0:T(8,128)S(1)}, f32[2,8,6144]{2,1,0:T(8,128)}, u32[]{:S(2)}) copy-start(f32[2,8,6144]{2,1,0:T(8,128)} %get-tuple-element.42) | copy-start | bytes 1179652
Sparse Core Ops, SparseCore 0:
  462.7 75.3 all-reduce.1
  771.3 158.4 reduce-scatter.1

commit v6 on v5

v6 whole, which is shorter than its diff:
```python
import functools

import jax
import jax.numpy as jnp
from jax import lax
from jax.experimental import pallas as pl
from jax.experimental.pallas import tpu as pltpu
from jax.sharding import PartitionSpec as P

LN_EPS = 1e-5
VMEM_LIMIT = 64 * 1024 * 1024 - 65536
BF16 = jnp.bfloat16
F32 = jnp.float32

RIGHT, LEFT, PART, FAR_R, FAR_L, PASS_L, PASS_R, PASS_F = range(8)


def stack_heads(rows, dst, first, heads, dim):
    for h in range(heads):
        dst[h * dim : (h + 1) * dim, :] = rows[first : first + dim, h * dim : (h + 1) * dim]


def scaled_scores(scores_s, lanes, first, dim):
    scores = scores_s[: first + dim, lanes] * dim**-0.5
    keys = lax.broadcasted_iota(jnp.int32, scores.shape, 0)
    queries = lax.broadcasted_iota(jnp.int32, scores.shape, 1) + first
    return jnp.where(keys <= queries, scores, -1e30)


ACROSS = (((1,), (1,)), ((), ()))
DOWN = (((0,), (0,)), ((), ()))


def attend(qkv, out, stats, scores_s, probs_s, q_s, heads, dim):
    rows = qkv.shape[0]
    width = heads * dim
    for first in range(0, rows, dim):
        last = first + dim
        stack_heads(qkv, q_s, first, heads, dim)
        scores_s[:last, :] = lax.dot_general(qkv[:last, width : width + dim], q_s[...], ACROSS, preferred_element_type=F32)

        @pl.loop(0, heads, unroll=2)
        def _(h):
            lanes = pl.ds(pl.multiple_of(h * dim, dim), dim)
            scores = scaled_scores(scores_s, lanes, first, dim)
            top = jnp.max(scores, axis=0, keepdims=True)
            weights = jnp.exp(scores - top)
            share = 1.0 / jnp.sum(weights, axis=0, keepdims=True)
            probs_s[:last, lanes] = (weights * share).astype(BF16)
            stats[h, 0:1, first:last] = top
            stats[h, 1:2, first:last] = share

        turned = lax.dot_general(qkv[:last, width + dim :], probs_s[:last, :], DOWN, preferred_element_type=F32)
        for h in range(heads):
            out[first:last, h * dim : (h + 1) * dim] = turned[:, h * dim : (h + 1) * dim].T.astype(BF16)


def attend_backward(qkv, grad_att, grad_q, grad_kv, stats, scores_s, grad_p_s, probs_s, grad_s_s, q_s, att_s, heads, dim):
    rows = qkv.shape[0]
    width = heads * dim
    grad_kv[...] = jnp.zeros_like(grad_kv)
    for first in range(0, rows, dim):
        last = first + dim
        stack_heads(qkv, q_s, first, heads, dim)
        stack_heads(grad_att, att_s, first, heads, dim)
        scores_s[:last, :] = lax.dot_general(qkv[:last, width : width + dim], q_s[...], ACROSS, preferred_element_type=F32)
        grad_p_s[:last, :] = lax.dot_general(qkv[:last, width + dim :], att_s[...], ACROSS, preferred_element_type=F32)

        @pl.loop(0, heads, unroll=2)
        def _(h):
            lanes = pl.ds(pl.multiple_of(h * dim, dim), dim)
            scores = scaled_scores(scores_s, lanes, first, dim)
            probs = jnp.exp(scores - stats[h, 0:1, first:last]) * stats[h, 1:2, first:last]
            grad_p = grad_p_s[:last, lanes].astype(BF16).astype(F32)
            row_dot = jnp.sum(probs * grad_p, axis=0, keepdims=True)
            grad_s_s[:last, lanes] = (probs * (grad_p - row_dot) * dim**-0.5).astype(BF16)
            probs_s[:last, lanes] = probs.astype(BF16)

        turned = lax.dot_general(qkv[:last, width : width + dim], grad_s_s[:last, :], DOWN, preferred_element_type=F32)
        for h in range(heads):
            grad_q[first:last, h * dim : (h + 1) * dim] = turned[:, h * dim : (h + 1) * dim].T.astype(BF16)
        grad_kv[:last, :dim] += jnp.dot(grad_s_s[:last, :], q_s[...], preferred_element_type=F32)
        grad_kv[:last, dim:] += jnp.dot(probs_s[:last, :], att_s[...], preferred_element_type=F32)


def block_kernel(heads, dim, x_hbm, dy_hbm, gamma, beta, wq_hbm, wkv_hbm, b_q, b_kv, wo_hbm, b_o,
                 h_full, dy_full, att_out, o_part, dq_out, dkv_part, dkv_full, y_out, dh_early, dh_late, dh_sum, dbo, ln_stats,
                 own, w_buf, wo_buf, h_buf, qkv_buf, att_buf, da_buf, dq_buf, dkv_buf, part_buf, total, stats,
                 scores_s, grad_p_s, probs_s, grad_s_s, q_s, att_s, theirs, far_in, near_in, kv_theirs, kv_far_in, kv_near_in,
                 send, recv, x_sem, dy_sem, keep_sem, w_sem, h_sem, att_sem, dq_sem, dkv_sem, part_sem, load_sem,
                 ours_sem, pair_send, pair_recv, far_send, far_recv, near_send, near_recv, free,
                 kv_ours_sem, kv_pair_send, kv_pair_recv, kv_far_send, kv_far_recv, kv_near_send, kv_near_recv, kv_send, kv_recv, kv_keep_sem):
    batch, rows, width = x_hbm.shape
    early = dh_early.shape[0]
    half = rows // 2
    wide = width // 2
    units = 2 * batch
    scatters = batch + early
    ring = h_full.shape[1] // rows
    chips = ring // 2
    q_width = heads * dim
    kv_width = 2 * dim
    tile = 512
    me = lax.axis_index("tp")
    partner = me + 1 - 2 * lax.rem(me, 2)
    right, left, far_chip = lax.rem(me + 2, ring), lax.rem(me + ring - 2, ring), lax.rem(me + ring // 2, ring)
    OURS, NEAR, SUM, FAR, X, Y = 0, 4, 10, 13, units, units + 1

    barrier = pltpu.get_barrier_semaphore()
    for other in (left, right, partner):
        pl.semaphore_signal(barrier, inc=1, device_id={"tp": other}, device_id_type=pl.DeviceIdType.MESH)
    pl.semaphore_wait(barrier, 3)

    def remote(src, dst, sems, to):
        return pltpu.make_async_remote_copy(
            src_ref=src, dst_ref=dst, send_sem=sems[0], recv_sem=sems[1], device_id={"tp": to}, device_id_type=pl.DeviceIdType.MESH)

    def columns(low, high, act, step=tile):
        @pl.loop(low, high, step=step)
        def _(n):
            act(pl.ds(pl.multiple_of(n, step), step))

    def block(full, b, owner, first=0, count=rows):
        return full.at[b, pl.ds(pl.multiple_of(owner * rows + first, half), count)]

    def move(kind, full, b, u):
        if kind in (RIGHT, LEFT, PART):
            src, dst = own.at[u], block(full, b, me)
        elif kind in (FAR_R, FAR_L):
            src = dst = block(full, b, left, 0, half) if kind == FAR_R else block(full, b, right, half, half)
        else:
            src = dst = block(full, b, {PASS_L: left, PASS_R: right, PASS_F: far_chip}[kind])
        to = {RIGHT: right, FAR_R: right, LEFT: left, FAR_L: left}.get(kind, partner)
        return remote(src, dst, (send.at[kind, u], recv.at[kind, u]), to)

    def keep(full, b, u):
        return pltpu.make_async_copy(own.at[u], block(full, b, me), keep_sem.at[u])

    def load_x(b):
        return pltpu.make_async_copy(x_hbm.at[b], own.at[units + lax.rem(b, 2)], x_sem.at[lax.rem(b, 2)])

    def load_dy(b):
        return pltpu.make_async_copy(dy_hbm.at[b], own.at[2 * b + 1], dy_sem.at[b])

    def turn(u, h_act, dy_act):
        b = lax.div(u, 2)
        inside = jnp.logical_and(u >= 0, u < units)

        @pl.when(jnp.logical_and(inside, lax.rem(u, 2) == 0))
        def _():
            h_act(b)

        @pl.when(jnp.logical_and(inside, lax.rem(u, 2) == 1))
        def _():
            dy_act(b)

    def unit(u, act):
        turn(u, lambda b: act(h_full, b, u), lambda b: act(dy_full, b, u))

    def normalise(b):
        load_x(b).wait()
        slot = units + lax.rem(b, 2)

        @pl.loop(0, rows, step=16)
        def _(r):
            at = pl.ds(pl.multiple_of(r, 16), 16)
            x_wide = own[slot, at, :].astype(F32)
            mean = jnp.mean(x_wide, axis=-1, keepdims=True)
            centred = x_wide - mean
            inv_std = lax.rsqrt(jnp.mean(centred * centred, axis=-1, keepdims=True) + LN_EPS)
            own[2 * b, at, :] = (centred * inv_std * gamma[...] + beta[...]).astype(BF16)
            ln_stats[0, b, at, :] = jnp.broadcast_to(mean, (16, 128))
            ln_stats[1, b, at, :] = jnp.broadcast_to(inv_std, (16, 128))

        @pl.when(b + 2 < batch)
        def _():
            load_x(b + 2).start()

    def launch(u):
        turn(u, normalise, lambda b: load_dy(b).wait())

        def act(full, b, u):
            for kind in (RIGHT, LEFT, PART):
                move(kind, full, b, u).start()
            keep(full, b, u).start()

        unit(u, act)

    def forward(full, b, u):
        move(RIGHT, full, b, u).wait_recv()
        move(FAR_R, full, b, u).start()
        move(LEFT, full, b, u).wait_recv()
        move(FAR_L, full, b, u).start()

    def share(full, b, u):
        move(PASS_L, full, b, u).start()
        move(PASS_R, full, b, u).start()

    def share_far(full, b, u):
        move(FAR_R, full, b, u).wait_recv()
        move(FAR_L, full, b, u).wait_recv()
        move(PASS_F, full, b, u).start()

    def complete(full, b, u):
        for kind in (PART, PASS_L, PASS_R, PASS_F):
            move(kind, full, b, u).wait_recv()
        keep(full, b, u).wait()

    def retire(full, b, u):
        for kind in range(8):
            move(kind, full, b, u).wait_send()

    def load_block(full, b):
        load = pltpu.make_async_copy(full.at[b], h_buf, h_sem.at[0])
        load.start()
        load.wait()

    def project(b):
        load_block(h_full, b)

        def act(at):
            qkv_buf[:, at] = (jnp.dot(h_buf[...], w_buf[:, at], preferred_element_type=F32) + b_q[:, at]).astype(BF16)

        columns(0, q_width, act, 256)
        at = pl.ds(q_width, kv_width)
        qkv_buf[:, at] = (jnp.dot(h_buf[...], w_buf[:, at], preferred_element_type=F32) + b_kv[...]).astype(BF16)

    def store_att(b):
        return pltpu.make_async_copy(att_buf, att_out.at[b], att_sem.at[0])

    def store_part(out, b, n):
        at = pl.ds(pl.multiple_of(n, tile), tile)
        slot = lax.rem(lax.div(n, tile), 2)
        return pltpu.make_async_copy(part_buf.at[slot], out.at[b, :, at], part_sem.at[slot])

    def make_part(product, store):
        @pl.loop(0, width, step=tile)
        def _(n):
            @pl.when(n >= 2 * tile)
            def _():
                store_part(o_part, 0, n - 2 * tile).wait()

            part_buf[lax.rem(lax.div(n, tile), 2)] = product(pl.ds(pl.multiple_of(n, tile), tile)).astype(BF16)
            store(n)

        for n in (width - 2 * tile, width - tile):
            store_part(o_part, 0, n).wait()

    def attend_and_project(b):
        @pl.when(b > 0)
        def _():
            store_att(b - 1).wait()

        attend(qkv_buf, att_buf, stats, scores_s, probs_s, q_s, heads, dim)
        store_att(b).start()
        make_part(lambda at: jnp.dot(att_buf[...], wo_buf[:, at], preferred_element_type=F32), lambda n: store_part(o_part, b, n).start())

    def grad_attended(b):
        load_block(dy_full, b)

        def act(at):
            da_buf[:, at] = lax.dot_general(h_buf[...], wo_buf[at, :], ACROSS, preferred_element_type=F32).astype(BF16)

        columns(0, q_width, act, 256)

        def add(at):
            dbo[:, at] += jnp.sum(h_buf[:, at].astype(F32).reshape(-1, 8, tile), axis=0)

        columns(0, width, add)

    def store_dq(b):
        return pltpu.make_async_copy(dq_buf, dq_out.at[b], dq_sem.at[0])

    def store_dkv(b, owner):
        return pltpu.make_async_copy(dkv_buf.at[pl.ds(owner * rows, rows)], dkv_part.at[owner, pl.ds(pl.multiple_of(b * rows, rows), rows)], dkv_sem.at[owner])

    def stored(b):
        store_dq(b).wait()
        for owner in range(ring):
            store_dkv(b, owner).wait()

    def differentiate(b):
        @pl.when(b > 0)
        def _():
            stored(b - 1)

        attend_backward(qkv_buf, da_buf, dq_buf, total, stats, scores_s, grad_p_s, probs_s, grad_s_s, q_s, att_s, heads, dim)
        dkv_buf[...] = total[...].astype(BF16)
        store_dq(b).start()
        for owner in range(ring):
            store_dkv(b, owner).start()

    def grad_part(b):
        copies = [pltpu.make_async_copy(dq_out.at[b], qkv_buf.at[:, pl.ds(0, q_width)], load_sem.at[ring])]
        for owner in range(ring):
            copies.append(pltpu.make_async_copy(dkv_part.at[owner, pl.ds(pl.multiple_of(b * rows, rows), rows)],
                                                qkv_buf.at[pl.ds(owner * rows, rows), pl.ds(q_width, kv_width)], load_sem.at[owner]))
        for copy in copies:
            copy.start()
        for copy in copies:
            copy.wait()

        def store(n):
            @pl.when(b < early)
            def _():
                store_part(dh_early, b, n).start()

            @pl.when(b >= early)
            def _():
                store_part(dh_late, b - early, n).start()

        make_part(lambda at: lax.dot_general(qkv_buf[...], w_buf[at, :], ACROSS, preferred_element_type=F32), store)

    def line(owner):
        return pl.ds(pl.multiple_of(owner * rows, rows), rows)

    def sourced(u, act):
        @pl.when(u < batch)
        def _():
            act(o_part.at[u])

        @pl.when(u >= batch)
        def _():
            act(dh_early.at[u - batch])

    def mine(part, r):
        return pltpu.make_async_copy(part.at[line(lax.rem(me + 2 * r, ring))], own.at[OURS + r], ours_sem.at[r])

    def pair(part, r):
        return remote(part.at[line(lax.rem(partner + 2 * r, ring))], theirs.at[r], (pair_send.at[r], pair_recv.at[r]), partner)

    def far(u, way):
        cols = pl.ds(way * wide, wide)
        return remote(own.at[FAR + lax.rem(u, 2), :, cols], far_in.at[lax.rem(u, 3), :, cols],
                      (far_send.at[lax.rem(u, 2), way], far_recv.at[lax.rem(u, 3), way]), (right, left)[way])

    def near(u, way):
        slot = lax.rem(u, 3)
        return remote(own.at[NEAR + 2 * slot + way], near_in.at[slot, way], (near_send.at[slot, way], near_recv.at[slot, way]), (right, left)[way])

    def fetch(u):
        @pl.when(u >= 1)
        def _():
            pl.semaphore_wait(free, 1)
            for r in range(chips):
                pair(o_part.at[0], r).wait_send()

        def act(part):
            for r in range(chips):
                pair(part, r).start()
            for r in range(chips):
                mine(part, r).start()

        sourced(u, act)

    def combine(u):
        slot2, slot3 = lax.rem(u, 2), lax.rem(u, 3)
        for r in range(chips):
            mine(o_part.at[0], r).wait()
            pair(o_part.at[0], r).wait_recv()

        @pl.when(u >= 2)
        def _():
            for way in range(2):
                far(u - 2, way).wait_send()

        @pl.when(u >= 3)
        def _():
            for way in range(2):
                near(u - 3, way).wait_send()

        def chip_sum(r, at):
            return (own[OURS + r, :, at].astype(F32) + theirs[r, :, at].astype(F32)).astype(BF16)

        def act_far(at):
            own[FAR + slot2, :, at] = chip_sum(chips // 2, at)

        columns(0, width, act_far)
        for way in range(2):
            far(u, way).start()

        def act(at):
            own[NEAR + 2 * slot3, :, at] = chip_sum(1, at)
            own[NEAR + 2 * slot3 + 1, :, at] = chip_sum(chips - 1, at)
            own[SUM + slot3, :, at] = chip_sum(0, at)

        columns(0, width, act)

        @pl.when(u + 1 < scatters)
        def _():
            pl.semaphore_signal(free, inc=1, device_id={"tp": partner}, device_id_type=pl.DeviceIdType.MESH)

    def relay(u):
        slot = lax.rem(u, 3)
        for way in range(2):
            far(u, way).wait_recv()
        for way in range(2):
            def act(at):
                place = NEAR + 2 * slot + way
                own[place, :, at] = (own[place, :, at].astype(F32) + far_in[slot, :, at].astype(F32)).astype(BF16)

            columns(way * wide, way * wide + wide, act)
        for way in range(2):
            near(u, way).start()

    def scatter_x(u):
        return pltpu.make_async_copy(x_hbm.at[u], own.at[X], load_sem.at[ring + 1])

    def store_y(out, b):
        return pltpu.make_async_copy(own.at[Y], out.at[b], load_sem.at[ring + 2])

    def finish(u):
        slot = lax.rem(u, 3)
        for way in range(2):
            near(u, way).wait_recv()

        @pl.when(u > 0)
        def _():
            store_y(y_out, 0).wait()

        def whole(at):
            return own[SUM + slot, :, at].astype(F32) + near_in[slot, 0, :, at].astype(F32) + near_in[slot, 1, :, at].astype(F32)

        @pl.when(u < batch)
        def _():
            scatter_x(u).wait()

            def act(at):
                own[Y, :, at] = (own[X, :, at].astype(F32) + whole(at) + b_o[:, at]).astype(BF16)

            columns(0, width, act)
            store_y(y_out, u).start()

        @pl.when(u >= batch)
        def _():
            def act(at):
                own[Y, :, at] = whole(at).astype(BF16)

            columns(0, width, act)
            store_y(dh_sum, u - batch).start()

        @pl.when(u + 1 < batch)
        def _():
            scatter_x(u + 1).start()

    pick = lambda ref, n: ref.at[:, pl.ds(n * kv_width, kv_width)]
    kv_ours = [pick(probs_s, 0), pick(probs_s, 1), pick(probs_s, 2), pick(grad_s_s, 0)]
    kv_far, kv_sum = pick(grad_s_s, 1), pick(da_buf, 2)
    kv_near = [pick(da_buf, 0), pick(da_buf, 1)]
    kv_rows = batch * rows
    kv_half = kv_rows // 2

    def kv_mine(r):
        return pltpu.make_async_copy(dkv_part.at[lax.rem(me + 2 * r, ring)], kv_ours[r], kv_ours_sem.at[r])

    def kv_pair(r):
        return remote(dkv_part.at[lax.rem(partner + 2 * r, ring)], kv_theirs.at[r], (kv_pair_send.at[r], kv_pair_recv.at[r]), partner)

    def kv_far_copy(way):
        at = pl.ds(way * kv_half, kv_half)
        return remote(kv_far.at[at], kv_far_in.at[at], (kv_far_send.at[way], kv_far_recv.at[way]), (right, left)[way])

    def kv_near_copy(way):
        return remote(kv_near[way], kv_near_in.at[way], (kv_near_send.at[way], kv_near_recv.at[way]), (right, left)[way])

    def kv_move(kind):
        if kind in (RIGHT, LEFT, PART):
            src, dst = kv_sum, dkv_full.at[me]
        elif kind in (FAR_R, FAR_L):
            src = dst = dkv_full.at[left, pl.ds(0, kv_half)] if kind == FAR_R else dkv_full.at[right, pl.ds(kv_half, kv_half)]
        else:
            src = dst = dkv_full.at[{PASS_L: left, PASS_R: right, PASS_F: far_chip}[kind]]
        to = {RIGHT: right, FAR_R: right, LEFT: left, FAR_L: left}.get(kind, partner)
        return remote(src, dst, (kv_send.at[kind], kv_recv.at[kind]), to)

    def kv_keep():
        return pltpu.make_async_copy(kv_sum, dkv_full.at[me], kv_keep_sem.at[0])

    def kv_steps():
        def start():
            stored(batch - 1)
            for r in range(chips):
                kv_pair(r).start()
                kv_mine(r).start()

        def sum_chip():
            for r in range(chips):
                kv_mine(r).wait()
                kv_pair(r).wait_recv()
            chip = lambda r: (kv_ours[r][...].astype(F32) + kv_theirs[r].astype(F32)).astype(BF16)
            kv_far[...] = chip(chips // 2)
            for way in range(2):
                kv_far_copy(way).start()
            kv_near[0][...] = chip(1)
            kv_near[1][...] = chip(chips - 1)

        def relay_far():
            for way in range(2):
                kv_far_copy(way).wait_recv()
            for way in range(2):
                at = slice(way * kv_half, way * kv_half + kv_half)
                kv_near[way][at, :] = (kv_near[way][at, :].astype(F32) + kv_far_in[at, :].astype(F32)).astype(BF16)
            for way in range(2):
                kv_near_copy(way).start()

        def sum_all():
            for way in range(2):
                kv_near_copy(way).wait_recv()
            chip = kv_ours[0][...].astype(F32) + kv_theirs[0].astype(F32)
            kv_sum[...] = (chip + kv_near_in[0].astype(F32) + kv_near_in[1].astype(F32)).astype(BF16)
            for kind in (RIGHT, LEFT, PART):
                kv_move(kind).start()
            kv_keep().start()

        def spread():
            kv_move(RIGHT).wait_recv()
            kv_move(FAR_R).start()
            kv_move(LEFT).wait_recv()
            kv_move(FAR_L).start()
            kv_move(PASS_L).start()
            kv_move(PASS_R).start()

        def spread_far():
            kv_move(FAR_R).wait_recv()
            kv_move(FAR_L).wait_recv()
            kv_move(PASS_F).start()

        def settle_kv():
            for kind in (PART, PASS_L, PASS_R, PASS_F):
                kv_move(kind).wait_recv()
            kv_keep().wait()
            for kind in range(8):
                kv_move(kind).wait_send()
            for way in range(2):
                kv_far_copy(way).wait_send()
                kv_near_copy(way).wait_send()
            for r in range(chips):
                kv_pair(r).wait_send()

        return start, sum_chip, relay_far, sum_all, spread, spread_far, settle_kv

    load_x(0).start()
    load_dy(0).start()
    load_x(1).start()
    weights = (pltpu.make_async_copy(wq_hbm, w_buf.at[:, pl.ds(0, q_width)], w_sem.at[0]),
               pltpu.make_async_copy(wkv_hbm, w_buf.at[:, pl.ds(q_width, kv_width)], w_sem.at[1]),
               pltpu.make_async_copy(wo_hbm, wo_buf, w_sem.at[2]))
    launch(0)
    launch(1)
    for copy in weights:
        copy.start()
    for b in range(1, batch):
        load_dy(b).start()
    dbo[...] = jnp.zeros_like(dbo)
    for copy in weights:
        copy.wait()

    lead = units - 2

    @pl.loop(0, lead + scatters + 3)
    def _(s):
        t = s - lead
        when = lambda low, high: pl.when(jnp.logical_and(t >= low, t < high))

        @pl.when(s < units)
        def _():
            unit(s, forward)

        launch(s + 2)

        @pl.when(s < units)
        def _():
            unit(s, share)

        unit(s - 2, retire)

        @when(1, scatters + 1)
        def _():
            combine(t - 1)

        @when(2, scatters + 2)
        def _():
            relay(t - 2)

        turn(s - 2, attend_and_project, differentiate)
        unit(s - 1, share_far)
        unit(s - 1, complete)
        turn(s - 1, project, grad_attended)

        @when(3, scatters + 3)
        def _():
            finish(t - 3)

        @when(0, scatters)
        def _():
            fetch(t)

        @when(2, 3)
        def _():
            scatter_x(0).start()

        for n, act in enumerate(kv_steps()):
            @when(4 + n, 5 + n)
            def _():
                act()

        @when(4, 4 + batch)
        def _():
            grad_part(t - 4)

    store_att(batch - 1).wait()
    store_y(y_out, 0).wait()
    for r in range(chips):
        pair(o_part.at[0], r).wait_send()
    for way in range(2):
        for u in (scatters - 2, scatters - 1):
            far(u, way).wait_send()
        for u in (scatters - 3, scatters - 2, scatters - 1):
            near(u, way).wait_send()


def attention_block(x_loc, dy_loc, gamma, beta, w_q, w_kv, b_q, b_kv, w_o, b_o, early, ring, dim):
    batch, rows, width = x_loc.shape
    q_width, kv_width = w_q.shape[1], w_kv.shape[1]
    qkv_width = q_width + kv_width
    seq = rows * ring
    units = 2 * batch
    chips = ring // 2
    heads = q_width // dim
    hbm = pl.BlockSpec(memory_space=pl.ANY)
    vmem = pl.BlockSpec(memory_space=pltpu.VMEM)
    dma = pltpu.SemaphoreType.DMA
    full = lambda n, w: jax.ShapeDtypeStruct((n, seq, w), BF16)
    at_home = lambda n: jax.ShapeDtypeStruct((n, rows, width), BF16)
    owned = jax.ShapeDtypeStruct((ring, batch * rows, kv_width), BF16)
    lo, hi = (lambda *shape: pltpu.VMEM(shape, BF16)), (lambda *shape: pltpu.VMEM(shape, F32))
    return pl.pallas_call(
        functools.partial(block_kernel, heads, dim),
        name="attention_block",
        out_shape=(full(batch, width), full(batch, width), full(batch, q_width), full(batch, width), full(batch, q_width), owned, owned, at_home(batch),
                   full(early, width), full(batch - early, width), at_home(early),
                   jax.ShapeDtypeStruct((8, width), F32), jax.ShapeDtypeStruct((2, batch, rows, 128), F32)),
        in_specs=[hbm, hbm, vmem, vmem, hbm, hbm, vmem, vmem, hbm, vmem],
        out_specs=(hbm,) * 11 + (vmem, vmem),
        scratch_shapes=[
            lo(units + 2, rows, width), lo(width, qkv_width), lo(q_width, width), lo(seq, width), lo(seq, qkv_width), lo(seq, q_width), lo(seq, q_width),
            lo(seq, q_width), lo(seq, kv_width), lo(2, seq, 512), hi(seq, kv_width), hi(heads, 8, seq),
            hi(seq, q_width), hi(seq, q_width), lo(seq, q_width), lo(seq, q_width), lo(q_width, dim), lo(q_width, dim),
            lo(chips, rows, width), lo(3, rows, width), lo(3, 2, rows, width),
            lo(chips, batch * rows, kv_width), lo(batch * rows, kv_width), lo(2, batch * rows, kv_width),
            dma((8, units)), dma((8, units)), dma((2,)), dma((batch,)), dma((units,)), dma((3,)), dma((1,)), dma((1,)), dma((1,)), dma((ring,)), dma((2,)),
            dma((ring + 3,)),
            dma((chips,)), dma((chips,)), dma((chips,)), dma((2, 2)), dma((3, 2)), dma((3, 2)), dma((3, 2)), pltpu.SemaphoreType.REGULAR,
            dma((chips,)), dma((chips,)), dma((chips,)), dma((2,)), dma((2,)), dma((2,)), dma((2,)), dma((8,)), dma((8,)), dma((1,))],
        compiler_params=pltpu.CompilerParams(collective_id=0, has_side_effects=True, vmem_limit_bytes=VMEM_LIMIT),
        cost_estimate=pl.CostEstimate(flops=8 * batch * seq * width * qkv_width, bytes_accessed=12 * batch * seq * width, transcendentals=0),
    )(x_loc, dy_loc, gamma, beta, w_q, w_kv, b_q, b_kv, w_o, b_o)


def norm_backward_kernel(dh, x, dy, ln_stats, gamma, *refs):
    dx, sums = refs[-2:]
    rows, width = x.shape[1:]
    tile = 512

    @pl.when(pl.program_id(0) == 0)
    def _():
        sums[...] = jnp.zeros_like(sums)

    mean, inv_std = ln_stats[0, 0, :, :1], ln_stats[1, 0, :, :1]
    by_lane = lambda v: sum(v[:, n : n + 128] for n in range(0, tile, 128))
    by_sublane = lambda v: jnp.sum(v.reshape(-1, 8, tile), axis=0)
    plain = along = jnp.zeros((rows, 128), F32)
    for n in range(0, width, tile):
        at = slice(n, n + tile)
        grad_h = dh[0, :, at].astype(F32)
        x_hat = (x[0, :, at].astype(F32) - mean) * inv_std
        both = grad_h * x_hat
        plain = plain + by_lane(grad_h * gamma[:, at])
        along = along + by_lane(both * gamma[:, at])
        sums[0, :, at] += by_sublane(both)
        sums[1, :, at] += by_sublane(grad_h)
    plain = jnp.sum(plain, axis=-1, keepdims=True) / width
    along = jnp.sum(along, axis=-1, keepdims=True) / width
    for n in range(0, width, tile):
        at = slice(n, n + tile)
        x_hat = (x[0, :, at].astype(F32) - mean) * inv_std
        grad_in = inv_std * (dh[0, :, at].astype(F32) * gamma[:, at] - plain - x_hat * along)
        dx[0, :, at] = (dy[0, :, at].astype(F32) + grad_in).astype(BF16)


def norm_backward(grad_h, x_loc, dy_loc, ln_stats, gamma, first, started):
    rows, width = x_loc.shape[1:]
    count = grad_h.shape[0]
    block = lambda skip: pl.BlockSpec((1, rows, width), lambda b: (b + skip, 0, 0))
    still = lambda shape: pl.BlockSpec(shape, lambda b: (0,) * len(shape))
    extra = [] if started is None else [started]
    return pl.pallas_call(
        norm_backward_kernel,
        name="norm_backward",
        grid=(count,),
        out_shape=(jax.ShapeDtypeStruct(x_loc.shape, BF16), jax.ShapeDtypeStruct((2, 8, width), F32)),
        in_specs=[block(0), block(first), block(first), pl.BlockSpec((2, 1, rows, 128), lambda b: (0, b + first, 0, 0)), still(gamma.shape)]
        + [pl.BlockSpec(memory_space=pl.ANY)] * len(extra),
        out_specs=(block(first), still((2, 8, width))),
        input_output_aliases={5: 0} if extra else {},
        compiler_params=pltpu.CompilerParams(vmem_limit_bytes=VMEM_LIMIT),
        cost_estimate=pl.CostEstimate(flops=60 * count * rows * width, bytes_accessed=8 * count * rows * width, transcendentals=0),
    )(grad_h, x_loc, dy_loc, ln_stats, gamma, *extra)


def settle(values):
    block = pl.BlockSpec((1,) + values.shape[1:], lambda b: (b, 0, 0))

    def body(src, dst):
        dst[...] = src[...]

    return pl.pallas_call(
        body, name="settle", grid=(values.shape[0],), out_shape=jax.ShapeDtypeStruct(values.shape, values.dtype), in_specs=[block], out_specs=block,
        cost_estimate=pl.CostEstimate(flops=values.size * 100, bytes_accessed=values.size * 4, transcendentals=0))(values)


def sum_kernel(ring, parts, out, gathered, send, recv):
    me = lax.axis_index("tp")
    barrier = pltpu.get_barrier_semaphore()
    others = [lax.rem(me + k, ring) for k in range(1, ring)]
    for other in others:
        pl.semaphore_signal(barrier, inc=1, device_id={"tp": other}, device_id_type=pl.DeviceIdType.MESH)
    pl.semaphore_wait(barrier, ring - 1)

    def copy(k):
        return pltpu.make_async_remote_copy(
            src_ref=parts, dst_ref=gathered.at[me], send_sem=send.at[k], recv_sem=recv.at[k],
            device_id={"tp": lax.rem(me + k, ring)}, device_id_type=pl.DeviceIdType.MESH)

    for k in range(1, ring):
        copy(k).start()
    gathered[me] = parts[...]
    for k in range(1, ring):
        copy(k).wait_recv()
    total = gathered[0]
    for k in range(1, ring):
        total = total + gathered[k]
    out[...] = total
    for k in range(1, ring):
        copy(k).wait_send()


def sum_over_ring(parts, ring):
    vmem = pl.BlockSpec(memory_space=pltpu.VMEM)
    return pl.pallas_call(
        functools.partial(sum_kernel, ring),
        name="sum_over_ring",
        out_shape=jax.ShapeDtypeStruct(parts.shape, F32),
        in_specs=[vmem],
        out_specs=vmem,
        scratch_shapes=[pltpu.VMEM((ring,) + parts.shape, F32), pltpu.SemaphoreType.DMA((ring,)), pltpu.SemaphoreType.DMA((ring,))],
        compiler_params=pltpu.CompilerParams(collective_id=2, has_side_effects=True),
    )(parts)


def solution(mesh):
    ring = mesh.shape["tp"]

    def device_block(x_loc, ln_gamma, ln_beta, w_q, b_q, w_kv, b_kv, w_o, b_o, dy_loc):
        head_dim = w_kv.shape[1] // 2
        batch, own_rows, width = x_loc.shape
        early = 3 * batch // 8
        normed_full, dy_full, merged, _, grad_q, _, kv_owned, y_loc, _, dh_part, dh_early, bo_rows, ln_stats = attention_block(
            x_loc, dy_loc, ln_gamma[None, :], ln_beta[None, :], w_q, w_kv, b_q[None, :], b_kv[None, :], w_o, b_o[None, :], early, ring, head_dim)
        dh_late = lax.psum_scatter(dh_part, "tp", scatter_dimension=1, tiled=True)
        kv_owned = kv_owned.reshape(ring, batch, own_rows, 2 * head_dim)
        grad_kv = jnp.moveaxis(kv_owned, 0, 1).reshape(batch, ring * own_rows, 2 * head_dim)

        grad_q, merged, y_loc, bo_rows = lax.optimization_barrier((grad_q, merged, y_loc, bo_rows))
        y_loc = settle(y_loc)
        grad_bo = jnp.sum(bo_rows, axis=0)
        grad_wo = jnp.einsum("bse,bsd->ed", merged, dy_full, preferred_element_type=jnp.float32)
        grad_wq = jnp.einsum("bsd,bse->de", normed_full, grad_q, preferred_element_type=jnp.float32)
        grad_bq = jnp.sum(grad_q, axis=(0, 1), dtype=jnp.float32)
        grad_wkv = jnp.einsum("bsd,bsc->dc", normed_full, grad_kv, preferred_element_type=jnp.float32)
        grad_bkv = jnp.sum(grad_kv, axis=(0, 1), dtype=jnp.float32)
        gamma = ln_gamma[None, :]
        started, parts_early = norm_backward(dh_early, x_loc, dy_loc, ln_stats, gamma, 0, None)
        grad_x, parts_late = norm_backward(dh_late, x_loc, dy_loc, ln_stats, gamma, early, started)
        sums = sum_over_ring(jnp.sum(parts_early + parts_late, axis=1).reshape(-1, 128), ring).reshape(2, width)
        return (y_loc, grad_x, sums[0], sums[1], grad_wq, grad_bq, grad_wkv, grad_bkv, grad_wo, grad_bo)

    return jax.shard_map(
        device_block,
        mesh=mesh,
        in_specs=(P("dp", "tp", None), P(None), P(None), P(None, "tp"), P("tp"), P(None, None), P(None), P("tp", None), P(None), P("dp", "tp", None)),
        out_specs=(P("dp", "tp", None), P("dp", "tp", None), P("dp"), P("dp"), P("dp", "tp"), P(("dp", "tp")), P("dp", None), P("dp"), P(("dp", "tp"), None), P("dp")),
        check_vma=False,
    )
```

time: 971 us -> 937 us (0.965)
  Pallas kernels: 798 us -> 764 us
    pallas_call x2 -> x1, Pallas kernels: 762 us -> 728 us  [attention_block(): pl.pallas_call(functools.partial(block_kernel, heads, dim), name='attenti...]
  transfers between devices with their start and end apart: 2 -> 1, of which waited for: 1 -> 1; matrix products, arithmetic and copies ran while one was open for 14% -> 14% of each run, Pallas kernels for 34% -> 2%
where the time goes in v6:
time: 937 us; the launch traced here: 925 us
  Pallas kernels  764 us (82%)
  matrix products  119 us (13%)
  between operations  14.3 us (2%)
  waiting for transfers between devices  13.6 us (1%)
    pallas_call x1, Pallas kernels, attention_block(): pl.pallas_call(functools.partial(block_kernel, heads, dim), name='attenti...  728 us
    dot_general x1, matrix products, device_block(): jnp.einsum('bsd,bse->de', normed_full, grad_q, preferred_element_type=jnp...  48 us
    dot_general x1, matrix products, device_block(): jnp.einsum('bse,bsd->ed', merged, dy_full, preferred_element_type=jnp.flo...  46.6 us
    dot_general x1, matrix products, device_block(): jnp.einsum('bsd,bsc->dc', normed_full, grad_kv, preferred_element_type=jn...  24.3 us
  transfers between devices with their start and end apart: 1, of which 1 were waited for; matrix products, arithmetic and copies ran while one was open for 14% of the time, Pallas kernels for 2%

profile of v6, /device:TPU:112, one launch (start us, length us, event | category | flops | bytes accessed | tf_op | source)
XLA Modules:
  0.0 925.2 jit_solution(5343114838812851255)
XLA Ops:
  7.2 0.1 reduce-scatter.2.cloned.1.call-start
  7.3 1.3 broadcast_in_dim.18.b_q
  8.5 728.5 %attention_block.1 = (bf16[8,512,6144]{2,1,0:T(8,128)(2,1)}, bf16[8,512,6144]{2,1,0:T(8,128)(2,1)}, bf16[8,512,768]{2,1,0:T(8,128)(2,1)}, bf16[8,512,6144]{2,1,0...) custom-call(bf16[8,64,6144]{2,1,0:T(8,128)(2,1)} %x.3, ...), custom_call_target="tpu_custom_call" | custom-call | flops 206158430208 | bytes 301989888 | tf_op jit(solution)/shard_map/attention_block/pallas_call | solution.py:637
  737.0 0.0 copy-start
  737.0 0.0 copy-start.3
  737.0 0.1 reduce-scatter.2.cloned.1.call-update
  737.1 1.5 copy-done
  738.6 1.5 copy.22
  740.0 0.0 copy-done.3
  740.0 0.7 reduce_sum.39
  740.7 7.7 norm_backward.2
  748.4 0.0 copy-start.1
  748.4 8.1 settle.1
  756.4 0.0 copy-done.1
  756.4 0.0 copy-start.2
  756.4 1.1 convert_reduce_fusion.1
  757.5 0.0 slice-start.2
  757.5 4.5 convert_reduce_fusion
  762.1 0.0 copy-done.2
  762.1 24.3 %convolution_bitcast_fusion.2 = f32[6144,256]{1,0:T(8,128)} fusion(bf16[8,512,6144]{2,1,0:T(8,128)(2,1)} %get-tuple-element.40, bf16[8,512,256]{2,1,0:T(8,128)(2,1)S(1)} %bitcast.28), kind=kOutput, calls=%fused_computation.3 | convolution fusion | flops 12884901888 | bytes 58720256 | tf_op jit(solution)/shard_map/bsd,bsc->dc/dot_general | solution.py:780
  786.4 0.0 slice-done.2
  786.4 0.0 slice-done.3
  786.4 46.6 %convolution_bitcast_fusion.1 = f32[768,6144]{1,0:T(8,128)} fusion(bf16[8,512,768]{2,1,0:T(8,128)(2,1)S(1)} %bitcast.36, bf16[8,512,6144]{2,1,0:T(8,128)(2,1)} %get-tuple-element.44), kind=kOutput, calls=%fused_computation.2 | convolution fusion | flops 38654705664 | bytes 75497472 | tf_op jit(solution)/shard_map/bse,bsd->ed/dot_general | solution.py:777
  833.0 0.0 slice-done
  833.0 0.0 slice-done.1
  833.0 48.0 %convolution_bitcast_fusion = f32[6144,768]{1,0:T(8,128)} fusion(bf16[8,512,6144]{2,1,0:T(8,128)(2,1)} %get-tuple-element.40, bf16[8,512,768]{2,1,0:T(8,128)(2,1)S(1)} %bitcast.27), kind=kOutput, calls=%fused_computation.1 | convolution fusion | flops 38654705664 | bytes 75497472 | tf_op jit(solution)/shard_map/bsd,bse->de/dot_general | solution.py:778
  881.0 13.6 %reduce-scatter.2.cloned.1.call-done.dh = bf16[5,64,6144]{2,1,0:T(8,128)(2,1)} async-done(((bf16[5,512,6144]{2,1,0:T(8,128)(2,1)}), bf16[5,64,6144]{2,1,0:T(8,128)(2,1)}) %reduce-scatter.2.cloned.1.call-update) | async-done | bytes 3932176 | tf_op jit(solution)/shard_map/reduce_scatter | solution.py:770
  894.6 10.5 %norm_backward.3 = (bf16[8,64,6144]{2,1,0:T(8,128)(2,1)}, f32[2,8,6144]{2,1,0:T(8,128)}) custom-call(bf16[5,64,6144]{2,1,0:T(8,128)(2,1)} %reduce-scatter.2.cloned.1.call-done.dh, bf16[8,64,6144]{2,1,0:T(8,128)(2,1)} %x.3, bf16[8,64,6144]{2,1,0:T(8,128)(2,1)} %dy.3, f32[2,8,64,128]{3,2,1,0:T(8,128)} %get-tuple-element.34.ln_stats, ...), custom_call_target="tpu_custom_call", output_to_operand_aliasing={{0}: (5, {})} | custom-call | flops 117964800 | bytes 15728640 | tf_op jit(solution)/shard_map/norm_backward/pallas_call | solution.py:697
  905.0 1.3 add_reduce_fusion
  906.3 0.6 reshape.34.parts
  907.0 9.8 %sum_over_ring.1 = f32[96,128]{1,0:T(8,128)} custom-call(f32[96,128]{1,0:T(8,128)} %reshape.34.parts), custom_call_target="tpu_custom_call" | custom-call | tf_op jit(solution)/shard_map/sum_over_ring/pallas_call | solution.py:750
  916.7 1.4 slice_bitcast_fusion
  (5 shorter events, 0.0 us)
Async XLA Ops:
  7.2 887.4 %reduce-scatter.2.cloned.1.call-start = ((), (), s32[]{:S(2)}) async-start(), calls=%async_computation.1 | async-start | bytes 35389440 | tf_op jit(solution)/shard_map/reduce_scatter | solution.py:770
  737.0 1.6 copy-start
  737.0 3.0 copy-start.3
  748.4 8.1 copy-start.1
  756.4 5.7 copy-start.2
  757.5 28.8 %slice-start.2 = ((s8[6291456]{0:T(1024)(128)(4,1)}), s8[4194304]{0:T(1024)(128)(4,1)S(1)}, s32[]{:S(2)}) async-start(s8[6291456]{0:T(1024)(128)(4,1)} %bitcast.35), calls=%async_computation.4 | async-start | bytes 8388608
  762.1 24.3 %slice-start.3 = ((s8[6291456]{0:T(1024)(128)(4,1)}), s8[2097152]{0:T(1024)(128)(4,1)S(1)}, s32[]{:S(2)}) async-start(s8[6291456]{0:T(1024)(128)(4,1)} %bitcast.35), calls=%async_computation.5 | async-start | bytes 4194304
  762.1 70.9 %slice-start = ((s8[6291456]{0:T(1024)(128)(4,1)}), s8[2097152]{0:T(1024)(128)(4,1)S(1)}, s32[]{:S(2)}) async-start(s8[6291456]{0:T(1024)(128)(4,1)} %bitcast.26), calls=%async_computation.2 | async-start | bytes 4194304
  786.4 46.6 %slice-start.1 = ((s8[6291456]{0:T(1024)(128)(4,1)}), s8[4194304]{0:T(1024)(128)(4,1)S(1)}, s32[]{:S(2)}) async-start(s8[6291456]{0:T(1024)(128)(4,1)} %bitcast.26), calls=%async_computation.3 | async-start | bytes 8388608
Sparse Core Ops, SparseCore 0:
  737.2 157.3 reduce-scatter.1

commit v7 on v6

--- a/solution.py
+++ b/solution.py
@@ -84,12 +84,12 @@
 
 
 def block_kernel(heads, dim, x_hbm, dy_hbm, gamma, beta, wq_hbm, wkv_hbm, b_q, b_kv, wo_hbm, b_o,
-                 h_full, dy_full, att_out, o_part, dq_out, dkv_part, dkv_full, y_out, dh_early, dh_late, dh_sum, dbo, ln_stats,
-                 own, w_buf, wo_buf, h_buf, qkv_buf, att_buf, da_buf, dq_buf, dkv_buf, part_buf, total, stats,
+                 h_full, dy_full, att_out, o_part, dq_out, dkv_part, dkv_full, y_out, dh_early, dh_late, dh_theirs, dh_chip, dh_sum, dbo, dbq, ln_stats,
+                 own, bias, w_buf, wo_buf, h_buf, qkv_buf, att_buf, da_buf, dq_buf, dkv_buf, part_buf, total, stats,
                  scores_s, grad_p_s, probs_s, grad_s_s, q_s, att_s, theirs, far_in, near_in, kv_theirs, kv_far_in, kv_near_in,
                  send, recv, x_sem, dy_sem, keep_sem, w_sem, h_sem, att_sem, dq_sem, dkv_sem, part_sem, load_sem,
                  ours_sem, pair_send, pair_recv, far_send, far_recv, near_send, near_recv, free,
-                 kv_ours_sem, kv_pair_send, kv_pair_recv, kv_far_send, kv_far_recv, kv_near_send, kv_near_recv, kv_send, kv_recv, kv_keep_sem):
+                 kv_ours_sem, kv_pair_send, kv_pair_recv, kv_far_send, kv_far_recv, kv_near_send, kv_near_recv, kv_send, kv_recv, kv_keep_sem, late_send, late_recv, late_sem):
     batch, rows, width = x_hbm.shape
     early = dh_early.shape[0]
     half = rows // 2
@@ -219,11 +219,9 @@
         load_block(h_full, b)
 
         def act(at):
-            qkv_buf[:, at] = (jnp.dot(h_buf[...], w_buf[:, at], preferred_element_type=F32) + b_q[:, at]).astype(BF16)
-
-        columns(0, q_width, act, 256)
-        at = pl.ds(q_width, kv_width)
-        qkv_buf[:, at] = (jnp.dot(h_buf[...], w_buf[:, at], preferred_element_type=F32) + b_kv[...]).astype(BF16)
+            qkv_buf[:, at] = (jnp.dot(h_buf[...], w_buf[:, at], preferred_element_type=F32) + bias[:, at]).astype(BF16)
+
+        columns(0, q_width + kv_width, act, 256)
 
     def store_att(b):
         return pltpu.make_async_copy(att_buf, att_out.at[b], att_sem.at[0])
@@ -286,6 +284,11 @@
 
         attend_backward(qkv_buf, da_buf, dq_buf, total, stats, scores_s, grad_p_s, probs_s, grad_s_s, q_s, att_s, heads, dim)
         dkv_buf[...] = total[...].astype(BF16)
+
+        def add(at):
+            dbq[:, at] += jnp.sum(dq_buf[:, at].astype(F32).reshape(-1, 8, 256), axis=0)
+
+        columns(0, q_width, add, 256)
         store_dq(b).start()
         for owner in range(ring):
             store_dkv(b, owner).start()
@@ -442,6 +445,38 @@
         @pl.when(u + 1 < batch)
         def _():
             scatter_x(u + 1).start()
+
+    core = lax.rem(me, 2)
+
+    def late_pair(v, chip):
+        return remote(dh_late.at[v, line(2 * chip + 1 - core)], dh_theirs.at[v, pl.ds(chip * rows, rows)], (late_send.at[v, chip], late_recv.at[v, chip]), partner)
+
+    def late_loads(v):
+        copies = [pltpu.make_async_copy(dh_late.at[v, line(2 * chip + core)], h_buf.at[pl.ds(chip * rows, rows)], late_sem.at[chip]) for chip in range(chips)]
+        return copies + [pltpu.make_async_copy(dh_theirs.at[v], h_buf.at[pl.ds(chips * rows, chips * rows)], late_sem.at[chips])]
+
+    def late_store(v):
+        return pltpu.make_async_copy(h_buf.at[pl.ds(0, chips * rows)], dh_chip.at[v], late_sem.at[chips + 1])
+
+    def late_sum(v):
+        for chip in range(chips):
+            late_pair(v, chip).wait_recv()
+
+        @pl.when(v > 0)
+        def _():
+            late_store(v - 1).wait()
+
+        for copy in late_loads(v):
+            copy.start()
+        for copy in late_loads(v):
+            copy.wait()
+
+        def act(at):
+            mine_, theirs_ = h_buf[: chips * rows, at].astype(F32), h_buf[chips * rows :, at].astype(F32)
+            h_buf[: chips * rows, at] = (mine_ + theirs_).astype(BF16)
+
+        columns(0, width, act)
+        late_store(v).start()
 
     pick = lambda ref, n: ref.at[:, pl.ds(n * kv_width, kv_width)]
     kv_ours = [pick(probs_s, 0), pick(probs_s, 1), pick(probs_s, 2), pick(grad_s_s, 0)]
@@ -552,6 +587,9 @@
     for b in range(1, batch):
         load_dy(b).start()
     dbo[...] = jnp.zeros_like(dbo)
+    dbq[...] = jnp.zeros_like(dbq)
+    bias[:, pl.ds(0, q_width)] = b_q[...].reshape(1, q_width)
+    bias[:, pl.ds(q_width, kv_width)] = b_kv[...].reshape(1, kv_width)
     for copy in weights:
         copy.wait()
 
@@ -582,6 +620,10 @@
         def _():
             relay(t - 2)
 
+        @when(0, scatters)
+        def _():
+            fetch(t)
+
         turn(s - 2, attend_and_project, differentiate)
         unit(s - 1, share_far)
         unit(s - 1, complete)
@@ -591,10 +633,6 @@
         def _():
             finish(t - 3)
 
-        @when(0, scatters)
-        def _():
-            fetch(t)
-
         @when(2, 3)
         def _():
             scatter_x(0).start()
@@ -604,10 +642,23 @@
             def _():
                 act()
 
+        @when(5 + early, 5 + batch)
+        def _():
+            late_sum(t - 5 - early)
+
         @when(4, 4 + batch)
         def _():
             grad_part(t - 4)
 
+        @when(4 + early, 4 + batch)
+        def _():
+            for chip in range(chips):
+                late_pair(t - 4 - early, chip).start()
+
+    late_store(batch - early - 1).wait()
+    for chip in range(chips):
+        for v in range(batch - early):
+            late_pair(v, chip).wait_send()
     store_att(batch - 1).wait()
     store_y(y_out, 0).wait()
     for r in range(chips):
@@ -632,18 +683,19 @@
     dma = pltpu.SemaphoreType.DMA
     full = lambda n, w: jax.ShapeDtypeStruct((n, seq, w), BF16)
     at_home = lambda n: jax.ShapeDtypeStruct((n, rows, width), BF16)
+    half_seq = jax.ShapeDtypeStruct((batch - early, chips * rows, width), BF16)
     owned = jax.ShapeDtypeStruct((ring, batch * rows, kv_width), BF16)
     lo, hi = (lambda *shape: pltpu.VMEM(shape, BF16)), (lambda *shape: pltpu.VMEM(shape, F32))
     return pl.pallas_call(
         functools.partial(block_kernel, heads, dim),
         name="attention_block",
         out_shape=(full(batch, width), full(batch, width), full(batch, q_width), full(batch, width), full(batch, q_width), owned, owned, at_home(batch),
-                   full(early, width), full(batch - early, width), at_home(early),
-                   jax.ShapeDtypeStruct((8, width), F32), jax.ShapeDtypeStruct((2, batch, rows, 128), F32)),
+                   full(early, width), full(batch - early, width), half_seq, half_seq, at_home(early),
+                   jax.ShapeDtypeStruct((8, width), F32), jax.ShapeDtypeStruct((8, q_width), F32), jax.ShapeDtypeStruct((2, batch, rows, 128), F32)),
         in_specs=[hbm, hbm, vmem, vmem, hbm, hbm, vmem, vmem, hbm, vmem],
-        out_specs=(hbm,) * 11 + (vmem, vmem),
+        out_specs=(hbm,) * 13 + (vmem, vmem, vmem),
         scratch_shapes=[
-            lo(units + 2, rows, width), lo(width, qkv_width), lo(q_width, width), lo(seq, width), lo(seq, qkv_width), lo(seq, q_width), lo(seq, q_width),
+            lo(units + 2, rows, width), hi(1, qkv_width), lo(width, qkv_width), lo(q_width, width), lo(seq, width), lo(seq, qkv_width), lo(seq, q_width), lo(seq, q_width),
             lo(seq, q_width), lo(seq, kv_width), lo(2, seq, 512), hi(seq, kv_width), hi(heads, 8, seq),
             hi(seq, q_width), hi(seq, q_width), lo(seq, q_width), lo(seq, q_width), lo(q_width, dim), lo(q_width, dim),
             lo(chips, rows, width), lo(3, rows, width), lo(3, 2, rows, width),
@@ -651,14 +703,15 @@
             dma((8, units)), dma((8, units)), dma((2,)), dma((batch,)), dma((units,)), dma((3,)), dma((1,)), dma((1,)), dma((1,)), dma((ring,)), dma((2,)),
             dma((ring + 3,)),
             dma((chips,)), dma((chips,)), dma((chips,)), dma((2, 2)), dma((3, 2)), dma((3, 2)), dma((3, 2)), pltpu.SemaphoreType.REGULAR,
-            dma((chips,)), dma((chips,)), dma((chips,)), dma((2,)), dma((2,)), dma((2,)), dma((2,)), dma((8,)), dma((8,)), dma((1,))],
+            dma((chips,)), dma((chips,)), dma((chips,)), dma((2,)), dma((2,)), dma((2,)), dma((2,)), dma((8,)), dma((8,)), dma((1,)),
+            dma((batch - early, chips)), dma((batch - early, chips)), dma((chips + 2,))],
         compiler_params=pltpu.CompilerParams(collective_id=0, has_side_effects=True, vmem_limit_bytes=VMEM_LIMIT),
         cost_estimate=pl.CostEstimate(flops=8 * batch * seq * width * qkv_width, bytes_accessed=12 * batch * seq * width, transcendentals=0),
     )(x_loc, dy_loc, gamma, beta, w_q, w_kv, b_q, b_kv, w_o, b_o)
 
 
 def norm_backward_kernel(dh, x, dy, ln_stats, gamma, *refs):
-    dx, sums = refs[-2:]
+    dx, sums, x_hat_s, scaled_s = refs[-4:]
     rows, width = x.shape[1:]
     tile = 512
 
@@ -667,24 +720,30 @@
         sums[...] = jnp.zeros_like(sums)
 
     mean, inv_std = ln_stats[0, 0, :, :1], ln_stats[1, 0, :, :1]
-    by_lane = lambda v: sum(v[:, n : n + 128] for n in range(0, tile, 128))
+    by_lane = lambda v: v[:, :128] + v[:, 128:256] + v[:, 256:384] + v[:, 384:]
     by_sublane = lambda v: jnp.sum(v.reshape(-1, 8, tile), axis=0)
-    plain = along = jnp.zeros((rows, 128), F32)
-    for n in range(0, width, tile):
-        at = slice(n, n + tile)
+
+    def gather_sums(n, carry):
+        plain, along = carry
+        at = pl.ds(pl.multiple_of(n * tile, tile), tile)
         grad_h = dh[0, :, at].astype(F32)
         x_hat = (x[0, :, at].astype(F32) - mean) * inv_std
-        both = grad_h * x_hat
-        plain = plain + by_lane(grad_h * gamma[:, at])
-        along = along + by_lane(both * gamma[:, at])
-        sums[0, :, at] += by_sublane(both)
+        scaled = grad_h * gamma[:, at]
+        x_hat_s[:, at] = x_hat
+        scaled_s[:, at] = scaled
+        sums[0, :, at] += by_sublane(grad_h * x_hat)
         sums[1, :, at] += by_sublane(grad_h)
+        return plain + by_lane(scaled), along + by_lane(scaled * x_hat)
+
+    zero = jnp.zeros((rows, 128), F32)
+    plain, along = lax.fori_loop(0, width // tile, gather_sums, (zero, zero), unroll=2)
     plain = jnp.sum(plain, axis=-1, keepdims=True) / width
     along = jnp.sum(along, axis=-1, keepdims=True) / width
-    for n in range(0, width, tile):
-        at = slice(n, n + tile)
-        x_hat = (x[0, :, at].astype(F32) - mean) * inv_std
-        grad_in = inv_std * (dh[0, :, at].astype(F32) * gamma[:, at] - plain - x_hat * along)
+
+    @pl.loop(0, width // tile, unroll=2)
+    def _(n):
+        at = pl.ds(pl.multiple_of(n * tile, tile), tile)
+        grad_in = inv_std * (scaled_s[:, at] - plain - x_hat_s[:, at] * along)
         dx[0, :, at] = (dy[0, :, at].astype(F32) + grad_in).astype(BF16)
 
 
@@ -702,6 +761,7 @@
         in_specs=[block(0), block(first), block(first), pl.BlockSpec((2, 1, rows, 128), lambda b: (0, b + first, 0, 0)), still(gamma.shape)]
         + [pl.BlockSpec(memory_space=pl.ANY)] * len(extra),
         out_specs=(block(first), still((2, 8, width))),
+        scratch_shapes=[pltpu.VMEM((rows, width), F32), pltpu.VMEM((rows, width), F32)],
         input_output_aliases={5: 0} if extra else {},
         compiler_params=pltpu.CompilerParams(vmem_limit_bytes=VMEM_LIMIT),
         cost_estimate=pl.CostEstimate(flops=60 * count * rows * width, bytes_accessed=8 * count * rows * width, transcendentals=0),
@@ -709,22 +769,28 @@
 
 
 def settle(values):
-    block = pl.BlockSpec((1,) + values.shape[1:], lambda b: (b, 0, 0))
+    block = pl.BlockSpec((2,) + values.shape[1:], lambda b: (b, 0, 0))
 
     def body(src, dst):
         dst[...] = src[...]
 
     return pl.pallas_call(
-        body, name="settle", grid=(values.shape[0],), out_shape=jax.ShapeDtypeStruct(values.shape, values.dtype), in_specs=[block], out_specs=block,
+        body, name="settle", grid=(values.shape[0] // 2,), out_shape=jax.ShapeDtypeStruct(values.shape, values.dtype), in_specs=[block], out_specs=block,
+        compiler_params=pltpu.CompilerParams(vmem_limit_bytes=VMEM_LIMIT),
         cost_estimate=pl.CostEstimate(flops=values.size * 100, bytes_accessed=values.size * 4, transcendentals=0))(values)
 
 
-def sum_kernel(ring, parts, out, gathered, send, recv):
+def sum_kernel(ring, first, second, out, parts, gathered, send, recv):
     me = lax.axis_index("tp")
     barrier = pltpu.get_barrier_semaphore()
     others = [lax.rem(me + k, ring) for k in range(1, ring)]
     for other in others:
         pl.semaphore_signal(barrier, inc=1, device_id={"tp": other}, device_id_type=pl.DeviceIdType.MESH)
+    groups = first.shape[2] // 128
+    for kind in range(2):
+        row = jnp.sum(first[kind] + second[kind], axis=0, keepdims=True)
+        for n in range(groups):
+            parts[kind * groups + n : kind * groups + n + 1, :] = row[:, n * 128 : (n + 1) * 128]
     pl.semaphore_wait(barrier, ring - 1)
 
     def copy(k):
@@ -745,17 +811,18 @@
         copy(k).wait_send()
 
 
-def sum_over_ring(parts, ring):
+def sum_over_ring(first, second, ring):
     vmem = pl.BlockSpec(memory_space=pltpu.VMEM)
+    shape = (2 * first.shape[2] // 128, 128)
     return pl.pallas_call(
         functools.partial(sum_kernel, ring),
         name="sum_over_ring",
-        out_shape=jax.ShapeDtypeStruct(parts.shape, F32),
-        in_specs=[vmem],
+        out_shape=jax.ShapeDtypeStruct(shape, F32),
+        in_specs=[vmem, vmem],
         out_specs=vmem,
-        scratch_shapes=[pltpu.VMEM((ring,) + parts.shape, F32), pltpu.SemaphoreType.DMA((ring,)), pltpu.SemaphoreType.DMA((ring,))],
+        scratch_shapes=[pltpu.VMEM(shape, F32), pltpu.VMEM((ring,) + shape, F32), pltpu.SemaphoreType.DMA((ring,)), pltpu.SemaphoreType.DMA((ring,))],
         compiler_params=pltpu.CompilerParams(collective_id=2, has_side_effects=True),
-    )(parts)
+    )(first, second)
 
 
 def solution(mesh):
@@ -765,24 +832,25 @@
         head_dim = w_kv.shape[1] // 2
         batch, own_rows, width = x_loc.shape
         early = 3 * batch // 8
-        normed_full, dy_full, merged, _, grad_q, _, kv_owned, y_loc, _, dh_part, dh_early, bo_rows, ln_stats = attention_block(
-            x_loc, dy_loc, ln_gamma[None, :], ln_beta[None, :], w_q, w_kv, b_q[None, :], b_kv[None, :], w_o, b_o[None, :], early, ring, head_dim)
-        dh_late = lax.psum_scatter(dh_part, "tp", scatter_dimension=1, tiled=True)
+        normed_full, dy_full, merged, _, grad_q, _, kv_owned, y_loc, _, _, _, dh_chip, dh_early, bo_rows, bq_rows, ln_stats = attention_block(
+            x_loc, dy_loc, ln_gamma[None, :], ln_beta[None, :], w_q, w_kv, b_q, b_kv, w_o, b_o[None, :], early, ring, head_dim)
+        lines = [[i for i in range(ring) if i % 2 == core] for core in range(2)]
+        dh_late = lax.psum_scatter(dh_chip, "tp", scatter_dimension=1, tiled=True, axis_index_groups=lines)
         kv_owned = kv_owned.reshape(ring, batch, own_rows, 2 * head_dim)
         grad_kv = jnp.moveaxis(kv_owned, 0, 1).reshape(batch, ring * own_rows, 2 * head_dim)
 
-        grad_q, merged, y_loc, bo_rows = lax.optimization_barrier((grad_q, merged, y_loc, bo_rows))
+        grad_q, merged, y_loc = lax.optimization_barrier((grad_q, merged, y_loc))
         y_loc = settle(y_loc)
         grad_bo = jnp.sum(bo_rows, axis=0)
         grad_wo = jnp.einsum("bse,bsd->ed", merged, dy_full, preferred_element_type=jnp.float32)
         grad_wq = jnp.einsum("bsd,bse->de", normed_full, grad_q, preferred_element_type=jnp.float32)
-        grad_bq = jnp.sum(grad_q, axis=(0, 1), dtype=jnp.float32)
+        grad_bq = jnp.sum(bq_rows, axis=0)
         grad_wkv = jnp.einsum("bsd,bsc->dc", normed_full, grad_kv, preferred_element_type=jnp.float32)
         grad_bkv = jnp.sum(grad_kv, axis=(0, 1), dtype=jnp.float32)
         gamma = ln_gamma[None, :]
         started, parts_early = norm_backward(dh_early, x_loc, dy_loc, ln_stats, gamma, 0, None)
         grad_x, parts_late = norm_backward(dh_late, x_loc, dy_loc, ln_stats, gamma, early, started)
-        sums = sum_over_ring(jnp.sum(parts_early + parts_late, axis=1).reshape(-1, 128), ring).reshape(2, width)
+        sums = sum_over_ring(parts_early, parts_late, ring).reshape(2, width)
         return (y_loc, grad_x, sums[0], sums[1], grad_wq, grad_bq, grad_wkv, grad_bkv, grad_wo, grad_bo)
 
     return jax.shard_map(

time: 937 us -> 898 us (0.958); the launches traced: 925 us -> 896 us
  waiting for transfers between devices: 13.6 us -> 0.06 us
  Pallas kernels: 764 us -> 753 us
    reduce_scatter x1, waiting for transfers between devices: 13.6 us -> 0.01 us  [device_block(): lax.psum_scatter(dh_chip, 'tp', scatter_dimension=1, tiled=True, axis_ind...]
    pallas_call x1, Pallas kernels: 728 us -> 716 us  [attention_block(): pl.pallas_call(functools.partial(block_kernel, heads, dim), name='attenti...]
  transfers between devices with their start and end apart: 1 -> 1, of which waited for: 1 -> 0; matrix products, arithmetic and copies ran while one was open for 14% -> 14% of each run, Pallas kernels for 2% -> 2%
where the time goes in v7:
time: 898 us; the launch traced here: 896 us
  Pallas kernels  753 us (84%)
  matrix products  121 us (13%)
  between operations  14.1 us (2%)
    pallas_call x1, Pallas kernels, attention_block(): pl.pallas_call(functools.partial(block_kernel, heads, dim), name='attenti...  716 us
    dot_general x1, matrix products, device_block(): jnp.einsum('bsd,bse->de', normed_full, grad_q, preferred_element_type=jnp...  49.1 us
    dot_general x1, matrix products, device_block(): jnp.einsum('bse,bsd->ed', merged, dy_full, preferred_element_type=jnp.flo...  46.4 us
    dot_general x1, matrix products, device_block(): jnp.einsum('bsd,bsc->dc', normed_full, grad_kv, preferred_element_type=jn...  25.4 us
    pallas_call x2, Pallas kernels, norm_backward(): pl.pallas_call(norm_backward_kernel, name='norm_backward', grid=(count,),...  19.1 us
  transfers between devices with their start and end apart: 1, of which 0 were waited for; matrix products, arithmetic and copies ran while one was open for 14% of the time, Pallas kernels for 2%

profile of v7, /device:TPU:112, one launch (start us, length us, event | category | flops | bytes accessed | tf_op | source)
XLA Modules:
  0.0 896.1 jit_solution(4652534474458493669)
XLA Ops:
  7.2 0.1 reduce-scatter.2.cloned.1.call-start
  7.3 715.6 %attention_block.1 = (bf16[8,512,6144]{2,1,0:T(8,128)(2,1)}, bf16[8,512,6144]{2,1,0:T(8,128)(2,1)}, bf16[8,512,768]{2,1,0:T(8,128)(2,1)}, bf16[8,512,6144]{2,1,0...) custom-call(bf16[8,64,6144]{2,1,0:T(8,128)(2,1)} %x.3, ...), custom_call_target="tpu_custom_call" | custom-call | flops 206158430208 | bytes 301989888 | tf_op jit(solution)/shard_map/attention_block/pallas_call | solution.py:689
  722.9 0.0 copy-start
  722.9 0.0 copy-start.2
  722.9 0.0 copy-start.1
  722.9 0.1 reduce-scatter.2.cloned.1.call-update
  723.0 1.5 copy-done
  724.5 1.5 copy.22
  725.9 0.0 copy-done.2
  725.9 0.6 reduce_sum.27
  726.5 0.0 copy-done.1
  726.5 0.7 reduce_sum.29
  727.2 7.8 norm_backward.2
  735.0 5.9 settle.1
  740.9 0.0 slice-start
  740.9 2.9 convert_reduce_fusion
  743.8 0.0 slice-start.1
  743.8 25.4 %convolution_bitcast_fusion.2 = f32[6144,256]{1,0:T(8,128)} fusion(bf16[8,512,6144]{2,1,0:T(8,128)(2,1)} %get-tuple-element.39, bf16[8,512,256]{2,1,0:T(8,128)(2,1)} %bitcast.25), kind=kOutput, calls=%fused_computation.2 | convolution fusion | flops 12884901888 | bytes 58720256 | tf_op jit(solution)/shard_map/bsd,bsc->dc/dot_general | solution.py:848
  769.1 0.0 slice-done
  769.1 0.0 slice-done.1
  769.1 46.4 %convolution_bitcast_fusion.1 = f32[768,6144]{1,0:T(8,128)} fusion(bf16[8,512,768]{2,1,0:T(8,128)(2,1)S(1)} %bitcast.32, bf16[8,512,6144]{2,1,0:T(8,128)(2,1)} %get-tuple-element.44), kind=kOutput, calls=%fused_computation.1 | convolution fusion | flops 38654705664 | bytes 75497472 | tf_op jit(solution)/shard_map/bse,bsd->ed/dot_general | solution.py:845
  815.5 49.1 %convolution_bitcast_fusion = f32[6144,768]{1,0:T(8,128)} fusion(bf16[8,512,6144]{2,1,0:T(8,128)(2,1)} %get-tuple-element.39, bf16[8,512,768]{2,1,0:T(8,128)(2,1)} %get-tuple-element.40), kind=kOutput, calls=%fused_computation | convolution fusion | flops 38654705664 | bytes 75497472 | tf_op jit(solution)/shard_map/bsd,bse->de/dot_general | solution.py:846
  864.5 0.0 reduce-scatter.2.cloned.1.call-done.dh
  864.5 11.3 %norm_backward.3 = (bf16[8,64,6144]{2,1,0:T(8,128)(2,1)}, f32[2,8,6144]{2,1,0:T(8,128)}) custom-call(bf16[5,64,6144]{2,1,0:T(8,128)(2,1)} %reduce-scatter.2.cloned.1.call-done.dh, bf16[8,64,6144]{2,1,0:T(8,128)(2,1)} %x.3, bf16[8,64,6144]{2,1,0:T(8,128)(2,1)} %dy.3, f32[2,8,64,128]{3,2,1,0:T(8,128)} %get-tuple-element.33.ln_stats, ...), custom_call_target="tpu_custom_call", output_to_operand_aliasing={{0}: (5, {})} | custom-call | flops 117964800 | bytes 15728640 | tf_op jit(solution)/shard_map/norm_backward/pallas_call | solution.py:756
  875.8 12.1 %sum_over_ring.1 = f32[96,128]{1,0:T(8,128)} custom-call(f32[2,8,6144]{2,1,0:T(8,128)} %get-tuple-element.37.first, f32[2,8,6144]{2,1,0:T(8,128)} %get-tuple-element.38.second), custom_call_target="tpu_custom_call" | custom-call | tf_op jit(solution)/shard_map/sum_over_ring/pallas_call | solution.py:817
  887.9 1.4 slice_bitcast_fusion
  (1 shorter events, 0.0 us)
Async XLA Ops:
  7.2 857.3 %reduce-scatter.2.cloned.1.call-start = ((), (), s32[]{:S(2)}) async-start(), calls=%async_computation.1 | async-start | bytes 19660800 | tf_op jit(solution)/shard_map/reduce_scatter | solution.py:838
  722.9 1.6 copy-start
  722.9 3.0 copy-start.2
  722.9 3.6 copy-start.1
  740.9 28.2 %slice-start = ((s8[6291456]{0:T(1024)(128)(4,1)}), s8[4194304]{0:T(1024)(128)(4,1)S(1)}, s32[]{:S(2)}) async-start(s8[6291456]{0:T(1024)(128)(4,1)} %bitcast.31), calls=%async_computation.2 | async-start | bytes 8388608
  743.8 25.4 %slice-start.1 = ((s8[6291456]{0:T(1024)(128)(4,1)}), s8[2097152]{0:T(1024)(128)(4,1)S(1)}, s32[]{:S(2)}) async-start(s8[6291456]{0:T(1024)(128)(4,1)} %bitcast.31), calls=%async_computation.3 | async-start | bytes 4194304
Sparse Core Ops, SparseCore 0:
  723.1 137.4 reduce-scatter.1

commit v8 on v7

--- a/solution.py
+++ b/solution.py
@@ -84,14 +84,14 @@
 
 
 def block_kernel(heads, dim, x_hbm, dy_hbm, gamma, beta, wq_hbm, wkv_hbm, b_q, b_kv, wo_hbm, b_o,
-                 h_full, dy_full, att_out, o_part, dq_out, dkv_part, dkv_full, y_out, dh_early, dh_late, dh_theirs, dh_chip, dh_sum, dbo, dbq, ln_stats,
+                 h_full, dy_full, att_out, o_part, dq_out, dkv_part, dkv_full, y_out, dh_part, o_theirs, o_chip, dh_sum, dbo, dbq, ln_stats,
                  own, bias, w_buf, wo_buf, h_buf, qkv_buf, att_buf, da_buf, dq_buf, dkv_buf, part_buf, total, stats,
                  scores_s, grad_p_s, probs_s, grad_s_s, q_s, att_s, theirs, far_in, near_in, kv_theirs, kv_far_in, kv_near_in,
                  send, recv, x_sem, dy_sem, keep_sem, w_sem, h_sem, att_sem, dq_sem, dkv_sem, part_sem, load_sem,
                  ours_sem, pair_send, pair_recv, far_send, far_recv, near_send, near_recv, free,
                  kv_ours_sem, kv_pair_send, kv_pair_recv, kv_far_send, kv_far_recv, kv_near_send, kv_near_recv, kv_send, kv_recv, kv_keep_sem, late_send, late_recv, late_sem):
     batch, rows, width = x_hbm.shape
-    early = dh_early.shape[0]
+    early = y_out.shape[0]
     half = rows // 2
     wide = width // 2
     units = 2 * batch
@@ -294,37 +294,23 @@
             store_dkv(b, owner).start()
 
     def grad_part(b):
-        copies = [pltpu.make_async_copy(dq_out.at[b], qkv_buf.at[:, pl.ds(0, q_width)], load_sem.at[ring])]
-        for owner in range(ring):
-            copies.append(pltpu.make_async_copy(dkv_part.at[owner, pl.ds(pl.multiple_of(b * rows, rows), rows)],
-                                                qkv_buf.at[pl.ds(owner * rows, rows), pl.ds(q_width, kv_width)], load_sem.at[owner]))
-        for copy in copies:
-            copy.start()
-        for copy in copies:
-            copy.wait()
-
-        def store(n):
-            @pl.when(b < early)
-            def _():
-                store_part(dh_early, b, n).start()
-
-            @pl.when(b >= early)
-            def _():
-                store_part(dh_late, b - early, n).start()
-
-        make_part(lambda at: lax.dot_general(qkv_buf[...], w_buf[at, :], ACROSS, preferred_element_type=F32), store)
+        def product(at):
+            from_q = lax.dot_general(dq_buf[...], w_buf[at, :q_width], ACROSS, preferred_element_type=F32)
+            return from_q + lax.dot_general(dkv_buf[...], w_buf[at, q_width:], ACROSS, preferred_element_type=F32)
+
+        make_part(product, lambda n: store_part(dh_part, b, n).start())
 
     def line(owner):
         return pl.ds(pl.multiple_of(owner * rows, rows), rows)
 
     def sourced(u, act):
-        @pl.when(u < batch)
+        @pl.when(u < early)
         def _():
             act(o_part.at[u])
 
-        @pl.when(u >= batch)
-        def _():
-            act(dh_early.at[u - batch])
+        @pl.when(u >= early)
+        def _():
+            act(dh_part.at[u - early])
 
     def mine(part, r):
         return pltpu.make_async_copy(part.at[line(lax.rem(me + 2 * r, ring))], own.at[OURS + r], ours_sem.at[r])
@@ -424,7 +410,7 @@
         def whole(at):
             return own[SUM + slot, :, at].astype(F32) + near_in[slot, 0, :, at].astype(F32) + near_in[slot, 1, :, at].astype(F32)
 
-        @pl.when(u < batch)
+        @pl.when(u < early)
         def _():
             scatter_x(u).wait()
 
@@ -434,29 +420,29 @@
             columns(0, width, act)
             store_y(y_out, u).start()
 
-        @pl.when(u >= batch)
+        @pl.when(u >= early)
         def _():
             def act(at):
                 own[Y, :, at] = whole(at).astype(BF16)
 
             columns(0, width, act)
-            store_y(dh_sum, u - batch).start()
-
-        @pl.when(u + 1 < batch)
+            store_y(dh_sum, u - early).start()
+
+        @pl.when(u + 1 < early)
         def _():
             scatter_x(u + 1).start()
 
     core = lax.rem(me, 2)
 
     def late_pair(v, chip):
-        return remote(dh_late.at[v, line(2 * chip + 1 - core)], dh_theirs.at[v, pl.ds(chip * rows, rows)], (late_send.at[v, chip], late_recv.at[v, chip]), partner)
+        return remote(o_part.at[early + v, line(2 * chip + 1 - core)], o_theirs.at[v, pl.ds(chip * rows, rows)], (late_send.at[v, chip], late_recv.at[v, chip]), partner)
 
     def late_loads(v):
-        copies = [pltpu.make_async_copy(dh_late.at[v, line(2 * chip + core)], h_buf.at[pl.ds(chip * rows, rows)], late_sem.at[chip]) for chip in range(chips)]
-        return copies + [pltpu.make_async_copy(dh_theirs.at[v], h_buf.at[pl.ds(chips * rows, chips * rows)], late_sem.at[chips])]
+        copies = [pltpu.make_async_copy(o_part.at[early + v, line(2 * chip + core)], h_buf.at[pl.ds(chip * rows, rows)], late_sem.at[chip]) for chip in range(chips)]
+        return copies + [pltpu.make_async_copy(o_theirs.at[v], h_buf.at[pl.ds(chips * rows, chips * rows)], late_sem.at[chips])]
 
     def late_store(v):
-        return pltpu.make_async_copy(h_buf.at[pl.ds(0, chips * rows)], dh_chip.at[v], late_sem.at[chips + 1])
+        return pltpu.make_async_copy(h_buf.at[pl.ds(0, chips * rows)], o_chip.at[v], late_sem.at[chips + 1])
 
     def late_sum(v):
         for chip in range(chips):
@@ -624,7 +610,18 @@
         def _():
             fetch(t)
 
+        @when(3, 5)
+        def _():
+            grad_part(batch - 5 + t)
+
         turn(s - 2, attend_and_project, differentiate)
+
+        @pl.when(jnp.logical_and(s < units - 1, lax.rem(s, 2) == 1))
+        def _():
+            @pl.when(s >= 3)
+            def _():
+                grad_part(lax.div(s - 3, 2))
+
         unit(s - 1, share_far)
         unit(s - 1, complete)
         turn(s - 1, project, grad_attended)
@@ -642,18 +639,14 @@
             def _():
                 act()
 
-        @when(5 + early, 5 + batch)
-        def _():
-            late_sum(t - 5 - early)
-
-        @when(4, 4 + batch)
-        def _():
-            grad_part(t - 4)
-
-        @when(4 + early, 4 + batch)
+        @when(6, 6 + batch - early)
+        def _():
+            late_sum(t - 6)
+
+        @when(5, 5 + batch - early)
         def _():
             for chip in range(chips):
-                late_pair(t - 4 - early, chip).start()
+                late_pair(t - 5, chip).start()
 
     late_store(batch - early - 1).wait()
     for chip in range(chips):
@@ -689,11 +682,11 @@
     return pl.pallas_call(
         functools.partial(block_kernel, heads, dim),
         name="attention_block",
-        out_shape=(full(batch, width), full(batch, width), full(batch, q_width), full(batch, width), full(batch, q_width), owned, owned, at_home(batch),
-                   full(early, width), full(batch - early, width), half_seq, half_seq, at_home(early),
+        out_shape=(full(batch, width), full(batch, width), full(batch, q_width), full(batch, width), full(batch, q_width), owned, owned, at_home(early),
+                   full(batch, width), half_seq, half_seq, at_home(batch),
                    jax.ShapeDtypeStruct((8, width), F32), jax.ShapeDtypeStruct((8, q_width), F32), jax.ShapeDtypeStruct((2, batch, rows, 128), F32)),
         in_specs=[hbm, hbm, vmem, vmem, hbm, hbm, vmem, vmem, hbm, vmem],
-        out_specs=(hbm,) * 13 + (vmem, vmem, vmem),
+        out_specs=(hbm,) * 12 + (vmem, vmem, vmem),
         scratch_shapes=[
             lo(units + 2, rows, width), hi(1, qkv_width), lo(width, qkv_width), lo(q_width, width), lo(seq, width), lo(seq, qkv_width), lo(seq, q_width), lo(seq, q_width),
             lo(seq, q_width), lo(seq, kv_width), lo(2, seq, 512), hi(seq, kv_width), hi(heads, 8, seq),
@@ -710,8 +703,7 @@
     )(x_loc, dy_loc, gamma, beta, w_q, w_kv, b_q, b_kv, w_o, b_o)
 
 
-def norm_backward_kernel(dh, x, dy, ln_stats, gamma, *refs):
-    dx, sums, x_hat_s, scaled_s = refs[-4:]
+def norm_backward_kernel(dh, x, dy, ln_stats, gamma, dx, sums, x_hat_s, scaled_s):
     rows, width = x.shape[1:]
     tile = 512
 
@@ -747,48 +739,150 @@
         dx[0, :, at] = (dy[0, :, at].astype(F32) + grad_in).astype(BF16)
 
 
-def norm_backward(grad_h, x_loc, dy_loc, ln_stats, gamma, first, started):
-    rows, width = x_loc.shape[1:]
-    count = grad_h.shape[0]
-    block = lambda skip: pl.BlockSpec((1, rows, width), lambda b: (b + skip, 0, 0))
+def norm_backward(grad_h, x_loc, dy_loc, ln_stats, gamma):
+    batch, rows, width = x_loc.shape
+    block = pl.BlockSpec((1, rows, width), lambda b: (b, 0, 0))
     still = lambda shape: pl.BlockSpec(shape, lambda b: (0,) * len(shape))
-    extra = [] if started is None else [started]
     return pl.pallas_call(
         norm_backward_kernel,
         name="norm_backward",
-        grid=(count,),
+        grid=(batch,),
         out_shape=(jax.ShapeDtypeStruct(x_loc.shape, BF16), jax.ShapeDtypeStruct((2, 8, width), F32)),
-        in_specs=[block(0), block(first), block(first), pl.BlockSpec((2, 1, rows, 128), lambda b: (0, b + first, 0, 0)), still(gamma.shape)]
-        + [pl.BlockSpec(memory_space=pl.ANY)] * len(extra),
-        out_specs=(block(first), still((2, 8, width))),
+        in_specs=[block, block, block, pl.BlockSpec((2, 1, rows, 128), lambda b: (0, b, 0, 0)), still(gamma.shape)],
+        out_specs=(block, still((2, 8, width))),
         scratch_shapes=[pltpu.VMEM((rows, width), F32), pltpu.VMEM((rows, width), F32)],
-        input_output_aliases={5: 0} if extra else {},
         compiler_params=pltpu.CompilerParams(vmem_limit_bytes=VMEM_LIMIT),
-        cost_estimate=pl.CostEstimate(flops=60 * count * rows * width, bytes_accessed=8 * count * rows * width, transcendentals=0),
-    )(grad_h, x_loc, dy_loc, ln_stats, gamma, *extra)
-
-
-def settle(values):
-    block = pl.BlockSpec((2,) + values.shape[1:], lambda b: (b, 0, 0))
+        cost_estimate=pl.CostEstimate(flops=60 * batch * rows * width, bytes_accessed=8 * batch * rows * width, transcendentals=0),
+    )(grad_h, x_loc, dy_loc, ln_stats, gamma)
+
+
+def turn_rows(rows, dst, place):
+    count, cols = rows.shape
+    chunk = 512
+
+    @pl.loop(0, count, step=chunk)
+    def _(k):
+        at = pl.ds(pl.multiple_of(k, chunk), chunk)
+        dst[place : place + cols, at] = rows[at, :].T
+
+
+def grad_wo_kernel(att, dy, out, turned):
+    @pl.when(pl.program_id(0) == 0)
+    def _():
+        turn_rows(att, turned, 0)
+
+    @pl.loop(0, out.shape[1], step=256)
+    def _(n):
+        at = pl.ds(pl.multiple_of(n, 256), 256)
+        out[:, at] = jnp.dot(turned[...], dy[:, at], preferred_element_type=F32)
+
+
+def whole(shape):
+    return pl.BlockSpec(shape, lambda n: (0,) * len(shape), pipeline_mode=pl.Buffered(1))
+
+
+def grad_wo(att, dy):
+    tokens, q_width = att.shape
+    width = dy.shape[1]
+    tile = 512
+    return pl.pallas_call(
+        grad_wo_kernel,
+        name="grad_wo",
+        grid=(width // tile,),
+        out_shape=jax.ShapeDtypeStruct((q_width, width), F32),
+        in_specs=[whole(att.shape), pl.BlockSpec((tokens, tile), lambda n: (0, n))],
+        out_specs=pl.BlockSpec((q_width, tile), lambda n: (0, n)),
+        scratch_shapes=[pltpu.VMEM((q_width, tokens), BF16)],
+        compiler_params=pltpu.CompilerParams(vmem_limit_bytes=VMEM_LIMIT),
+        cost_estimate=pl.CostEstimate(flops=2 * tokens * q_width * width, bytes_accessed=2 * tokens * width + 4 * q_width * width, transcendentals=0),
+    )(att, dy)
+
+
+def grad_wq_kernel(rows, grad_q, kv_owned, h, out_q, out_kv, kv_sums, turned, kv_lines):
+    tokens, q_width = grad_q.shape
+    ring, owned, kv_width = kv_owned.shape
+    first = q_width - kv_width
+
+    @pl.when(pl.program_id(0) == 0)
+    def _():
+        turn_rows(grad_q, turned, 0)
+
+        @pl.loop(0, owned, step=rows)
+        def _(r):
+            for owner in range(ring):
+                place = pl.multiple_of(r * ring + owner * rows, rows)
+                kv_lines[pl.ds(place, rows), :] = kv_owned[owner, pl.ds(pl.multiple_of(r, rows), rows), :]
+
+        turn_rows(kv_lines, turned, q_width)
+        kv_sums[...] = jnp.zeros_like(kv_sums)
+
+        @pl.loop(0, tokens, step=512)
+        def _(k):
+            kv_sums[...] += jnp.sum(kv_lines[pl.ds(pl.multiple_of(k, 512), 512), :].astype(F32).reshape(-1, 8, kv_width), axis=0)
+
+    @pl.loop(0, out_q.shape[0], step=256)
+    def _(n):
+        at = pl.ds(pl.multiple_of(n, 256), 256)
+        out_q[at, :first] = jnp.dot(turned[:first, :], h[:, at], preferred_element_type=F32).T
+        late = jnp.dot(turned[first:, :], h[:, at], preferred_element_type=F32).T
+        out_q[at, first:] = late[:, :kv_width]
+        out_kv[at, :] = late[:, kv_width:]
+
+
+def grad_wq(grad_q, kv_owned, h, rows):
+    tokens, q_width = grad_q.shape
+    kv_width = kv_owned.shape[2]
+    width = h.shape[1]
+    tile = 512
+    return pl.pallas_call(
+        functools.partial(grad_wq_kernel, rows),
+        name="grad_wq",
+        grid=(width // tile,),
+        out_shape=(jax.ShapeDtypeStruct((width, q_width), F32), jax.ShapeDtypeStruct((width, kv_width), F32), jax.ShapeDtypeStruct((8, kv_width), F32)),
+        in_specs=[whole(grad_q.shape), whole(kv_owned.shape), pl.BlockSpec((tokens, tile), lambda n: (0, n))],
+        out_specs=(pl.BlockSpec((tile, q_width), lambda n: (n, 0)), pl.BlockSpec((tile, kv_width), lambda n: (n, 0)), pl.BlockSpec((8, kv_width), lambda n: (0, 0))),
+        scratch_shapes=[pltpu.VMEM((q_width + kv_width, tokens), BF16), pltpu.VMEM((tokens, kv_width), BF16)],
+        compiler_params=pltpu.CompilerParams(vmem_limit_bytes=VMEM_LIMIT),
+        cost_estimate=pl.CostEstimate(flops=2 * tokens * (q_width + kv_width) * width, bytes_accessed=2 * tokens * width + 4 * (q_width + kv_width) * width, transcendentals=0),
+    )(grad_q, kv_owned, h)
+
+
+def settle(values, count):
+    block = pl.BlockSpec((1,) + values.shape[1:], lambda b: (b, 0, 0))
 
     def body(src, dst):
         dst[...] = src[...]
 
     return pl.pallas_call(
-        body, name="settle", grid=(values.shape[0] // 2,), out_shape=jax.ShapeDtypeStruct(values.shape, values.dtype), in_specs=[block], out_specs=block,
+        body, name="settle", grid=(values.shape[0],), out_shape=jax.ShapeDtypeStruct((count,) + values.shape[1:], values.dtype), in_specs=[block], out_specs=block,
         compiler_params=pltpu.CompilerParams(vmem_limit_bytes=VMEM_LIMIT),
         cost_estimate=pl.CostEstimate(flops=values.size * 100, bytes_accessed=values.size * 4, transcendentals=0))(values)
 
 
-def sum_kernel(ring, first, second, out, parts, gathered, send, recv):
+def finish_y(o_late, x_loc, b_o, started):
+    count, rows, width = o_late.shape
+    first = x_loc.shape[0] - count
+    late = pl.BlockSpec((1, rows, width), lambda b: (b + first, 0, 0))
+
+    def body(o, x, b_o, _, y):
+        y[...] = (x[...].astype(F32) + o[...].astype(F32) + b_o[...][None]).astype(BF16)
+
+    return pl.pallas_call(
+        body, name="finish_y", grid=(count,), out_shape=jax.ShapeDtypeStruct(x_loc.shape, BF16),
+        in_specs=[pl.BlockSpec((1, rows, width), lambda b: (b, 0, 0)), late, pl.BlockSpec((1, width), lambda b: (0, 0)), pl.BlockSpec(memory_space=pl.ANY)],
+        out_specs=late, input_output_aliases={3: 0}, compiler_params=pltpu.CompilerParams(vmem_limit_bytes=VMEM_LIMIT),
+        cost_estimate=pl.CostEstimate(flops=o_late.size * 100, bytes_accessed=o_late.size * 6, transcendentals=0))(o_late, x_loc, b_o, started)
+
+
+def sum_kernel(ring, rows, out, parts, gathered, send, recv):
     me = lax.axis_index("tp")
     barrier = pltpu.get_barrier_semaphore()
     others = [lax.rem(me + k, ring) for k in range(1, ring)]
     for other in others:
         pl.semaphore_signal(barrier, inc=1, device_id={"tp": other}, device_id_type=pl.DeviceIdType.MESH)
-    groups = first.shape[2] // 128
+    groups = rows.shape[2] // 128
     for kind in range(2):
-        row = jnp.sum(first[kind] + second[kind], axis=0, keepdims=True)
+        row = jnp.sum(rows[kind], axis=0, keepdims=True)
         for n in range(groups):
             parts[kind * groups + n : kind * groups + n + 1, :] = row[:, n * 128 : (n + 1) * 128]
     pl.semaphore_wait(barrier, ring - 1)
@@ -811,18 +905,18 @@
         copy(k).wait_send()
 
 
-def sum_over_ring(first, second, ring):
+def sum_over_ring(rows, ring):
     vmem = pl.BlockSpec(memory_space=pltpu.VMEM)
-    shape = (2 * first.shape[2] // 128, 128)
+    shape = (2 * rows.shape[2] // 128, 128)
     return pl.pallas_call(
         functools.partial(sum_kernel, ring),
         name="sum_over_ring",
         out_shape=jax.ShapeDtypeStruct(shape, F32),
-        in_specs=[vmem, vmem],
+        in_specs=[vmem],
         out_specs=vmem,
         scratch_shapes=[pltpu.VMEM(shape, F32), pltpu.VMEM((ring,) + shape, F32), pltpu.SemaphoreType.DMA((ring,)), pltpu.SemaphoreType.DMA((ring,))],
         compiler_params=pltpu.CompilerParams(collective_id=2, has_side_effects=True),
-    )(first, second)
+    )(rows)
 
 
 def solution(mesh):
@@ -832,26 +926,19 @@
         head_dim = w_kv.shape[1] // 2
         batch, own_rows, width = x_loc.shape
         early = 3 * batch // 8
-        normed_full, dy_full, merged, _, grad_q, _, kv_owned, y_loc, _, _, _, dh_chip, dh_early, bo_rows, bq_rows, ln_stats = attention_block(
+        normed_full, dy_full, merged, _, grad_q, _, kv_owned, y_early, _, _, o_chip, grad_h, bo_rows, bq_rows, ln_stats = attention_block(
             x_loc, dy_loc, ln_gamma[None, :], ln_beta[None, :], w_q, w_kv, b_q, b_kv, w_o, b_o[None, :], early, ring, head_dim)
         lines = [[i for i in range(ring) if i % 2 == core] for core in range(2)]
-        dh_late = lax.psum_scatter(dh_chip, "tp", scatter_dimension=1, tiled=True, axis_index_groups=lines)
-        kv_owned = kv_owned.reshape(ring, batch, own_rows, 2 * head_dim)
-        grad_kv = jnp.moveaxis(kv_owned, 0, 1).reshape(batch, ring * own_rows, 2 * head_dim)
-
-        grad_q, merged, y_loc = lax.optimization_barrier((grad_q, merged, y_loc))
-        y_loc = settle(y_loc)
-        grad_bo = jnp.sum(bo_rows, axis=0)
-        grad_wo = jnp.einsum("bse,bsd->ed", merged, dy_full, preferred_element_type=jnp.float32)
-        grad_wq = jnp.einsum("bsd,bse->de", normed_full, grad_q, preferred_element_type=jnp.float32)
-        grad_bq = jnp.sum(bq_rows, axis=0)
-        grad_wkv = jnp.einsum("bsd,bsc->dc", normed_full, grad_kv, preferred_element_type=jnp.float32)
-        grad_bkv = jnp.sum(grad_kv, axis=(0, 1), dtype=jnp.float32)
-        gamma = ln_gamma[None, :]
-        started, parts_early = norm_backward(dh_early, x_loc, dy_loc, ln_stats, gamma, 0, None)
-        grad_x, parts_late = norm_backward(dh_late, x_loc, dy_loc, ln_stats, gamma, early, started)
-        sums = sum_over_ring(parts_early, parts_late, ring).reshape(2, width)
-        return (y_loc, grad_x, sums[0], sums[1], grad_wq, grad_bq, grad_wkv, grad_bkv, grad_wo, grad_bo)
+        o_late = lax.psum_scatter(o_chip, "tp", scatter_dimension=1, tiled=True, axis_index_groups=lines)
+
+        flat = lambda v: v.reshape(-1, v.shape[-1])
+        grad_x, parts = norm_backward(grad_h, x_loc, dy_loc, ln_stats, ln_gamma[None, :])
+        sums = sum_over_ring(parts, ring).reshape(2, width)
+        wo_grad = grad_wo(flat(merged), flat(dy_full))
+        wq_grad, wkv_grad, kv_sums = grad_wq(flat(grad_q), kv_owned, flat(normed_full), own_rows)
+        grad_bq, grad_bkv, grad_bo = jnp.sum(bq_rows, axis=0), jnp.sum(kv_sums, axis=0), jnp.sum(bo_rows, axis=0)
+        y_loc = finish_y(o_late, x_loc, b_o[None, :], settle(y_early, batch))
+        return (y_loc, grad_x, sums[0], sums[1], wq_grad, grad_bq, wkv_grad, grad_bkv, wo_grad, grad_bo)
 
     return jax.shard_map(
         device_block,

time: 898 us -> 934 us (1.040)
  Pallas kernels: 753 us -> 912 us
  matrix products: 121 us -> 0 us
    pallas_call x3 -> x5, Pallas kernels: 25 us -> 150 us  [the longest x1 71.4 us: grad_wq(): pl.pallas_call(functools.partial(grad_wq_kernel, rows), name='grad_wq', g...]
    dot_general x3 -> x0, matrix products: 121 us -> none  [the longest x1 49.1 us: device_block(): jnp.einsum('bsd,bse->de', normed_full, grad_q, preferred_element_type=jnp...]
    pallas_call x1, Pallas kernels: 716 us -> 748 us  [attention_block(): pl.pallas_call(functools.partial(block_kernel, heads, dim), name='attenti...]
  transfers between devices with their start and end apart: 1 -> 1, of which waited for: 0 -> 0; matrix products, arithmetic and copies ran while one was open for 14% -> 0% of each run, Pallas kernels for 2% -> 17%
where the time goes in v8:
time: 934 us; the launch traced here: 931 us
  Pallas kernels  912 us (98%)
  between operations  14.1 us (2%)
    pallas_call x1, Pallas kernels, attention_block(): pl.pallas_call(functools.partial(block_kernel, heads, dim), name='attenti...  748 us
    pallas_call x1, Pallas kernels, grad_wq(): pl.pallas_call(functools.partial(grad_wq_kernel, rows), name='grad_wq', g...  71.4 us
    pallas_call x1, Pallas kernels, grad_wo(): pl.pallas_call(grad_wo_kernel, name='grad_wo', grid=(width // tile,), out...  51.1 us
  transfers between devices with their start and end apart: 1, of which 0 were waited for; matrix products, arithmetic and copies ran while one was open for 0% of the time, Pallas kernels for 17%

profile of v8, /device:TPU:112, one launch (start us, length us, event | category | flops | bytes accessed | tf_op | source)
XLA Modules:
  0.0 930.7 jit_solution(7088069826675588277)
XLA Ops:
  7.2 0.1 reduce-scatter.2.cloned.1.call-start
  7.3 748.4 %attention_block.1 = (bf16[8,512,6144]{2,1,0:T(8,128)(2,1)}, bf16[8,512,6144]{2,1,0:T(8,128)(2,1)}, bf16[8,512,768]{2,1,0:T(8,128)(2,1)}, bf16[8,512,6144]{2,1,0...) custom-call(bf16[8,64,6144]{2,1,0:T(8,128)(2,1)} %x.3, ...), custom_call_target="tpu_custom_call" | custom-call | flops 206158430208 | bytes 301989888 | tf_op jit(solution)/shard_map/attention_block/pallas_call | solution.py:682
  755.6 0.0 copy-start.1
  755.6 0.0 copy-start
  755.7 0.1 reduce-scatter.2.cloned.1.call-update
  755.7 0.7 copy-done.1
  756.4 0.6 reduce_sum.27
  757.0 0.0 copy-done
  757.0 0.7 reduce_sum.29
  757.6 17.0 %norm_backward.1 = (bf16[8,64,6144]{2,1,0:T(8,128)(2,1)}, f32[2,8,6144]{2,1,0:T(8,128)}) custom-call(bf16[8,64,6144]{2,1,0:T(8,128)(2,1)} %get-tuple-element.28.dh, bf16[8,64,6144]{2,1,0:T(8,128)(2,1)} %x.3, bf16[8,64,6144]{2,1,0:T(8,128)(2,1)} %dy.1, f32[2,8,64,128]{3,2,1,0:T(8,128)} %get-tuple-element.29.ln_stats, f32[1,6144]{1,0:T(1,128)} %bitcast.12), custom_call_target="tpu_custom_call" | custom-call | flops 188743680 | bytes 25165824 | tf_op jit(solution)/shard_map/norm_backward/pallas_call | solution.py:746
  774.7 13.2 %sum_over_ring.1 = f32[96,128]{1,0:T(8,128)} custom-call(f32[2,8,6144]{2,1,0:T(8,128)} %get-tuple-element.31.rows), custom_call_target="tpu_custom_call" | custom-call | tf_op jit(solution)/shard_map/sum_over_ring/pallas_call | solution.py:911
  787.8 71.4 %grad_wq.1 = (f32[6144,768]{1,0:T(8,128)}, f32[6144,256]{1,0:T(8,128)}, f32[8,256]{1,0:T(8,128)}) custom-call(bf16[4096,768]{1,0:T(8,128)(2,1)} %bitcast.19, bf16[8,512,256]{2,1,0:T(8,128)(2,1)} %get-tuple-element.33.kv_owned, bf16[4096,6144]{1,0:T(8,128)(2,1)} %bitcast.17), custom_call_target="tpu_custom_call" | custom-call | flops 51539607552 | bytes 75497472 | tf_op jit(solution)/shard_map/grad_wq/pallas_call | solution.py:837
  859.2 1.3 reduce_sum.28
  860.5 3.9 settle.1._
  864.4 1.4 slice_bitcast_fusion
  865.8 51.1 %grad_wo.1 = f32[768,6144]{1,0:T(8,128)} custom-call(bf16[4096,768]{1,0:T(8,128)(2,1)} %bitcast.18, bf16[4096,6144]{1,0:T(8,128)(2,1)} %bitcast.16), custom_call_target="tpu_custom_call" | custom-call | flops 38654705664 | bytes 69206016 | tf_op jit(solution)/shard_map/grad_wo/pallas_call | solution.py:788
  916.9 0.0 reduce-scatter.2.cloned.1.call-done.o
  916.9 7.0 finish_y.1
Async XLA Ops:
  7.2 909.7 %reduce-scatter.2.cloned.1.call-start = ((), (), s32[]{:S(2)}) async-start(), calls=%async_computation.1 | async-start | bytes 19660800 | tf_op jit(solution)/shard_map/reduce_scatter | solution.py:932
  755.6 0.7 copy-start.1
  755.6 1.3 copy-start
Sparse Core Ops, SparseCore 0:
  755.8 140.4 reduce-scatter.1

commit v9 on v8

--- a/solution.py
+++ b/solution.py
@@ -244,6 +244,15 @@
         for n in (width - 2 * tile, width - tile):
             store_part(o_part, 0, n).wait()
 
+    def project_out(b):
+        make_part(lambda at: jnp.dot(att_buf[...], wo_buf[:, at], preferred_element_type=F32), lambda n: store_part(o_part, b, n).start())
+
+    def project_out_late(b):
+        again = pltpu.make_async_copy(att_out.at[b], att_buf, load_sem.at[ring])
+        again.start()
+        again.wait()
+        project_out(b)
+
     def attend_and_project(b):
         @pl.when(b > 0)
         def _():
@@ -251,7 +260,10 @@
 
         attend(qkv_buf, att_buf, stats, scores_s, probs_s, q_s, heads, dim)
         store_att(b).start()
-        make_part(lambda at: jnp.dot(att_buf[...], wo_buf[:, at], preferred_element_type=F32), lambda n: store_part(o_part, b, n).start())
+
+        @pl.when(b < early)
+        def _():
+            project_out(b)
 
     def grad_attended(b):
         load_block(dy_full, b)
@@ -643,8 +655,13 @@
         def _():
             late_sum(t - 6)
 
+        @when(4, 5)
+        def _():
+            store_att(batch - 1).wait()
+
         @when(5, 5 + batch - early)
         def _():
+            project_out_late(early + t - 5)
             for chip in range(chips):
                 late_pair(t - 5, chip).start()
 
@@ -652,7 +669,6 @@
     for chip in range(chips):
         for v in range(batch - early):
             late_pair(v, chip).wait_send()
-    store_att(batch - 1).wait()
     store_y(y_out, 0).wait()
     for r in range(chips):
         pair(o_part.at[0], r).wait_send()
@@ -766,36 +782,8 @@
         dst[place : place + cols, at] = rows[at, :].T
 
 
-def grad_wo_kernel(att, dy, out, turned):
-    @pl.when(pl.program_id(0) == 0)
-    def _():
-        turn_rows(att, turned, 0)
-
-    @pl.loop(0, out.shape[1], step=256)
-    def _(n):
-        at = pl.ds(pl.multiple_of(n, 256), 256)
-        out[:, at] = jnp.dot(turned[...], dy[:, at], preferred_element_type=F32)
-
-
 def whole(shape):
     return pl.BlockSpec(shape, lambda n: (0,) * len(shape), pipeline_mode=pl.Buffered(1))
-
-
-def grad_wo(att, dy):
-    tokens, q_width = att.shape
-    width = dy.shape[1]
-    tile = 512
-    return pl.pallas_call(
-        grad_wo_kernel,
-        name="grad_wo",
-        grid=(width // tile,),
-        out_shape=jax.ShapeDtypeStruct((q_width, width), F32),
-        in_specs=[whole(att.shape), pl.BlockSpec((tokens, tile), lambda n: (0, n))],
-        out_specs=pl.BlockSpec((q_width, tile), lambda n: (0, n)),
-        scratch_shapes=[pltpu.VMEM((q_width, tokens), BF16)],
-        compiler_params=pltpu.CompilerParams(vmem_limit_bytes=VMEM_LIMIT),
-        cost_estimate=pl.CostEstimate(flops=2 * tokens * q_width * width, bytes_accessed=2 * tokens * width + 4 * q_width * width, transcendentals=0),
-    )(att, dy)
 
 
 def grad_wq_kernel(rows, grad_q, kv_owned, h, out_q, out_kv, kv_sums, turned, kv_lines):
@@ -925,7 +913,7 @@
     def device_block(x_loc, ln_gamma, ln_beta, w_q, b_q, w_kv, b_kv, w_o, b_o, dy_loc):
         head_dim = w_kv.shape[1] // 2
         batch, own_rows, width = x_loc.shape
-        early = 3 * batch // 8
+        early = batch // 4
         normed_full, dy_full, merged, _, grad_q, _, kv_owned, y_early, _, _, o_chip, grad_h, bo_rows, bq_rows, ln_stats = attention_block(
             x_loc, dy_loc, ln_gamma[None, :], ln_beta[None, :], w_q, w_kv, b_q, b_kv, w_o, b_o[None, :], early, ring, head_dim)
         lines = [[i for i in range(ring) if i % 2 == core] for core in range(2)]
@@ -934,7 +922,7 @@
         flat = lambda v: v.reshape(-1, v.shape[-1])
         grad_x, parts = norm_backward(grad_h, x_loc, dy_loc, ln_stats, ln_gamma[None, :])
         sums = sum_over_ring(parts, ring).reshape(2, width)
-        wo_grad = grad_wo(flat(merged), flat(dy_full))
+        wo_grad = jnp.einsum("bse,bsd->ed", merged, dy_full, preferred_element_type=jnp.float32)
         wq_grad, wkv_grad, kv_sums = grad_wq(flat(grad_q), kv_owned, flat(normed_full), own_rows)
         grad_bq, grad_bkv, grad_bo = jnp.sum(bq_rows, axis=0), jnp.sum(kv_sums, axis=0), jnp.sum(bo_rows, axis=0)
         y_loc = finish_y(o_late, x_loc, b_o[None, :], settle(y_early, batch))

time: 934 us -> 878 us (0.940)
  Pallas kernels: 912 us -> 801 us
  matrix products: 0 us -> 47.6 us
  waiting for transfers between devices: 0.06 us -> 10.1 us
    pallas_call x1, Pallas kernels: 748 us -> 689 us  [attention_block(): pl.pallas_call(functools.partial(block_kernel, heads, dim), name='attenti...]
    pallas_call x1 -> x0, Pallas kernels: 51.1 us -> none  [grad_wo(): pl.pallas_call(grad_wo_kernel, name='grad_wo', grid=(width // tile,), out...]
    dot_general x0 -> x1, matrix products: none -> 47.6 us  [device_block(): jnp.einsum('bse,bsd->ed', merged, dy_full, preferred_element_type=jnp.flo...]
    reduce_scatter x1, waiting for transfers between devices: 0.01 us -> 10 us  [device_block(): lax.psum_scatter(o_chip, 'tp', scatter_dimension=1, tiled=True, axis_inde...]
  transfers between devices with their start and end apart: 1 -> 1, of which waited for: 0 -> 1; matrix products, arithmetic and copies ran while one was open for 0% -> 6% of each run, Pallas kernels for 17% -> 12%
where the time goes in v9:
time: 878 us; the launch traced here: 877 us
  Pallas kernels  801 us (91%)
  matrix products  47.6 us (5%)
  between operations  14.1 us (2%)
  waiting for transfers between devices  10.1 us (1%)
    pallas_call x1, Pallas kernels, attention_block(): pl.pallas_call(functools.partial(block_kernel, heads, dim), name='attenti...  689 us
    pallas_call x1, Pallas kernels, grad_wq(): pl.pallas_call(functools.partial(grad_wq_kernel, rows), name='grad_wq', g...  71.4 us
    dot_general x1, matrix products, device_block(): jnp.einsum('bse,bsd->ed', merged, dy_full, preferred_element_type=jnp.flo...  47.6 us
  transfers between devices with their start and end apart: 1, of which 1 were waited for; matrix products, arithmetic and copies ran while one was open for 6% of the time, Pallas kernels for 12%

profile of v9, /device:TPU:112, one launch (start us, length us, event | category | flops | bytes accessed | tf_op | source)
XLA Modules:
  0.0 876.9 jit_solution(7543621193686289048)
XLA Ops:
  7.2 0.1 reduce-scatter.2.cloned.1.call-start
  7.3 688.5 %attention_block.1 = (bf16[8,512,6144]{2,1,0:T(8,128)(2,1)}, bf16[8,512,6144]{2,1,0:T(8,128)(2,1)}, bf16[8,512,768]{2,1,0:T(8,128)(2,1)}, bf16[8,512,6144]{2,1,0...) custom-call(bf16[8,64,6144]{2,1,0:T(8,128)(2,1)} %x.3, ...), custom_call_target="tpu_custom_call" | custom-call | flops 206158430208 | bytes 301989888 | tf_op jit(solution)/shard_map/attention_block/pallas_call | solution.py:698
  695.8 0.0 copy-start.1
  695.8 0.0 copy-start
  695.8 0.1 reduce-scatter.2.cloned.1.call-update
  695.9 0.7 copy-done.1
  696.5 0.6 reduce_sum.27
  697.1 0.0 copy-done
  697.1 0.7 reduce_sum.29
  697.8 17.0 %norm_backward.1 = (bf16[8,64,6144]{2,1,0:T(8,128)(2,1)}, f32[2,8,6144]{2,1,0:T(8,128)}) custom-call(bf16[8,64,6144]{2,1,0:T(8,128)(2,1)} %get-tuple-element.28.dh, bf16[8,64,6144]{2,1,0:T(8,128)(2,1)} %x.3, bf16[8,64,6144]{2,1,0:T(8,128)(2,1)} %dy.1, f32[2,8,64,128]{3,2,1,0:T(8,128)} %get-tuple-element.29.ln_stats, f32[1,6144]{1,0:T(1,128)} %bitcast.14), custom_call_target="tpu_custom_call" | custom-call | flops 188743680 | bytes 25165824 | tf_op jit(solution)/shard_map/norm_backward/pallas_call | solution.py:762
  714.8 13.8 %sum_over_ring.1 = f32[96,128]{1,0:T(8,128)} custom-call(f32[2,8,6144]{2,1,0:T(8,128)} %get-tuple-element.31.rows), custom_call_target="tpu_custom_call" | custom-call | tf_op jit(solution)/shard_map/sum_over_ring/pallas_call | solution.py:899
  728.7 71.4 %grad_wq.1 = (f32[6144,768]{1,0:T(8,128)}, f32[6144,256]{1,0:T(8,128)}, f32[8,256]{1,0:T(8,128)}) custom-call(bf16[4096,768]{1,0:T(8,128)(2,1)} %bitcast.19, bf16[8,512,256]{2,1,0:T(8,128)(2,1)} %get-tuple-element.33.kv_owned, bf16[4096,6144]{1,0:T(8,128)(2,1)} %bitcast.18), custom_call_target="tpu_custom_call" | custom-call | flops 51539607552 | bytes 75497472 | tf_op jit(solution)/shard_map/grad_wq/pallas_call | solution.py:825
  800.0 1.3 reduce_sum.28
  801.3 2.3 settle.1._
  803.6 1.4 slice_bitcast_fusion
  805.0 47.6 %convolution_bitcast_fusion = f32[768,6144]{1,0:T(8,128)} fusion(bf16[8,512,768]{2,1,0:T(8,128)(2,1)} %get-tuple-element.39, bf16[8,512,6144]{2,1,0:T(8,128)(2,1)} %get-tuple-element.40), kind=kOutput, calls=%fused_computation | convolution fusion | flops 38654705664 | bytes 75497472 | tf_op jit(solution)/shard_map/bse,bsd->ed/dot_general | solution.py:925
  852.5 10.0 %reduce-scatter.2.cloned.1.call-done.o = bf16[6,64,6144]{2,1,0:T(8,128)(2,1)} async-done(((bf16[6,256,6144]{2,1,0:T(8,128)(2,1)}), bf16[6,64,6144]{2,1,0:T(8,128)(2,1)}) %reduce-scatter.2.cloned.1.call-update) | async-done | bytes 4718608 | tf_op jit(solution)/shard_map/reduce_scatter | solution.py:920
  862.6 7.5 finish_y.1
Async XLA Ops:
  7.2 855.4 %reduce-scatter.2.cloned.1.call-start = ((), (), s32[]{:S(2)}) async-start(), calls=%async_computation.1 | async-start | bytes 23592960 | tf_op jit(solution)/shard_map/reduce_scatter | solution.py:920
  695.8 0.7 copy-start.1
  695.8 1.3 copy-start
Sparse Core Ops, SparseCore 0:
  696.0 166.5 reduce-scatter.1

commit v10 on v9

--- a/solution.py
+++ b/solution.py
@@ -453,8 +453,9 @@
         copies = [pltpu.make_async_copy(o_part.at[early + v, line(2 * chip + core)], h_buf.at[pl.ds(chip * rows, rows)], late_sem.at[chip]) for chip in range(chips)]
         return copies + [pltpu.make_async_copy(o_theirs.at[v], h_buf.at[pl.ds(chips * rows, chips * rows)], late_sem.at[chips])]
 
-    def late_store(v):
-        return pltpu.make_async_copy(h_buf.at[pl.ds(0, chips * rows)], o_chip.at[v], late_sem.at[chips + 1])
+    def late_stores(v):
+        return [pltpu.make_async_copy(h_buf.at[pl.ds(chip * rows, rows)], o_chip.at[chip, pl.ds(pl.multiple_of(v * rows, rows), rows)],
+                                      late_sem.at[chips + 1 + chip]) for chip in range(chips)]
 
     def late_sum(v):
         for chip in range(chips):
@@ -462,7 +463,8 @@
 
         @pl.when(v > 0)
         def _():
-            late_store(v - 1).wait()
+            for copy in late_stores(v - 1):
+                copy.wait()
 
         for copy in late_loads(v):
             copy.start()
@@ -474,7 +476,8 @@
             h_buf[: chips * rows, at] = (mine_ + theirs_).astype(BF16)
 
         columns(0, width, act)
-        late_store(v).start()
+        for copy in late_stores(v):
+            copy.start()
 
     pick = lambda ref, n: ref.at[:, pl.ds(n * kv_width, kv_width)]
     kv_ours = [pick(probs_s, 0), pick(probs_s, 1), pick(probs_s, 2), pick(grad_s_s, 0)]
@@ -665,7 +668,8 @@
             for chip in range(chips):
                 late_pair(t - 5, chip).start()
 
-    late_store(batch - early - 1).wait()
+    for copy in late_stores(batch - early - 1):
+        copy.wait()
     for chip in range(chips):
         for v in range(batch - early):
             late_pair(v, chip).wait_send()
@@ -699,7 +703,7 @@
         functools.partial(block_kernel, heads, dim),
         name="attention_block",
         out_shape=(full(batch, width), full(batch, width), full(batch, q_width), full(batch, width), full(batch, q_width), owned, owned, at_home(early),
-                   full(batch, width), half_seq, half_seq, at_home(batch),
+                   full(batch, width), half_seq, jax.ShapeDtypeStruct((chips, (batch - early) * rows, width), BF16), at_home(batch),
                    jax.ShapeDtypeStruct((8, width), F32), jax.ShapeDtypeStruct((8, q_width), F32), jax.ShapeDtypeStruct((2, batch, rows, 128), F32)),
         in_specs=[hbm, hbm, vmem, vmem, hbm, hbm, vmem, vmem, hbm, vmem],
         out_specs=(hbm,) * 12 + (vmem, vmem, vmem),
@@ -713,7 +717,7 @@
             dma((ring + 3,)),
             dma((chips,)), dma((chips,)), dma((chips,)), dma((2, 2)), dma((3, 2)), dma((3, 2)), dma((3, 2)), pltpu.SemaphoreType.REGULAR,
             dma((chips,)), dma((chips,)), dma((chips,)), dma((2,)), dma((2,)), dma((2,)), dma((2,)), dma((8,)), dma((8,)), dma((1,)),
-            dma((batch - early, chips)), dma((batch - early, chips)), dma((chips + 2,))],
+            dma((batch - early, chips)), dma((batch - early, chips)), dma((2 * chips + 1,))],
         compiler_params=pltpu.CompilerParams(collective_id=0, has_side_effects=True, vmem_limit_bytes=VMEM_LIMIT),
         cost_estimate=pl.CostEstimate(flops=8 * batch * seq * width * qkv_width, bytes_accessed=12 * batch * seq * width, transcendentals=0),
     )(x_loc, dy_loc, gamma, beta, w_q, w_kv, b_q, b_kv, w_o, b_o)
@@ -847,18 +851,42 @@
         cost_estimate=pl.CostEstimate(flops=values.size * 100, bytes_accessed=values.size * 4, transcendentals=0))(values)
 
 
+def finish_y_kernel(o_hbm, x_hbm, b_o, _, y_hbm, o_buf, x_buf, o_sem, x_sem, y_sem):
+    count, rows, width = o_hbm.shape
+    first = x_hbm.shape[0] - count
+    tile = 512
+    load_o = lambda v: pltpu.make_async_copy(o_hbm.at[v], o_buf.at[v], o_sem.at[v])
+    load_x = lambda v: pltpu.make_async_copy(x_hbm.at[first + v], x_buf.at[v], x_sem.at[v])
+    store_y = lambda v: pltpu.make_async_copy(o_buf.at[v], y_hbm.at[first + v], y_sem.at[v])
+    for v in range(count):
+        load_o(v).start()
+        load_x(v).start()
+
+    @pl.loop(0, count)
+    def _(v):
+        load_o(v).wait()
+        load_x(v).wait()
+
+        @pl.loop(0, width, step=tile)
+        def _(n):
+            at = pl.ds(pl.multiple_of(n, tile), tile)
+            o_buf[v, :, at] = (x_buf[v, :, at].astype(F32) + o_buf[v, :, at].astype(F32) + b_o[:, at]).astype(BF16)
+
+        store_y(v).start()
+
+    for v in range(count):
+        store_y(v).wait()
+
+
 def finish_y(o_late, x_loc, b_o, started):
     count, rows, width = o_late.shape
-    first = x_loc.shape[0] - count
-    late = pl.BlockSpec((1, rows, width), lambda b: (b + first, 0, 0))
-
-    def body(o, x, b_o, _, y):
-        y[...] = (x[...].astype(F32) + o[...].astype(F32) + b_o[...][None]).astype(BF16)
-
+    hbm = pl.BlockSpec(memory_space=pl.ANY)
+    dma = pltpu.SemaphoreType.DMA((count,))
     return pl.pallas_call(
-        body, name="finish_y", grid=(count,), out_shape=jax.ShapeDtypeStruct(x_loc.shape, BF16),
-        in_specs=[pl.BlockSpec((1, rows, width), lambda b: (b, 0, 0)), late, pl.BlockSpec((1, width), lambda b: (0, 0)), pl.BlockSpec(memory_space=pl.ANY)],
-        out_specs=late, input_output_aliases={3: 0}, compiler_params=pltpu.CompilerParams(vmem_limit_bytes=VMEM_LIMIT),
+        finish_y_kernel, name="finish_y", out_shape=jax.ShapeDtypeStruct(x_loc.shape, BF16),
+        in_specs=[hbm, hbm, pl.BlockSpec(memory_space=pltpu.VMEM), hbm], out_specs=hbm, input_output_aliases={3: 0},
+        scratch_shapes=[pltpu.VMEM(o_late.shape, BF16), pltpu.VMEM(o_late.shape, BF16), dma, dma, dma],
+        compiler_params=pltpu.CompilerParams(vmem_limit_bytes=VMEM_LIMIT),
         cost_estimate=pl.CostEstimate(flops=o_late.size * 100, bytes_accessed=o_late.size * 6, transcendentals=0))(o_late, x_loc, b_o, started)
 
 
@@ -917,7 +945,7 @@
         normed_full, dy_full, merged, _, grad_q, _, kv_owned, y_early, _, _, o_chip, grad_h, bo_rows, bq_rows, ln_stats = attention_block(
             x_loc, dy_loc, ln_gamma[None, :], ln_beta[None, :], w_q, w_kv, b_q, b_kv, w_o, b_o[None, :], early, ring, head_dim)
         lines = [[i for i in range(ring) if i % 2 == core] for core in range(2)]
-        o_late = lax.psum_scatter(o_chip, "tp", scatter_dimension=1, tiled=True, axis_index_groups=lines)
+        o_late = lax.psum_scatter(o_chip, "tp", scatter_dimension=0, tiled=True, axis_index_groups=lines).reshape(batch - early, own_rows, width)
 
         flat = lambda v: v.reshape(-1, v.shape[-1])
         grad_x, parts = norm_backward(grad_h, x_loc, dy_loc, ln_stats, ln_gamma[None, :])

time: 878 us -> 878 us (level)
  no operation moved by 1% of the time
where the time goes in v10:
time: 878 us; the launch traced here: 876 us
  Pallas kernels  800 us (91%)
  matrix products  47.6 us (5%)
  between operations  14.1 us (2%)
  waiting for transfers between devices  10.1 us (1%)
    pallas_call x1, Pallas kernels, attention_block(): pl.pallas_call(functools.partial(block_kernel, heads, dim), name='attenti...  689 us
    pallas_call x1, Pallas kernels, grad_wq(): pl.pallas_call(functools.partial(grad_wq_kernel, rows), name='grad_wq', g...  71.4 us
    dot_general x1, matrix products, device_block(): jnp.einsum('bse,bsd->ed', merged, dy_full, preferred_element_type=jnp.flo...  47.6 us
  transfers between devices with their start and end apart: 1, of which 1 were waited for; matrix products, arithmetic and copies ran while one was open for 6% of the time, Pallas kernels for 12%

profile of v10, /device:TPU:112, one launch (start us, length us, event | category | flops | bytes accessed | tf_op | source)
XLA Modules:
  0.0 876.4 jit_solution(5272954954305716195)
XLA Ops:
  7.2 0.1 reduce-scatter.2.cloned.1.call-start
  7.3 688.5 %attention_block.1 = (bf16[8,512,6144]{2,1,0:T(8,128)(2,1)}, bf16[8,512,6144]{2,1,0:T(8,128)(2,1)}, bf16[8,512,768]{2,1,0:T(8,128)(2,1)}, bf16[8,512,6144]{2,1,0...) custom-call(bf16[8,64,6144]{2,1,0:T(8,128)(2,1)} %x.1, ...), custom_call_target="tpu_custom_call" | custom-call | flops 206158430208 | bytes 301989888 | tf_op jit(solution)/shard_map/attention_block/pallas_call | solution.py:702
  695.8 0.0 copy-start.1
  695.8 0.0 copy-start
  695.8 0.1 reduce-scatter.2.cloned.1.call-update
  695.9 0.7 copy-done.1
  696.5 0.6 reduce_sum.27
  697.1 0.0 copy-done
  697.1 0.7 reduce_sum.29
  697.8 17.0 %norm_backward.1 = (bf16[8,64,6144]{2,1,0:T(8,128)(2,1)}, f32[2,8,6144]{2,1,0:T(8,128)}) custom-call(bf16[8,64,6144]{2,1,0:T(8,128)(2,1)} %get-tuple-element.28.dh, bf16[8,64,6144]{2,1,0:T(8,128)(2,1)} %x.1, bf16[8,64,6144]{2,1,0:T(8,128)(2,1)} %dy.1, f32[2,8,64,128]{3,2,1,0:T(8,128)} %get-tuple-element.29.ln_stats, f32[1,6144]{1,0:T(1,128)} %bitcast.16), custom_call_target="tpu_custom_call" | custom-call | flops 188743680 | bytes 25165824 | tf_op jit(solution)/shard_map/norm_backward/pallas_call | solution.py:766
  714.8 13.8 %sum_over_ring.1 = f32[96,128]{1,0:T(8,128)} custom-call(f32[2,8,6144]{2,1,0:T(8,128)} %get-tuple-element.31.rows), custom_call_target="tpu_custom_call" | custom-call | tf_op jit(solution)/shard_map/sum_over_ring/pallas_call | solution.py:927
  728.7 71.4 %grad_wq.1 = (f32[6144,768]{1,0:T(8,128)}, f32[6144,256]{1,0:T(8,128)}, f32[8,256]{1,0:T(8,128)}) custom-call(bf16[4096,768]{1,0:T(8,128)(2,1)} %bitcast.21, bf16[8,512,256]{2,1,0:T(8,128)(2,1)} %get-tuple-element.33.kv_owned, bf16[4096,6144]{1,0:T(8,128)(2,1)} %bitcast.20), custom_call_target="tpu_custom_call" | custom-call | flops 51539607552 | bytes 75497472 | tf_op jit(solution)/shard_map/grad_wq/pallas_call | solution.py:829
  800.0 1.3 reduce_sum.28
  801.3 2.3 settle.1._
  803.6 1.4 slice_bitcast_fusion
  805.0 47.6 %convolution_bitcast_fusion = f32[768,6144]{1,0:T(8,128)} fusion(bf16[8,512,768]{2,1,0:T(8,128)(2,1)} %get-tuple-element.39, bf16[8,512,6144]{2,1,0:T(8,128)(2,1)} %get-tuple-element.40), kind=kOutput, calls=%fused_computation | convolution fusion | flops 38654705664 | bytes 75497472 | tf_op jit(solution)/shard_map/bse,bsd->ed/dot_general | solution.py:953
  852.6 10.0 %reduce-scatter.2.cloned.1.call-done = bf16[1,384,6144]{2,1,0:T(8,128)(2,1)} async-done(((bf16[4,384,6144]{2,1,0:T(8,128)(2,1)}), bf16[1,384,6144]{2,1,0:T(8,128)(2,1)}) %reduce-scatter.2.cloned.1.call-update) | async-done | bytes 4718608 | tf_op jit(solution)/shard_map/reduce_scatter | solution.py:948
  862.6 6.9 finish_y.1
Async XLA Ops:
  7.2 855.4 %reduce-scatter.2.cloned.1.call-start = ((), (), s32[]{:S(2)}) async-start(), calls=%async_computation.1 | async-start | bytes 23592960 | tf_op jit(solution)/shard_map/reduce_scatter | solution.py:948
  695.8 0.7 copy-start.1
  695.8 1.3 copy-start
Sparse Core Ops, SparseCore 0:
  696.0 166.5 reduce-scatter.1

commit v11 on v10

--- a/solution.py
+++ b/solution.py
@@ -109,7 +109,6 @@
     barrier = pltpu.get_barrier_semaphore()
     for other in (left, right, partner):
         pl.semaphore_signal(barrier, inc=1, device_id={"tp": other}, device_id_type=pl.DeviceIdType.MESH)
-    pl.semaphore_wait(barrier, 3)
 
     def remote(src, dst, sems, to):
         return pltpu.make_async_remote_copy(
@@ -176,15 +175,14 @@
         def _():
             load_x(b + 2).start()
 
+    def emit(full, b, u):
+        for kind in (RIGHT, LEFT, PART):
+            move(kind, full, b, u).start()
+        keep(full, b, u).start()
+
     def launch(u):
         turn(u, normalise, lambda b: load_dy(b).wait())
-
-        def act(full, b, u):
-            for kind in (RIGHT, LEFT, PART):
-                move(kind, full, b, u).start()
-            keep(full, b, u).start()
-
-        unit(u, act)
+        unit(u, emit)
 
     def forward(full, b, u):
         move(RIGHT, full, b, u).wait_recv()
@@ -581,8 +579,11 @@
     weights = (pltpu.make_async_copy(wq_hbm, w_buf.at[:, pl.ds(0, q_width)], w_sem.at[0]),
                pltpu.make_async_copy(wkv_hbm, w_buf.at[:, pl.ds(q_width, kv_width)], w_sem.at[1]),
                pltpu.make_async_copy(wo_hbm, wo_buf, w_sem.at[2]))
-    launch(0)
-    launch(1)
+    normalise(0)
+    load_dy(0).wait()
+    pl.semaphore_wait(barrier, 3)
+    emit(h_full, 0, 0)
+    emit(dy_full, 0, 1)
     for copy in weights:
         copy.start()
     for b in range(1, batch):

time: 878 us -> 876 us (level)
  no operation moved by 1% of the time
where the time goes in v11:
time: 876 us; the launch traced here: 875 us
  Pallas kernels  799 us (91%)
  matrix products  47.6 us (5%)
  between operations  14.1 us (2%)
  waiting for transfers between devices  10 us (1%)
    pallas_call x1, Pallas kernels, attention_block(): pl.pallas_call(functools.partial(block_kernel, heads, dim), name='attenti...  688 us
    pallas_call x1, Pallas kernels, grad_wq(): pl.pallas_call(functools.partial(grad_wq_kernel, rows), name='grad_wq', g...  71.4 us
    dot_general x1, matrix products, device_block(): jnp.einsum('bse,bsd->ed', merged, dy_full, preferred_element_type=jnp.flo...  47.6 us
  transfers between devices with their start and end apart: 1, of which 1 were waited for; matrix products, arithmetic and copies ran while one was open for 6% of the time, Pallas kernels for 12%

profile of v11, /device:TPU:112, one launch (start us, length us, event | category | flops | bytes accessed | tf_op | source)
XLA Modules:
  0.0 874.9 jit_solution(16137288954479229777)
XLA Ops:
  7.2 0.1 reduce-scatter.2.cloned.1.call-start
  7.3 688.2 %attention_block.1 = (bf16[8,512,6144]{2,1,0:T(8,128)(2,1)}, bf16[8,512,6144]{2,1,0:T(8,128)(2,1)}, bf16[8,512,768]{2,1,0:T(8,128)(2,1)}, bf16[8,512,6144]{2,1,0...) custom-call(bf16[8,64,6144]{2,1,0:T(8,128)(2,1)} %x.1, ...), custom_call_target="tpu_custom_call" | custom-call | flops 206158430208 | bytes 301989888 | tf_op jit(solution)/shard_map/attention_block/pallas_call | solution.py:703
  695.5 0.0 copy-start.1
  695.5 0.0 copy-start
  695.5 0.1 reduce-scatter.2.cloned.1.call-update
  695.6 0.7 copy-done.1
  696.2 0.6 reduce_sum.27
  696.8 0.0 copy-done
  696.8 0.7 reduce_sum.29
  697.5 16.6 %norm_backward.1 = (bf16[8,64,6144]{2,1,0:T(8,128)(2,1)}, f32[2,8,6144]{2,1,0:T(8,128)}) custom-call(bf16[8,64,6144]{2,1,0:T(8,128)(2,1)} %get-tuple-element.28.dh, bf16[8,64,6144]{2,1,0:T(8,128)(2,1)} %x.1, bf16[8,64,6144]{2,1,0:T(8,128)(2,1)} %dy.1, f32[2,8,64,128]{3,2,1,0:T(8,128)} %get-tuple-element.29.ln_stats, f32[1,6144]{1,0:T(1,128)} %bitcast.16), custom_call_target="tpu_custom_call" | custom-call | flops 188743680 | bytes 25165824 | tf_op jit(solution)/shard_map/norm_backward/pallas_call | solution.py:767
  714.1 13.2 %sum_over_ring.1 = f32[96,128]{1,0:T(8,128)} custom-call(f32[2,8,6144]{2,1,0:T(8,128)} %get-tuple-element.31.rows), custom_call_target="tpu_custom_call" | custom-call | tf_op jit(solution)/shard_map/sum_over_ring/pallas_call | solution.py:928
  727.2 71.4 %grad_wq.1 = (f32[6144,768]{1,0:T(8,128)}, f32[6144,256]{1,0:T(8,128)}, f32[8,256]{1,0:T(8,128)}) custom-call(bf16[4096,768]{1,0:T(8,128)(2,1)} %bitcast.21, bf16[8,512,256]{2,1,0:T(8,128)(2,1)} %get-tuple-element.33.kv_owned, bf16[4096,6144]{1,0:T(8,128)(2,1)} %bitcast.20), custom_call_target="tpu_custom_call" | custom-call | flops 51539607552 | bytes 75497472 | tf_op jit(solution)/shard_map/grad_wq/pallas_call | solution.py:830
  798.6 1.3 reduce_sum.28
  799.9 2.3 settle.1._
  802.2 1.4 slice_bitcast_fusion
  803.6 47.6 %convolution_bitcast_fusion = f32[768,6144]{1,0:T(8,128)} fusion(bf16[8,512,768]{2,1,0:T(8,128)(2,1)} %get-tuple-element.39, bf16[8,512,6144]{2,1,0:T(8,128)(2,1)} %get-tuple-element.40), kind=kOutput, calls=%fused_computation | convolution fusion | flops 38654705664 | bytes 75497472 | tf_op jit(solution)/shard_map/bse,bsd->ed/dot_general | solution.py:954
  851.1 10.0 %reduce-scatter.2.cloned.1.call-done = bf16[1,384,6144]{2,1,0:T(8,128)(2,1)} async-done(((bf16[4,384,6144]{2,1,0:T(8,128)(2,1)}), bf16[1,384,6144]{2,1,0:T(8,128)(2,1)}) %reduce-scatter.2.cloned.1.call-update) | async-done | bytes 4718608 | tf_op jit(solution)/shard_map/reduce_scatter | solution.py:949
  861.1 6.9 finish_y.1
Async XLA Ops:
  7.2 853.9 %reduce-scatter.2.cloned.1.call-start = ((), (), s32[]{:S(2)}) async-start(), calls=%async_computation.1 | async-start | bytes 23592960 | tf_op jit(solution)/shard_map/reduce_scatter | solution.py:949
  695.5 0.7 copy-start.1
  695.5 1.3 copy-start
Sparse Core Ops, SparseCore 0:
  695.7 165.3 reduce-scatter.1
